TPU v7x, 32 devices: a whole 2x2x4 slice. The times are simulated.
32 devices in a mesh: gx: 8 (over z, y), gy: 4 (over x, core).
Axes of the slice: x: 2, y: 2, z: 4, core: 2. Of those that a mesh axis runs over, the one named last changes fastest.
Arguments:
- level_cotangent: float32 [128, 64, 128], P('gx', 'gy'), may hold values from -6 to 6
- velocity_cotangent: float32 [3, 128, 64, 128], P(None, 'gx', 'gy'), may hold values from -6 to 6
- fraction: float32 [2, 3, 128, 64, 128], P(None, None, 'gx', 'gy'), may hold values from 0 to 1
- shift_x: int32 [8, 4, 2], P('gx', 'gy'), may hold values from -2 to 2
- shift_y: int32 [8, 4, 2], P('gx', 'gy'), may hold values from -1 to 1
- region_labels: int32 [128, 64, 128], P('gx', 'gy'), may hold values 0 or 1
- phase_rates: float32 [2], replicated, may hold values from 0.04 to 0.16
Outputs:
- level_gradient: float32 [128, 64, 128], P('gx', 'gy')
- velocity_gradient: float32 [3, 128, 64, 128], P(None, 'gx', 'gy')
All inputs are finite; a program needn't handle non-finite values. No bound on the sum of `region_labels` on one device may be relied on, other than what follows from the above.
Results may differ from a plain program's by a relative error of at most 0.0001.
Values sent between devices are 32-bit elements; how exact they have to be, the bound alone decides.
No kernel may reach another device: no remote copies, remote signals or barrier semaphores. Data moves between devices by JAX's collectives and lax.ppermute only.
A program may use at most 128 MiB of HBM per device.

v0:
```python
import jax
import jax.numpy as jnp
from jax import lax
from jax.sharding import PartitionSpec as P

STEPS = 2


BUOYANCY = 0.8


def shifted(value, axis, steps):
    count = lax.axis_size(axis)
    pairs = [(source, (source + steps) % count) for source in range(count)]
    return lax.ppermute(value, axis, pairs)


def extended(cells, sides, width):
    for axis, dim in sides:
        count = lax.axis_size(axis)
        head = lax.slice_in_dim(cells, 0, width, axis=dim)
        tail = lax.slice_in_dim(cells, cells.shape[dim] - width, cells.shape[dim], axis=dim)
        cells = jnp.concatenate(
            [
                lax.ppermute(tail, axis, [(i, (i + 1) % count) for i in range(count)]),
                cells,
                lax.ppermute(head, axis, [((i + 1) % count, i) for i in range(count)]),
            ],
            axis=dim,
        )
    return cells


def cubic_weights(position):
    squared = position * position
    cubed = squared * position
    return (
        (2.0 * squared - cubed - position) * 0.5,
        (3.0 * cubed - 5.0 * squared + 2.0) * 0.5,
        (4.0 * squared - 3.0 * cubed + position) * 0.5,
        (cubed - squared) * 0.5,
    )


def sweep(padded, rate_padded):
    middle = padded[:, 1:-1, 1:-1]
    rate_middle = rate_padded[1:-1, 1:-1]
    summed = middle
    sides = (
        (padded[:, 2:, 1:-1], rate_padded[2:, 1:-1]),
        (padded[:, :-2, 1:-1], rate_padded[:-2, 1:-1]),
        (padded[:, 1:-1, 2:], rate_padded[1:-1, 2:]),
        (padded[:, 1:-1, :-2], rate_padded[1:-1, :-2]),
    )
    for neighbour, neighbour_rate in sides:
        summed = summed + 0.5 * (rate_middle + neighbour_rate) * (neighbour - middle)
    for distance in (1, -1):
        summed = summed + 0.5 * (rate_middle + jnp.roll(rate_middle, distance, -1)) * (
            jnp.roll(middle, distance, -1) - middle
        )
    return summed


def spread_back(stacked, fractions):
    cells_x = stacked.shape[1]
    cells_y = stacked.shape[2]
    weights_x = cubic_weights(fractions[0])
    weights_y = cubic_weights(fractions[1])
    weights_z = cubic_weights(fractions[2])
    patches = jnp.zeros((4, cells_x + 3, cells_y + 3, stacked.shape[3]), jnp.float32)
    for off_x in range(4):
        for off_y in range(4):
            weighted = stacked * (weights_x[off_x] * weights_y[off_y])
            column = jnp.zeros_like(weighted)
            for off_z in range(4):
                column = column + jnp.roll(weighted * weights_z[off_z], off_z - 1, -1)
            patches = patches + jnp.pad(
                column, ((0, 0), (off_x, 3 - off_x), (off_y, 3 - off_y), (0, 0))
            )
    return patches


def route(patches, own_x, own_y):
    slot_stack = jnp.stack([jnp.where(own_y == move_y, patches, 0.0) for move_y in (-1, 0, 1)])
    arrived_slots = jnp.where(own_x == 0, slot_stack, 0.0)
    for move_x in (-2, -1, 1, 2):
        masked_part = jnp.where(own_x == move_x, slot_stack, 0.0)
        arrived_slots = arrived_slots + shifted(masked_part, "gx", move_x)
    received = arrived_slots[1]
    for move_y in (-1, 1):
        received = received + shifted(arrived_slots[move_y + 1], "gy", move_y)
    return received


def fold_rims(received):
    cells_x = received.shape[1] - 3
    inner = received[:, 1 : cells_x + 1]
    for distance, start_row, rim_rows in (
        (-1, cells_x - 1, received[:, 0:1]),
        (1, 0, received[:, cells_x + 1 : cells_x + 3]),
    ):
        arrived = shifted(rim_rows, "gx", distance)
        inner = inner + jnp.pad(
            arrived, ((0, 0), (start_row, cells_x - start_row - arrived.shape[1]), (0, 0), (0, 0))
        )
    cells_y = inner.shape[2] - 3
    folded = inner[:, :, 1 : cells_y + 1]
    for distance, start_row, rim_rows in (
        (-1, cells_y - 1, inner[:, :, 0:1]),
        (1, 0, inner[:, :, cells_y + 1 : cells_y + 3]),
    ):
        arrived = shifted(rim_rows, "gy", distance)
        folded = folded + jnp.pad(
            arrived, ((0, 0), (0, 0), (start_row, cells_y - start_row - arrived.shape[2]), (0, 0))
        )
    return folded


def on_device(
    level_cotangent, velocity_cotangent, fraction, shift_x, shift_y, region_labels, phase_rates
):
    cell_rate = jnp.where(region_labels == 1, phase_rates[1], phase_rates[0])
    rate_deep = extended(cell_rate, (("gx", 0), ("gy", 1)), 2)
    rate_near = rate_deep[1:-1, 1:-1]
    level_now = level_cotangent
    velocity_now = velocity_cotangent
    for step_index in range(STEPS - 1, -1, -1):
        diffused = velocity_now
        for sweep_index in range(2):
            padded = extended(diffused, (("gx", 1), ("gy", 2)), 1)
            diffused = sweep(padded, rate_near)
        level_part = level_now + BUOYANCY * diffused[2]
        stacked = jnp.concatenate([level_part[None], diffused], 0)
        patches = spread_back(stacked, fraction[step_index])
        received = route(patches, shift_x[0, 0, step_index], shift_y[0, 0, step_index])
        moved = fold_rims(received)
        level_now = moved[0]
        velocity_now = moved[1:]
    return (level_now, velocity_now)


def solution(mesh):
    in_specs = (
        P("gx", "gy", None),
        P(None, "gx", "gy", None),
        P(None, None, "gx", "gy", None),
        P("gx", "gy", None),
        P("gx", "gy", None),
        P("gx", "gy", None),
        P(),
    )
    out_specs = (P("gx", "gy", None), P(None, "gx", "gy", None))
    return jax.shard_map(
        on_device, mesh=mesh, in_specs=in_specs, out_specs=out_specs, check_vma=False
    )
```

profile of v0, /device:TPU:0, one launch (start us, length us, event | category | flops | bytes accessed | tf_op | source)
XLA Modules:
  0.0 596.2 jit_solution(3168019821336647561)
XLA Ops:
  1.9 2.1 broadcast_select_fusion.8
  4.1 6.1 %collective-permute-start = (f32[2,16,128]{2,1,0:T(8,128)S(1)}, f32[2,16,128]{2,1,0:T(8,128)S(1)}, u32[]{:S(2)}, u32[]{:S(2)}) collective-permute-start(f32[2,16,128]{2,1,0:T(8,128)S(1)} %get-tuple-element.235), channel_id=1, source_target_pairs={{4,0},{8,4},{12,8},{16,12},{20,16},{24,20},{28,24},{0,28},{5,1},{9... | collective-permute-start | bytes 49160 | tf_op jit(solution)/shard_map/ppermute | solution.py:27
  11.5 4.8 collective-permute-start.1
  31.3 2.0 fusion.54
  33.3 2.0 collective-permute-start.8
  37.3 4.6 collective-permute-done.9
  47.5 4.8 multiply_multiply_fusion.94
  55.8 2.8 multiply_multiply_fusion.95
  105.4 3.5 fusion.69
  109.0 3.6 fusion.73
  112.6 3.5 fusion.77
  116.2 3.0 fusion.81
  119.3 2.2 fusion.85
  121.7 2.5 fusion.89
  124.3 2.2 fusion.93
  126.5 2.2 fusion.97
  128.8 2.7 select_bitcast_fusion.5
  133.3 2.0 collective-permute-start.14
  135.3 2.0 collective-permute-start.15
  137.9 46.4 %collective-permute-done.12 = f32[3,4,19,19,128]{4,1,3,2,0:T(4,128)S(1)} collective-permute-done((f32[3,4,19,19,128]{4,1,3,2,0:T(4,128)S(1)}, f32[3,4,19,19,128]{4,1,3,2,0:T(4,128)S(1)}, u32[]{:S(2)}, u32[]{:S(2)}) %collective-permute-start.12) | collective-permute-done | bytes 2218016 | tf_op jit(solution)/shard_map/ppermute | solution.py:15
  184.3 46.4 %collective-permute-done.13 = f32[3,4,19,19,128]{4,1,3,2,0:T(4,128)S(1)} collective-permute-done((f32[3,4,19,19,128]{4,1,3,2,0:T(4,128)S(1)}, f32[3,4,19,19,128]{4,1,3,2,0:T(4,128)S(1)}, u32[]{:S(2)}, u32[]{:S(2)}) %collective-permute-start.13) | collective-permute-done | bytes 2218016 | tf_op jit(solution)/shard_map/ppermute | solution.py:15
  230.7 45.4 %collective-permute-done.15 = f32[3,4,19,19,128]{4,1,3,2,0:T(4,128)S(1)} collective-permute-done((f32[3,4,19,19,128]{4,1,3,2,0:T(4,128)S(1)}, f32[3,4,19,19,128]{4,1,3,2,0:T(4,128)S(1)}, u32[]{:S(2)}, u32[]{:S(2)}) %collective-permute-start.15) | collective-permute-done | bytes 2218016 | tf_op jit(solution)/shard_map/ppermute | solution.py:15
  278.3 16.2 %collective-permute-done.16 = f32[4,19,19,128]{3,0,2,1:T(4,128)S(1)} collective-permute-done((f32[4,19,19,128]{3,0,2,1:T(4,128)S(1)}, f32[4,19,19,128]{3,0,2,1:T(4,128)S(1)}, u32[]{:S(2)}, u32[]{:S(2)}) %collective-permute-start.16) | collective-permute-done | bytes 739360 | tf_op jit(solution)/shard_map/ppermute | solution.py:15
  296.3 3.5 collective-permute-start.19
  301.1 2.8 collective-permute-done.18
  310.5 3.9 collective-permute-start.22
  316.1 5.4 collective-permute-done.23
  326.7 2.0 collective-permute-start.27
  330.6 2.8 collective-permute-done.27
  339.3 4.7 multiply_multiply_fusion.46
  347.4 2.5 multiply_multiply_fusion.47
  393.0 3.5 fusion.105
  396.5 3.5 fusion.109
  400.1 3.7 fusion.113
  403.9 2.2 fusion.117
  406.3 2.2 fusion.121
  408.6 2.4 fusion.125
  411.1 2.2 fusion.129
  413.3 2.2 fusion.133
  415.5 2.7 select_bitcast_fusion.2
  420.1 2.0 collective-permute-start.32
  422.1 2.0 collective-permute-start.33
  424.8 46.3 %collective-permute-done.30 = f32[3,4,19,19,128]{4,1,3,2,0:T(4,128)S(1)} collective-permute-done((f32[3,4,19,19,128]{4,1,3,2,0:T(4,128)S(1)}, f32[3,4,19,19,128]{4,1,3,2,0:T(4,128)S(1)}, u32[]{:S(2)}, u32[]{:S(2)}) %collective-permute-start.30) | collective-permute-done | bytes 2218016 | tf_op jit(solution)/shard_map/ppermute | solution.py:15
  471.1 46.1 %collective-permute-done.31 = f32[3,4,19,19,128]{4,1,3,2,0:T(4,128)S(1)} collective-permute-done((f32[3,4,19,19,128]{4,1,3,2,0:T(4,128)S(1)}, f32[3,4,19,19,128]{4,1,3,2,0:T(4,128)S(1)}, u32[]{:S(2)}, u32[]{:S(2)}) %collective-permute-start.31) | collective-permute-done | bytes 2218016 | tf_op jit(solution)/shard_map/ppermute | solution.py:15
  517.2 45.4 %collective-permute-done.33 = f32[3,4,19,19,128]{4,1,3,2,0:T(4,128)S(1)} collective-permute-done((f32[3,4,19,19,128]{4,1,3,2,0:T(4,128)S(1)}, f32[3,4,19,19,128]{4,1,3,2,0:T(4,128)S(1)}, u32[]{:S(2)}, u32[]{:S(2)}) %collective-permute-start.33) | collective-permute-done | bytes 2218016 | tf_op jit(solution)/shard_map/ppermute | solution.py:15
  564.6 16.0 %collective-permute-done.34 = f32[4,19,19,128]{3,0,2,1:T(4,128)S(1)} collective-permute-done((f32[4,19,19,128]{3,0,2,1:T(4,128)S(1)}, f32[4,19,19,128]{3,0,2,1:T(4,128)S(1)}, u32[]{:S(2)}, u32[]{:S(2)}) %collective-permute-start.34) | collective-permute-done | bytes 739360 | tf_op jit(solution)/shard_map/ppermute | solution.py:15
  582.8 3.7 collective-permute-start.37
  587.6 2.9 collective-permute-done.36
  (319 shorter events, 153.8 us)
Async XLA Ops:
  4.1 21.1 %collective-permute-start = (f32[2,16,128]{2,1,0:T(8,128)S(1)}, f32[2,16,128]{2,1,0:T(8,128)S(1)}, u32[]{:S(2)}, u32[]{:S(2)}) collective-permute-start(f32[2,16,128]{2,1,0:T(8,128)S(1)} %get-tuple-element.235), channel_id=1, source_target_pairs={{4,0},{8,4},{12,8},{16,12},{20,16},{24,20},{28,24},{0,28},{5,1},{9... | collective-permute-start | bytes 49160 | tf_op jit(solution)/shard_map/ppermute | solution.py:27
  10.2 15.0 %collective-permute-start.2 = (f32[2,16,128]{2,1,0:T(8,128)S(1)}, f32[2,16,128]{2,1,0:T(8,128)S(1)}, u32[]{:S(2)}, u32[]{:S(2)}) collective-permute-start(f32[2,16,128]{2,1,0:T(8,128)S(1)} %get-tuple-element.234), channel_id=1, source_target_pairs={{0,4},{4,8},{8,12},{12,16},{16,20},{20,24},{24,28},{28,0},{1,5},{5... | collective-permute-start | bytes 49160 | tf_op jit(solution)/shard_map/ppermute | solution.py:25
  11.4 14.3 %collective-permute-start.3 = (f32[3,1,16,128]{3,0,2,1:T(4,128)S(1)}, f32[3,1,16,128]{3,0,2,1:T(4,128)S(1)}, u32[]{:S(2)}, u32[]{:S(2)}) collective-permute-start(f32[3,1,16,128]{3,0,2,1:T(4,128)S(1)} %get-tuple-element.227), channel_id=1, source_target_pairs={{0,4},{4,8},{8,12},{12,16},{16,20},{20,24},{24,28},{28,0},{1,5},{5... | collective-permute-start | bytes 73736 | tf_op jit(solution)/shard_map/ppermute | solution.py:25
  11.5 14.6 %collective-permute-start.1 = (f32[3,1,16,128]{3,0,2,1:T(4,128)S(1)}, f32[3,1,16,128]{3,0,2,1:T(4,128)S(1)}, u32[]{:S(2)}, u32[]{:S(2)}) collective-permute-start(f32[3,1,16,128]{3,0,2,1:T(4,128)S(1)} %get-tuple-element.226), channel_id=1, source_target_pairs={{4,0},{8,4},{12,8},{16,12},{20,16},{24,20},{28,24},{0,28},{5,1},{9... | collective-permute-start | bytes 73736 | tf_op jit(solution)/shard_map/ppermute | solution.py:27
  18.3 7.5 %copy-start.43 = (f32[3,16,16,128]{3,2,1,0:T(8,128)S(1)}, f32[3,16,16,128]{3,2,1,0:T(8,128)}, u32[]{:S(2)}) copy-start(f32[3,16,16,128]{3,2,1,0:T(8,128)} %param.8) | copy-start | bytes 1179652
  25.2 2.3 collective-permute-start.4
  25.4 3.4 collective-permute-start.6
  26.2 3.9 collective-permute-start.5
  27.5 3.8 collective-permute-start.7
  33.3 4.0 collective-permute-start.8
  35.3 6.6 %collective-permute-start.9 = (f32[3,1,16,128]{3,0,2,1:T(4,128)S(1)}, f32[3,1,16,128]{3,0,2,1:T(4,128)S(1)}, u32[]{:S(2)}, u32[]{:S(2)}) collective-permute-start(f32[3,1,16,128]{3,0,2,1:T(4,128)S(1)} %get-tuple-element.220), channel_id=1, source_target_pairs={{0,4},{4,8},{8,12},{12,16},{16,20},{20,24},{24,28},{28,0},{1,5},{5... | collective-permute-start | bytes 73736 | tf_op jit(solution)/shard_map/ppermute | solution.py:25
  41.9 1.7 collective-permute-start.10
  42.0 3.5 collective-permute-start.11
  42.9 4.2 copy-start.47
  108.9 3.6 copy-start.42
  133.2 51.1 %collective-permute-start.12 = (f32[3,4,19,19,128]{4,1,3,2,0:T(4,128)S(1)}, f32[3,4,19,19,128]{4,1,3,2,0:T(4,128)S(1)}, u32[]{:S(2)}, u32[]{:S(2)}) collective-permute-start(f32[3,4,19,19,128]{4,1,3,2,0:T(4,128)S(1)} %get-tuple-element.22), channel_id=1, source_target_pairs={{0,24},{4,28},{8,0},{12,4},{16,8},{20,12},{24,16},{28,20},{1,25},{... | collective-permute-start | bytes 6653960 | tf_op jit(solution)/shard_map/ppermute | solution.py:15
  133.3 97.5 %collective-permute-start.13 = (f32[3,4,19,19,128]{4,1,3,2,0:T(4,128)S(1)}, f32[3,4,19,19,128]{4,1,3,2,0:T(4,128)S(1)}, u32[]{:S(2)}, u32[]{:S(2)}) collective-permute-start(f32[3,4,19,19,128]{4,1,3,2,0:T(4,128)S(1)} %get-tuple-element.23), channel_id=1, source_target_pairs={{0,28},{4,0},{8,4},{12,8},{16,12},{20,16},{24,20},{28,24},{1,29},{... | collective-permute-start | bytes 6653960 | tf_op jit(solution)/shard_map/ppermute | solution.py:15
  133.3 97.4 %collective-permute-start.14 = (f32[3,4,19,19,128]{4,1,3,2,0:T(4,128)S(1)}, f32[3,4,19,19,128]{4,1,3,2,0:T(4,128)S(1)}, u32[]{:S(2)}, u32[]{:S(2)}) collective-permute-start(f32[3,4,19,19,128]{4,1,3,2,0:T(4,128)S(1)} %get-tuple-element.24), channel_id=1, source_target_pairs={{0,4},{4,8},{8,12},{12,16},{16,20},{20,24},{24,28},{28,0},{1,5},{5... | collective-permute-start | bytes 6653960 | tf_op jit(solution)/shard_map/ppermute | solution.py:15
  135.3 140.7 %collective-permute-start.15 = (f32[3,4,19,19,128]{4,1,3,2,0:T(4,128)S(1)}, f32[3,4,19,19,128]{4,1,3,2,0:T(4,128)S(1)}, u32[]{:S(2)}, u32[]{:S(2)}) collective-permute-start(f32[3,4,19,19,128]{4,1,3,2,0:T(4,128)S(1)} %get-tuple-element.25), channel_id=1, source_target_pairs={{0,8},{4,12},{8,16},{12,20},{16,24},{20,28},{24,0},{28,4},{1,9},{5... | collective-permute-start | bytes 6653960 | tf_op jit(solution)/shard_map/ppermute | solution.py:15
  277.7 16.8 %collective-permute-start.16 = (f32[4,19,19,128]{3,0,2,1:T(4,128)S(1)}, f32[4,19,19,128]{3,0,2,1:T(4,128)S(1)}, u32[]{:S(2)}, u32[]{:S(2)}) collective-permute-start(f32[4,19,19,128]{3,0,2,1:T(4,128)S(1)} %get-tuple-element.20), channel_id=1, source_target_pairs={{0,3},{1,0},{2,1},{3,2},{4,7},{5,4},{6,5},{7,6},{8,11},{9,8},{10,9... | collective-permute-start | bytes 2217992 | tf_op jit(solution)/shard_map/ppermute | solution.py:15
  277.8 18.2 %collective-permute-start.17 = (f32[4,19,19,128]{3,0,2,1:T(4,128)S(1)}, f32[4,19,19,128]{3,0,2,1:T(4,128)S(1)}, u32[]{:S(2)}, u32[]{:S(2)}) collective-permute-start(f32[4,19,19,128]{3,0,2,1:T(4,128)S(1)} %get-tuple-element.21), channel_id=1, source_target_pairs={{0,1},{1,2},{2,3},{3,0},{4,5},{5,6},{6,7},{7,4},{8,9},{9,10},{10,1... | collective-permute-start | bytes 2217992 | tf_op jit(solution)/shard_map/ppermute | solution.py:15
  296.3 7.6 %collective-permute-start.19 = (f32[4,2,19,128]{3,0,2,1:T(4,128)S(1)}, f32[4,2,19,128]{3,0,2,1:T(4,128)S(1)}, u32[]{:S(2)}, u32[]{:S(2)}) collective-permute-start(f32[4,2,19,128]{3,0,2,1:T(4,128)S(1)} %slice.1365), channel_id=1, source_target_pairs={{0,4},{4,8},{8,12},{12,16},{16,20},{20,24},{24,28},{28,0},{1,5},{5... | collective-permute-start | bytes 233480 | tf_op jit(solution)/shard_map/ppermute | solution.py:15
  299.7 4.1 collective-permute-start.18
  303.9 6.5 %collective-permute-start.21 = (f32[4,16,2,128]{3,0,2,1:T(4,128)S(1)}, f32[4,16,2,128]{3,0,2,1:T(4,128)S(1)}, u32[]{:S(2)}, u32[]{:S(2)}) collective-permute-start(f32[4,16,2,128]{3,0,2,1:T(4,128)S(1)} %slice.1368), channel_id=1, source_target_pairs={{0,1},{1,2},{2,3},{3,0},{4,5},{5,6},{6,7},{7,4},{8,9},{9,10},{10,1... | collective-permute-start | bytes 196616 | tf_op jit(solution)/shard_map/ppermute | solution.py:15
  304.0 6.4 %collective-permute-start.20 = (f32[4,16,1,128]{3,0,2,1:T(4,128)S(1)}, f32[4,16,1,128]{3,0,2,1:T(4,128)S(1)}, u32[]{:S(2)}, u32[]{:S(2)}) collective-permute-start(f32[4,16,1,128]{3,0,2,1:T(4,128)S(1)} %slice.1367), channel_id=1, source_target_pairs={{0,3},{1,0},{2,1},{3,2},{4,7},{5,4},{6,5},{7,6},{8,11},{9,8},{10,9... | collective-permute-start | bytes 98312 | tf_op jit(solution)/shard_map/ppermute | solution.py:15
  310.5 5.5 collective-permute-start.22
  314.5 7.0 %collective-permute-start.23 = (f32[3,1,16,128]{3,0,2,1:T(4,128)S(1)}, f32[3,1,16,128]{3,0,2,1:T(4,128)S(1)}, u32[]{:S(2)}, u32[]{:S(2)}) collective-permute-start(f32[3,1,16,128]{3,0,2,1:T(4,128)S(1)} %get-tuple-element.214), channel_id=1, source_target_pairs={{0,4},{4,8},{8,12},{12,16},{16,20},{20,24},{24,28},{28,0},{1,5},{5... | collective-permute-start | bytes 73736 | tf_op jit(solution)/shard_map/ppermute | solution.py:25
  321.5 1.7 collective-permute-start.24
  321.6 3.5 collective-permute-start.25
  326.6 4.0 collective-permute-start.26
  326.7 6.7 %collective-permute-start.27 = (f32[3,1,16,128]{3,0,2,1:T(4,128)S(1)}, f32[3,1,16,128]{3,0,2,1:T(4,128)S(1)}, u32[]{:S(2)}, u32[]{:S(2)}) collective-permute-start(f32[3,1,16,128]{3,0,2,1:T(4,128)S(1)} %get-tuple-element.208), channel_id=1, source_target_pairs={{0,4},{4,8},{8,12},{12,16},{16,20},{20,24},{24,28},{28,0},{1,5},{5... | collective-permute-start | bytes 73736 | tf_op jit(solution)/shard_map/ppermute | solution.py:25
  333.4 1.7 collective-permute-start.28
  333.4 3.4 collective-permute-start.29
  400.1 3.7 copy-start.34
  400.1 3.7 copy-start.35
  400.1 3.7 copy-start.36
  400.1 3.7 copy-start.37
  400.1 3.7 copy-start.38
  420.0 51.1 %collective-permute-start.30 = (f32[3,4,19,19,128]{4,1,3,2,0:T(4,128)S(1)}, f32[3,4,19,19,128]{4,1,3,2,0:T(4,128)S(1)}, u32[]{:S(2)}, u32[]{:S(2)}) collective-permute-start(f32[3,4,19,19,128]{4,1,3,2,0:T(4,128)S(1)} %get-tuple-element.16), channel_id=1, source_target_pairs={{0,24},{4,28},{8,0},{12,4},{16,8},{20,12},{24,16},{28,20},{1,25},{... | collective-permute-start | bytes 6653960 | tf_op jit(solution)/shard_map/ppermute | solution.py:15
  420.0 97.1 %collective-permute-start.31 = (f32[3,4,19,19,128]{4,1,3,2,0:T(4,128)S(1)}, f32[3,4,19,19,128]{4,1,3,2,0:T(4,128)S(1)}, u32[]{:S(2)}, u32[]{:S(2)}) collective-permute-start(f32[3,4,19,19,128]{4,1,3,2,0:T(4,128)S(1)} %get-tuple-element.17), channel_id=1, source_target_pairs={{0,28},{4,0},{8,4},{12,8},{16,12},{20,16},{24,20},{28,24},{1,29},{... | collective-permute-start | bytes 6653960 | tf_op jit(solution)/shard_map/ppermute | solution.py:15
  420.1 97.1 %collective-permute-start.32 = (f32[3,4,19,19,128]{4,1,3,2,0:T(4,128)S(1)}, f32[3,4,19,19,128]{4,1,3,2,0:T(4,128)S(1)}, u32[]{:S(2)}, u32[]{:S(2)}) collective-permute-start(f32[3,4,19,19,128]{4,1,3,2,0:T(4,128)S(1)} %get-tuple-element.18), channel_id=1, source_target_pairs={{0,4},{4,8},{8,12},{12,16},{16,20},{20,24},{24,28},{28,0},{1,5},{5... | collective-permute-start | bytes 6653960 | tf_op jit(solution)/shard_map/ppermute | solution.py:15
  422.1 140.4 %collective-permute-start.33 = (f32[3,4,19,19,128]{4,1,3,2,0:T(4,128)S(1)}, f32[3,4,19,19,128]{4,1,3,2,0:T(4,128)S(1)}, u32[]{:S(2)}, u32[]{:S(2)}) collective-permute-start(f32[3,4,19,19,128]{4,1,3,2,0:T(4,128)S(1)} %get-tuple-element.19), channel_id=1, source_target_pairs={{0,8},{4,12},{8,16},{12,20},{16,24},{20,28},{24,0},{28,4},{1,9},{5... | collective-permute-start | bytes 6653960 | tf_op jit(solution)/shard_map/ppermute | solution.py:15
  564.1 16.6 %collective-permute-start.34 = (f32[4,19,19,128]{3,0,2,1:T(4,128)S(1)}, f32[4,19,19,128]{3,0,2,1:T(4,128)S(1)}, u32[]{:S(2)}, u32[]{:S(2)}) collective-permute-start(f32[4,19,19,128]{3,0,2,1:T(4,128)S(1)} %get-tuple-element.14), channel_id=1, source_target_pairs={{0,3},{1,0},{2,1},{3,2},{4,7},{5,4},{6,5},{7,6},{8,11},{9,8},{10,9... | collective-permute-start | bytes 2217992 | tf_op jit(solution)/shard_map/ppermute | solution.py:15
  564.1 18.3 %collective-permute-start.35 = (f32[4,19,19,128]{3,0,2,1:T(4,128)S(1)}, f32[4,19,19,128]{3,0,2,1:T(4,128)S(1)}, u32[]{:S(2)}, u32[]{:S(2)}) collective-permute-start(f32[4,19,19,128]{3,0,2,1:T(4,128)S(1)} %get-tuple-element.15), channel_id=1, source_target_pairs={{0,1},{1,2},{2,3},{3,0},{4,5},{5,6},{6,7},{7,4},{8,9},{9,10},{10,1... | collective-permute-start | bytes 2217992 | tf_op jit(solution)/shard_map/ppermute | solution.py:15
  582.8 7.7 %collective-permute-start.37 = (f32[4,2,19,128]{3,0,2,1:T(4,128)S(1)}, f32[4,2,19,128]{3,0,2,1:T(4,128)S(1)}, u32[]{:S(2)}, u32[]{:S(2)}) collective-permute-start(f32[4,2,19,128]{3,0,2,1:T(4,128)S(1)} %slice.1485), channel_id=1, source_target_pairs={{0,4},{4,8},{8,12},{12,16},{16,20},{20,24},{24,28},{28,0},{1,5},{5... | collective-permute-start | bytes 233480 | tf_op jit(solution)/shard_map/ppermute | solution.py:15
  586.5 4.0 collective-permute-start.36
  590.5 3.7 collective-permute-start.39
  590.6 3.3 collective-permute-start.38
  (42 other events, 103.7 us)
where the time goes:
time: 604 us; the launch traced here: 596 us
  waiting for transfers between devices  346 us (57%)
  local copies, waits for them, and re-layouts  107 us (18%)
  other arithmetic  85.6 us (14%)
  starting transfers between devices  45.4 us (8%)
  between operations  12.6 us (2%)
    ppermute x20, waiting for transfers between devices, shifted(): return lax.ppermute(value, axis, pairs)  319 us
    slice x96, local copies, waits for them, and re-layouts, spread_back(): column = column + jnp.roll(weighted * weights_z[off_z], off_z - 1, -1)  96.6 us
    add x16, other arithmetic, spread_back(): column = column + jnp.roll(weighted * weights_z[off_z], off_z - 1, -1)  45 us
    ppermute x20, starting transfers between devices, shifted(): return lax.ppermute(value, axis, pairs)  22.4 us
    ppermute x10, waiting for transfers between devices, extended(): lax.ppermute(tail, axis, [(i, (i + 1) % count) for i in range(count)])  20.7 us
    ppermute x10, starting transfers between devices, extended(): lax.ppermute(head, axis, [((i + 1) % count, i) for i in range(count)])  18.5 us
    mul x6, other arithmetic, spread_back(): column = column + jnp.roll(weighted * weights_z[off_z], off_z - 1, -1)  15.7 us
  transfers between devices with their start and end apart: 40, of which 28 were waited for; matrix products, arithmetic and copies ran while one was open for 2% of the time, Pallas kernels for 0%

commit v1 on v0

v1 whole, which is shorter than its diff:
```python
import functools

import jax
import jax.numpy as jnp
from jax import lax
from jax.experimental import pallas as pl
from jax.experimental.pallas import tpu as pltpu
from jax.sharding import PartitionSpec as P

STEPS = 2
BUOYANCY = 0.8
FIELDS = 4
SUB = 8
VMEM = pl.BlockSpec(memory_space=pltpu.VMEM)
SMEM = pl.BlockSpec(memory_space=pltpu.SMEM)


def call(body, outs, args, specs, scratch=(), flops=1000000, name=None):
    moved = sum(a.size for a in args) * 4 + sum(o.size for o in outs) * 4
    return pl.pallas_call(
        body,
        out_shape=tuple(outs),
        in_specs=list(specs),
        out_specs=tuple(VMEM for _ in outs),
        scratch_shapes=list(scratch),
        compiler_params=pltpu.CompilerParams(vmem_limit_bytes=40 * 1024 * 1024),
        cost_estimate=pl.CostEstimate(flops=flops, bytes_accessed=moved, transcendentals=0),
        name=name,
    )(*args)


def f32(*shape):
    return jax.ShapeDtypeStruct(shape, jnp.float32)


def sublane(shape):
    return lax.broadcasted_iota(jnp.int32, shape, 0)


def turn(v, steps, axis):
    return pltpu.roll(v, steps % v.shape[axis], axis)


def cubic_weights(position):
    squared = position * position
    cubed = squared * position
    return (
        (2.0 * squared - cubed - position) * 0.5,
        (3.0 * cubed - 5.0 * squared + 2.0) * 0.5,
        (4.0 * squared - 3.0 * cubed + position) * 0.5,
        (cubed - squared) * 0.5,
    )


def prep_body(cx, cy, level, vel, labels, rates, state, rate, top, bot, left, right, c00, c01, c10, c11):
    pairs = cy // 2

    def row(x, _):
        state[x, pl.ds(0, cy, stride=FIELDS), :] = level[x]
        for f in range(3):
            state[x, pl.ds(f + 1, cy, stride=FIELDS), :] = vel[f, x]
        cell = jnp.where(labels[x] == 1, rates[1], rates[0])
        for f in range(FIELDS):
            rate[x, pl.ds(f, cy, stride=FIELDS), :] = cell
        return 0

    lax.fori_loop(0, cx, row, 0)

    def mixed(x, q):
        at = pl.ds(SUB * q, SUB)
        is_level = sublane(state[x, at, :].shape) % FIELDS == 0
        return jnp.where(is_level, rate[x, at, :], state[x, at, :])

    for k in range(2):
        for q in range(pairs):
            top[k * pairs + q] = mixed(k, q)
            bot[k * pairs + q] = mixed(cx - 2 + k, q)
    for x in range(cx):
        left[x] = mixed(x, 0)
        right[x] = mixed(x, pairs - 1)
    c00[0] = left[0]
    c01[0] = right[0]
    c10[0] = left[cx - 1]
    c11[0] = right[cx - 1]


def weights_body(cx, cy, step, fraction, out):
    def row(x, _):
        for d in range(3):
            for k, w in enumerate(cubic_weights(fraction[step, d, x])):
                for f in range(FIELDS):
                    out[4 * d + k, x, pl.ds(f, cy, stride=FIELDS), :] = w
        return 0

    lax.fori_loop(0, cx, row, 0)


def fill(pad, cx, pairs, own, xm, xp, ym, yp, c00, c01, c10, c11, change):
    wide = pairs + 2

    def row(x, _):
        for q in range(pairs):
            pad[(x + 2) * wide + q + 1] = own(x, q)
        pad[(x + 2) * wide] = change(ym[x])
        pad[(x + 2) * wide + pairs + 1] = change(yp[x])
        return 0

    lax.fori_loop(0, cx, row, 0)
    for k in range(2):
        for q in range(pairs):
            pad[k * wide + q + 1] = change(xm[k * pairs + q])
            pad[(cx + 2 + k) * wide + q + 1] = change(xp[k * pairs + q])
    pad[wide] = change(c00[0])
    pad[wide + pairs + 1] = change(c01[0])
    pad[(cx + 2) * wide] = change(c10[0])
    pad[(cx + 2) * wide + pairs + 1] = change(c11[0])


def coef_body(cx, pairs, rate, xm, xp, ym, yp, c00, c01, c10, c11, ax, yu, yd, zu, zd, c0, pad):
    wide = pairs + 2
    shape = pad.shape[1:]
    field = sublane(shape) % FIELDS
    half = sublane(shape) < FIELDS
    scale = jnp.where(field == 0, 0.0, 0.5)

    def spread_rate(v):
        v = jnp.where(field == 0, v, 0.0)
        v = v + turn(v, 1, 0)
        return v + turn(v, 2, 0)

    for k in (0, cx + 3):
        pad[k * wide] = jnp.zeros(shape, jnp.float32)
        pad[k * wide + pairs + 1] = jnp.zeros(shape, jnp.float32)
    fill(pad, cx, pairs, lambda x, q: rate[x * pairs + q], xm, xp, ym, yp, c00, c01, c10, c11, spread_rate)

    def faces(x, _):
        for j in range(wide):
            ax[x * wide + j] = (pad[x * wide + j] + pad[(x + 1) * wide + j]) * scale
        return 0

    lax.fori_loop(0, cx + 3, faces, 0)

    def row(x, _):
        flipped = [turn(pad[(x + 1) * wide + j], FIELDS, 0) for j in range(wide)]
        for j in range(wide):
            own = pad[(x + 1) * wide + j]
            up = jnp.where(half, flipped[j], flipped[min(j + 1, wide - 1)])
            down = jnp.where(half, flipped[max(j - 1, 0)], flipped[j])
            at = x * wide + j
            cyu = (own + up) * scale
            cyd = (own + down) * scale
            czu = (own + turn(own, -1, 1)) * scale
            czd = (own + turn(own, 1, 1)) * scale
            yu[at] = cyu
            yd[at] = cyd
            zu[at] = czu
            zd[at] = czd
            c0[at] = 1.0 - (ax[at] + ax[at + wide] + cyu + cyd + czu + czd)
        return 0

    lax.fori_loop(0, cx + 2, row, 0)


def sweep_row(src, base, lo, hi, coefs, at, half):
    ax, yu, yd, zu, zd, c0, wide = coefs
    own = {j: src[base + j] for j in range(max(lo - 1, 0), min(hi + 1, wide))}
    flipped = {j: turn(v, FIELDS, 0) for j, v in own.items()}
    for j in range(lo, hi):
        up = jnp.where(half, flipped[j], flipped.get(j + 1, flipped[j]))
        down = jnp.where(half, flipped.get(j - 1, flipped[j]), flipped[j])
        v = own[j]
        k = at + j
        total = c0[k] * v + ax[k] * src[base - wide + j] + ax[k + wide] * src[base + wide + j]
        total = total + yu[k] * up + yd[k] * down
        total = total + zu[k] * turn(v, -1, 1) + zd[k] * turn(v, 1, 1)
        yield j, total


def diffuse(cx, pairs, own, halos, coefs, pad, mid, g):
    wide = pairs + 2
    shape = pad.shape[1:]
    half = sublane(shape) < FIELDS
    lift = jnp.where(sublane(shape) % FIELDS == 0, BUOYANCY, 0.0)
    fill(pad, cx, pairs, lambda x, q: own[x * pairs + q], *halos, lambda v: v)
    coefs = coefs + (wide,)
    for r in (0, cx + 1):
        for j, v in sweep_row(pad, (r + 1) * wide, 1, pairs + 1, coefs, r * wide, half):
            mid[r * wide + j] = v

    def first(r, _):
        for j, v in sweep_row(pad, (r + 1) * wide, 0, wide, coefs, r * wide, half):
            mid[r * wide + j] = v
        return 0

    lax.fori_loop(1, cx + 1, first, 0)
    zero = jnp.zeros(shape, jnp.float32)
    for k in range(3 * pairs):
        g[k] = zero
        g[(cx + 3) * pairs + k] = zero

    def second(r, _):
        for j, v in sweep_row(mid, r * wide, 1, pairs + 1, coefs, r * wide, half):
            g[(r + 2) * pairs + j - 1] = v + lift * turn(v, -3, 0)
        return 0

    lax.fori_loop(1, cx + 1, second, 0)


def patch_row(g, w, cx, pairs, at):
    shape = g.shape[1:]
    half = sublane(shape) < FIELDS
    rows = [(at + 1 - a + 3, jnp.clip(at + 1 - a, 0, cx - 1)) for a in range(4)]
    before = None
    out = []
    zero = jnp.zeros(shape, jnp.float32)

    def finish(acc0, acc1, acc1_before):
        flipped = turn(acc1, FIELDS, 0) if acc1 is not None else zero
        flipped_before = turn(acc1_before, FIELDS, 0) if acc1_before is not None else zero
        value = jnp.where(half, flipped_before, flipped)
        return value if acc0 is None else acc0 + value

    p1 = p2 = p3 = p3_old = acc1_old = None
    for q in range(pairs):
        sums = [[None] * 4 for _ in range(4)]
        for a in range(4):
            padded, row = rows[a]
            k = pl.ds(SUB * q, SUB)
            h = g[padded * pairs + q] * w[a, row, k, :]
            wy = [w[4 + b, row, k, :] for b in range(4)]
            for c in range(4):
                hc = h * w[8 + c, row, k, :]
                for b in range(4):
                    t = hc * wy[b]
                    sums[b][c] = t if sums[b][c] is None else sums[b][c] + t
        p = []
        for b in range(4):
            s = sums[b]
            p.append((turn(s[0], -1, 1) + s[1]) + (turn(s[2], 1, 1) + turn(s[3], 2, 1)))
        acc1 = p[0] if p2 is None else p2 + p[0]
        acc0 = p1 if p3_old is None else p1 + p3_old
        out.append(finish(acc0, acc1, acc1_old))
        p3_old = p3
        p1, p2, p3 = p[1], p[2], p[3]
        acc1_old = acc1
    out.append(finish(p1 if p3_old is None else p1 + p3_old, p2, acc1_old))
    out.append(finish(p3, None, p2))
    return out


def spread(cx, pairs, rows_of, count, g, w, shift_x, shift_y, step, own, right, left, far):
    shape = g.shape[1:]
    move_x = shift_x[0, 0, step]
    move_y = shift_y[0, 0, step]
    here = jnp.where(move_y == 0, 1.0, 0.0)
    up = jnp.where(move_y == 1, 1.0, 0.0)
    down = jnp.where(move_y == -1, 1.0, 0.0)

    def row(i, _):
        out = patch_row(g, w, cx, pairs, rows_of(i))
        low, high = out[0], out[pairs + 1]
        for q in range(pairs):
            v = out[q + 1]
            o, r, l = v * here, v * up, v * down
            if q == 0:
                o = o + high * down
                r = r + high * here
            if q == pairs - 1:
                o = o + low * up
                l = l + low * here
            own[i * pairs + q] = o
            right[i * pairs + q] = r
            left[i * pairs + q] = l
        far[i] = high * up + low * down
        return 0

    lax.fori_loop(0, count, row, 0)
    mx = jnp.full(shape, move_x.astype(jnp.float32))
    right[count * pairs] = mx
    left[count * pairs] = mx
    far[count] = mx
    far[count + 1] = jnp.full(shape, move_y.astype(jnp.float32))


def diffuse_spread_body(cx, pairs, step, rows_of, count, *refs):
    own, halos, coefs, w, sx, sy = refs[0], refs[1:9], refs[9:15], refs[15], refs[16], refs[17]
    o, r, l, far, g, pad, mid = refs[18:]
    diffuse(cx, pairs, own, halos, coefs, pad, mid, g)
    spread(cx, pairs, rows_of, count, g, w, sx, sy, step, o, r, l, far)


def spread_body(cx, pairs, step, rows_of, count, g, w, sx, sy, o, r, l, far):
    spread(cx, pairs, rows_of, count, g, w, sx, sy, step, o, r, l, far)


def gather_body(pairs, step, main, rim_at, edge_of, has_high, has_low, *refs):
    own, right, left, far_low, far_high, sx, parity = refs[:7]
    e1, e0, f, k, t0, x3 = refs[7:]
    shape = own.shape[1:]
    count = own.shape[0] // pairs
    mine = jnp.full(shape, sx[0, 0, step].astype(jnp.float32))
    moves = (mine, right[count * pairs], left[count * pairs])
    far_moves = (far_low[count], far_high[count])
    far_gates = (far_low[count + 1] == 1.0, far_high[count + 1] == -1.0)
    side = parity[0]
    targets = (side, -side, 2 * side, -2 * side, 0)
    outs = (e1, e0, f, k, t0)

    def hit(move, t):
        t = t.astype(jnp.float32) if hasattr(t, "astype") else float(t)
        return jnp.where(move == t, 1.0, 0.0)

    def total(masks, fars, i, q):
        v = masks[0] * own[i * pairs + q] + masks[1] * right[i * pairs + q] + masks[2] * left[i * pairs + q]
        if q == 0:
            v = v + fars[0] * far_low[i]
        if q == pairs - 1:
            v = v + fars[1] * far_high[i]
        return v

    def masks_of(t):
        masks = [hit(m, t) for m in moves]
        fars = [jnp.where(gate, hit(m, t), 0.0) for gate, m in zip(far_gates, far_moves)]
        return masks, fars

    for out, t in zip(outs, targets):
        masks, fars = masks_of(t)

        def row(i, _, out=out, masks=masks, fars=fars):
            for q in range(pairs):
                out[i * pairs + q] = total(masks, fars, i + rim_at, q)
            return 0

        lax.fori_loop(0, main, row, 0)
        masks, fars = masks_of(t + edge_of)
        for source, row_at in (has_high or ()) + (has_low or ()):
            for q in range(pairs):
                out[row_at * pairs + q] = out[row_at * pairs + q] + total(masks, fars, source, q)
    masks, fars = masks_of(2 if has_high else -2)
    for n, (source, _) in enumerate((has_high or ()) + (has_low or ())):
        for q in range(pairs):
            x3[n * pairs + q] = total(masks, fars, source, q)


def merge(cx, pairs, main, parts, state):
    (t0a, e0a, fa, da, xa), (t0b, e0b, fb, db, xb) = parts
    for base, (t0, e0, f, d) in ((0, (t0a, e0a, fa, da)), (main[0], (t0b, e0b, fb, db))):

        def row(i, _, base=base, t0=t0, e0=e0, f=f, d=d):
            for q in range(pairs):
                at = i * pairs + q
                state((base + i), q, (t0[at] + e0[at]) + (f[at] + d[at]), False)
            return 0

        lax.fori_loop(0, main[0] if base == 0 else main[1], row, 0)
    for q in range(pairs):
        for k in range(2):
            state(k, q, xa[k * pairs + q], True)
        state(cx - 1, q, xb[q], True)


def merge_body(cx, pairs, main, *refs):
    parts = (refs[0:5], refs[5:10])
    out, top, bot, left, right, c00, c01, c10, c11 = refs[10:]

    def put(x, q, v, add):
        at = x * pairs + q
        out[at] = out[at] + v if add else v

    merge(cx, pairs, main, parts, put)
    for k in range(2 * pairs):
        top[k] = out[k]
        bot[k] = out[(cx - 2) * pairs + k]
    for x in range(cx):
        left[x] = out[x * pairs]
        right[x] = out[x * pairs + pairs - 1]
    c00[0] = left[0]
    c01[0] = right[0]
    c10[0] = left[cx - 1]
    c11[0] = right[cx - 1]


def finish_body(cx, cy, pairs, main, *refs):
    parts = (refs[0:5], refs[5:10])
    level, vel, out = refs[10:]

    def put(x, q, v, add):
        at = pl.ds(SUB * q, SUB)
        out[x, at, :] = out[x, at, :] + v if add else v

    merge(cx, pairs, main, parts, put)

    def row(x, _):
        level[x] = out[x, pl.ds(0, cy, stride=FIELDS), :]
        for f in range(3):
            vel[f, x] = out[x, pl.ds(f + 1, cy, stride=FIELDS), :]
        return 0

    lax.fori_loop(0, cx, row, 0)


def moved(value, axis, steps):
    count = lax.axis_size(axis)
    return lax.ppermute(value, axis, [(i, (i + steps) % count) for i in range(count)])


def moved_both(value, step_x, step_y):
    nx, ny = lax.axis_size("gx"), lax.axis_size("gy")
    pairs = [
        (x * ny + y, ((x + step_x) % nx) * ny + (y + step_y) % ny)
        for x in range(nx)
        for y in range(ny)
    ]
    return lax.ppermute(value, ("gx", "gy"), pairs)


def swapped(value):
    return lax.ppermute(value, "gx", [(i, i ^ 1) for i in range(lax.axis_size("gx"))])


def crossed(value, sign):
    count = lax.axis_size("gx")
    return lax.ppermute(
        value, "gx", [(i, (i + (2 if i % 2 else -2) * sign) % count) for i in range(count)]
    )


def exchange(top, bot, left, right, c00, c01, c10, c11):
    xm = moved(bot, "gx", 1)
    xp = moved(top, "gx", -1)
    ym = moved(right, "gy", 1)
    yp = moved(left, "gy", -1)
    mm = moved_both(c11, 1, 1)
    mp = moved_both(c10, 1, -1)
    pm = moved_both(c01, -1, 1)
    pp = moved_both(c00, -1, -1)
    return xm, xp, ym, yp, mm, mp, pm, pp


def on_device(level, vel, fraction, shift_x, shift_y, labels, rates):
    cx, cy, cz = level.shape
    pairs = cy // 2
    wide = pairs + 2
    ny = lax.axis_size("gy")
    parity = (2 * (lax.axis_index("gx") % 2) - 1).astype(jnp.int32).reshape(1)
    first = cx // 2
    main = (first, cx - first)

    def plane(n):
        return f32(n, SUB, cz)

    def scratch(n):
        return pltpu.VMEM((n, SUB, cz), jnp.float32)

    halo_outs = (
        [plane(2 * pairs)] * 2 + [plane(cx)] * 2 + [plane(1)] * 4
    )
    state, rate, *edges = call(
        functools.partial(prep_body, cx, cy),
        [f32(cx, FIELDS * cy, cz)] * 2 + halo_outs,
        (level, vel, labels, rates),
        [VMEM, VMEM, VMEM, SMEM],
        name="prep",
    )
    state = state.reshape(cx * pairs, SUB, cz)
    rate = rate.reshape(cx * pairs, SUB, cz)
    halos = exchange(*edges)
    weights = [
        call(
            functools.partial(weights_body, cx, cy, s),
            [f32(12, cx, FIELDS * cy, cz)],
            (fraction,),
            [VMEM],
            name="weights%d" % s,
        )[0]
        for s in range(STEPS)
    ]
    coefs = call(
        functools.partial(coef_body, cx, pairs),
        [plane((cx + 3) * wide)] + [plane((cx + 2) * wide)] * 5,
        (rate, *halos),
        [VMEM] * 9,
        [scratch((cx + 4) * wide)],
        name="coefs",
    )

    def rows_a(i):
        return jnp.where(i < 2, cx + i, i - 2)

    def rows_b(i):
        return jnp.where(i < 1, -1, first - 1 + i)

    counts = (main[0] + 2, main[1] + 1)
    for step in range(STEPS - 1, -1, -1):
        chunks = []
        spec_tail = [VMEM, SMEM, SMEM]

        def outs(n):
            return [plane(n * pairs), plane(n * pairs + 1), plane(n * pairs + 1), plane(n + 2)]

        *sent_a, g = call(
            functools.partial(diffuse_spread_body, cx, pairs, step, rows_a, counts[0]),
            outs(counts[0]) + [plane((cx + 6) * pairs)],
            (state, *halos, *coefs, weights[step], shift_x, shift_y),
            [VMEM] * 15 + spec_tail,
            [scratch((cx + 4) * wide), scratch((cx + 2) * wide)],
            flops=20000000,
            name="diffuse_spread_a%d" % step,
        )
        sent_b = call(
            functools.partial(spread_body, cx, pairs, step, rows_b, counts[1]),
            outs(counts[1]),
            (g, weights[step], shift_x, shift_y),
            [VMEM] + spec_tail,
            flops=10000000,
            name="spread_b%d" % step,
        )
        for n, (own, right, left, far) in enumerate((sent_a, sent_b)):
            right = moved(right, "gy", 1)
            left = moved(left, "gy", -1)
            far_low = moved(far, "gy", 2)
            far_high = far_low if ny == 4 else moved(far, "gy", -2)
            if n == 0:
                args = (2, -1, ((0, 0), (1, 1)), None)
            else:
                args = (1, 1, None, ((0, main[1] - 1),))
            e1, e0, f, k, t0, x3 = call(
                functools.partial(gather_body, pairs, step, main[n], *args),
                [plane(main[n] * pairs)] * 5 + [plane((2 if n == 0 else 1) * pairs)],
                (own, right, left, far_low, far_high, shift_x, parity),
                [VMEM] * 5 + [SMEM] * 2,
                flops=3000000,
                name="gather%d_%d" % (n, step),
            )
            e1 = swapped(e1)
            f = crossed(f, 1)
            x3 = moved(x3, "gx", 3 if n == 0 else -3)
            e0 = swapped(e0)
            d = crossed(k + e1, -1)
            chunks += [t0, e0, f, d, x3]
        if step:
            state, *edges = call(
                functools.partial(merge_body, cx, pairs, main),
                [plane(cx * pairs)] + halo_outs,
                chunks,
                [VMEM] * 10,
                name="merge%d" % step,
            )
            halos = exchange(*edges)
        else:
            return call(
                functools.partial(finish_body, cx, cy, pairs, main),
                [f32(cx, cy, cz), f32(3, cx, cy, cz)],
                chunks,
                [VMEM] * 10,
                [pltpu.VMEM((cx, FIELDS * cy, cz), jnp.float32)],
                name="finish",
            )


def solution(mesh):
    in_specs = (
        P("gx", "gy", None),
        P(None, "gx", "gy", None),
        P(None, None, "gx", "gy", None),
        P("gx", "gy", None),
        P("gx", "gy", None),
        P("gx", "gy", None),
        P(),
    )
    out_specs = (P("gx", "gy", None), P(None, "gx", "gy", None))
    return jax.shard_map(
        on_device, mesh=mesh, in_specs=in_specs, out_specs=out_specs, check_vma=False
    )
```

time: 604 us -> 187 us (0.31); the launches traced: 596 us -> 187 us
  waiting for transfers between devices: 346 us -> 92.2 us
  local copies, waits for them, and re-layouts: 107 us -> 7.27 us
  other arithmetic: 85.6 us -> 0.12 us
  Pallas kernels: 0 us -> 30 us
  between operations: 12.6 us -> 0.94 us
  starting transfers between devices: 45.4 us -> 56 us
    ppermute x40 -> x48, waiting for transfers between devices: 346 us -> 92.2 us  [the longest x8 33.4 us: moved_both(): return lax.ppermute(value, ('gx', 'gy'), pairs)]
    slice x127 -> x0, local copies, waits for them, and re-layouts: 104 us -> none  [the longest x96 96.6 us: spread_back(): column = column + jnp.roll(weighted * weights_z[off_z], off_z - 1, -1)]
    add x30 -> x4, other arithmetic: 55.6 us -> 0.12 us  [on_device(): d = crossed(k + e1, -1)]
    pallas_call x0 -> x14, Pallas kernels: none -> 30 us  [call(): pl.pallas_call(body, out_shape=tuple(outs), in_specs=list(specs), out_spe...]
    mul x11 -> x0, other arithmetic: 18.9 us -> none  [the longest x6 15.7 us: spread_back(): column = column + jnp.roll(weighted * weights_z[off_z], off_z - 1, -1)]
    ppermute x40 -> x48, starting transfers between devices: 45.4 us -> 56 us  [the longest x24 31.7 us: moved(): lax.ppermute(value, axis, [(i, (i + steps) % count) for i in range(count)])]
  transfers between devices with their start and end apart: 40 -> 48, of which waited for: 28 -> 23; matrix products, arithmetic and copies ran while one was open for 2% -> 0% of each run, Pallas kernels for 0% -> 7%
where the time goes in v1:
time: 187 us
  waiting for transfers between devices  92.2 us (49%)
  starting transfers between devices  56 us (30%)
  Pallas kernels  30 us (16%)
  local copies, waits for them, and re-layouts  7.27 us (4%)
    ppermute x8, waiting for transfers between devices, moved_both(): return lax.ppermute(value, ('gx', 'gy'), pairs)  33.4 us
    ppermute x24, starting transfers between devices, moved(): lax.ppermute(value, axis, [(i, (i + steps) % count) for i in range(count)])  31.7 us
    pallas_call x14, Pallas kernels, call(): pl.pallas_call(body, out_shape=tuple(outs), in_specs=list(specs), out_spe...  30 us
    ppermute x24, waiting for transfers between devices, moved(): lax.ppermute(value, axis, [(i, (i + steps) % count) for i in range(count)])  22.8 us
    ppermute x8, waiting for transfers between devices, swapped(): lax.ppermute(value, 'gx', [(i, i ^ 1) for i in range(lax.axis_size('gx'))])  18.4 us
    ppermute x8, waiting for transfers between devices, crossed(): lax.ppermute(value, 'gx', [(i, (i + (2 if i % 2 else -2) * sign) % count)...  17.7 us
    ppermute x8, starting transfers between devices, crossed(): lax.ppermute(value, 'gx', [(i, (i + (2 if i % 2 else -2) * sign) % count)...  14.7 us
    unnamed x36, local copies, waits for them, and re-layouts  7.27 us
  transfers between devices with their start and end apart: 48, of which 23 were waited for; matrix products, arithmetic and copies ran while one was open for 0% of the time, Pallas kernels for 7%

profile of v1, /device:TPU:0, one launch (start us, length us, event | category | flops | bytes accessed | tf_op | source)
XLA Modules:
  0.0 186.7 jit_solution(4719106565544237450)
XLA Ops:
  4.8 3.0 %collective-permute-start = (f32[16,8,128]{2,1,0:T(8,128)S(1)}, f32[16,8,128]{2,1,0:T(8,128)S(1)}, u32[]{:S(2)}, u32[]{:S(2)}) collective-permute-start(f32[16,8,128]{2,1,0:T(8,128)S(1)} %get-tuple-element.70), channel_id=1, source_target_pairs={{0,4},{4,8},{8,12},{12,16},{16,20},{20,24},{24,28},{28,0},{1,5},{5... | collective-permute-start | bytes 196616 | tf_op jit(solution)/shard_map/ppermute | solution.py:404
  7.9 3.1 %collective-permute-start.1 = (f32[16,8,128]{2,1,0:T(8,128)S(1)}, f32[16,8,128]{2,1,0:T(8,128)S(1)}, u32[]{:S(2)}, u32[]{:S(2)}) collective-permute-start(f32[16,8,128]{2,1,0:T(8,128)S(1)} %get-tuple-element.71), channel_id=1, source_target_pairs={{0,28},{4,0},{8,4},{12,8},{16,12},{20,16},{24,20},{28,24},{1,29},{... | collective-permute-start | bytes 196616 | tf_op jit(solution)/shard_map/ppermute | solution.py:404
  11.0 1.7 collective-permute-start.3
  12.7 6.6 %collective-permute-done.4.c00.refs_5_ = f32[1,8,128]{2,1,0:T(8,128)S(1)} collective-permute-done((f32[1,8,128]{2,1,0:T(8,128)S(1)}, f32[1,8,128]{2,1,0:T(8,128)S(1)}, u32[]{:S(2)}, u32[]{:S(2)}) %collective-permute-start.4) | collective-permute-done | bytes 4128 | tf_op jit(solution)/shard_map/ppermute | solution.py:414
  19.3 5.7 %collective-permute-done.5.c01.refs_6_ = f32[1,8,128]{2,1,0:T(8,128)S(1)} collective-permute-done((f32[1,8,128]{2,1,0:T(8,128)S(1)}, f32[1,8,128]{2,1,0:T(8,128)S(1)}, u32[]{:S(2)}, u32[]{:S(2)}) %collective-permute-start.5) | collective-permute-done | bytes 4128 | tf_op jit(solution)/shard_map/ppermute | solution.py:414
  25.1 3.9 %collective-permute-done.6.c10.refs_7_ = f32[1,8,128]{2,1,0:T(8,128)S(1)} collective-permute-done((f32[1,8,128]{2,1,0:T(8,128)S(1)}, f32[1,8,128]{2,1,0:T(8,128)S(1)}, u32[]{:S(2)}, u32[]{:S(2)}) %collective-permute-start.6) | collective-permute-done | bytes 4128 | tf_op jit(solution)/shard_map/ppermute | solution.py:414
  29.0 2.8 %collective-permute-start.7 = (f32[1,8,128]{2,1,0:T(8,128)S(1)}, f32[1,8,128]{2,1,0:T(8,128)S(1)}, u32[]{:S(2)}, u32[]{:S(2)}) collective-permute-start(f32[1,8,128]{2,1,0:T(8,128)S(1)} %get-tuple-element.77), channel_id=1, source_target_pairs={{0,31},{1,28},{2,29},{3,30},{4,3},{5,0},{6,1},{7,2},{8,7},{9,4},{1... | collective-permute-start | bytes 12296 | tf_op jit(solution)/shard_map/ppermute | solution.py:414
  31.8 1.1 copy-done
  33.5 2.0 %coefs.1 = (f32[190,8,128]{2,1,0:T(8,128)S(1)}, f32[180,8,128]{2,1,0:T(8,128)S(1)}, f32[180,8,128]{2,1,0:T(8,128)S(1)}, f32[180,8,128]{2,1,0:T(8,128)S(1)}, f32[...) custom-call(f32[128,8,128]{2,1,0:T(8,128)S(1)} %bitcast.3, f32[16,8,128]{2,1,0:T(8,128)S(1)} %collective-permute-done.xm.refs_1_, ...), custom_call_target="tpu_custom_call" | custom-call | flops 1000000 | bytes 5267456 | tf_op jit(solution)/shard_map/coefs/pallas_call | solution.py:20
  35.6 7.1 %diffuse_spread_a1.1 = (f32[80,8,128]{2,1,0:T(8,128)S(1)}, f32[81,8,128]{2,1,0:T(8,128)}, f32[81,8,128]{2,1,0:T(8,128)}, f32[12,8,128]{2,1,0:T(8,128)S(1)}, f32[176,8,128]{2,1,0:T(8,128)S(1)}) custom-call(f32[128,8,128]{2,1,0:T(8,128)S(1)} %bitcast.4, f32[16,8,128]{2,1,0:T(8,128)S(1)} %collective-permute-done.xm.refs_1_, ...), custom_call_target="tpu_custom_call" | custom-call | flops 20000000 | bytes 13320208 | tf_op jit(solution)/shard_map/diffuse_spread_a1/pallas_call | solution.py:20
  42.7 1.7 collective-permute-start.9
  44.4 3.5 %spread_b1.1 = (f32[72,8,128]{2,1,0:T(8,128)S(1)}, f32[73,8,128]{2,1,0:T(8,128)}, f32[73,8,128]{2,1,0:T(8,128)}, f32[11,8,128]{2,1,0:T(8,128)S(1)}) custom-call(f32[176,8,128]{2,1,0:T(8,128)S(1)} %get-tuple-element.95.g, f32[12,16,64,128]{3,2,1,0:T(8,128)S(1)} %weights1.1.refs_15_.w, s32[1,1,2]{2,1,0:T(1,128)S(1)} %copy-done.15, s32[1,1,2]{2,1,0:T(1,128)S(1)} %copy-done.16), custom_call_target="tpu_custom_call" | custom-call | flops 10000000 | bytes 7950352 | tf_op jit(solution)/shard_map/spread_b1/pallas_call | solution.py:20
  48.7 1.7 collective-permute-start.17
  50.9 9.5 %collective-permute-done.18.refs_3_.refs_4_ = f32[11,8,128]{2,1,0:T(8,128)S(1)} collective-permute-done((f32[11,8,128]{2,1,0:T(8,128)S(1)}, f32[11,8,128]{2,1,0:T(8,128)S(1)}, u32[]{:S(2)}, u32[]{:S(2)}) %collective-permute-start.18) | collective-permute-done | bytes 45088 | tf_op jit(solution)/shard_map/ppermute | solution.py:404
  61.8 1.8 gather1_1.1
  65.4 1.6 gather0_1.1
  67.0 1.3 collective-permute-start.13
  69.1 3.8 %collective-permute-start.23 = (f32[8,8,128]{2,1,0:T(8,128)S(1)}, f32[8,8,128]{2,1,0:T(8,128)S(1)}, u32[]{:S(2)}, u32[]{:S(2)}) collective-permute-start(f32[8,8,128]{2,1,0:T(8,128)S(1)} %get-tuple-element.105), channel_id=1, source_target_pairs={{0,20},{4,24},{8,28},{12,0},{16,4},{20,8},{24,12},{28,16},{1,21},{... | collective-permute-start | bytes 98312 | tf_op jit(solution)/shard_map/ppermute | solution.py:404
  73.9 2.8 %collective-permute-start.20 = (f32[64,8,128]{2,1,0:T(8,128)S(1)}, f32[64,8,128]{2,1,0:T(8,128)S(1)}, u32[]{:S(2)}, u32[]{:S(2)}) collective-permute-start(f32[64,8,128]{2,1,0:T(8,128)S(1)} %get-tuple-element.102), channel_id=1, source_target_pairs={{0,24},{4,12},{8,0},{12,20},{16,8},{20,28},{24,16},{28,4},{1,25},{... | collective-permute-start | bytes 786440 | tf_op jit(solution)/shard_map/ppermute | solution.py:423
  76.7 3.9 %collective-permute-done.13 = f32[64,8,128]{2,1,0:T(8,128)S(1)} collective-permute-done((f32[64,8,128]{2,1,0:T(8,128)S(1)}, f32[64,8,128]{2,1,0:T(8,128)S(1)}, u32[]{:S(2)}, u32[]{:S(2)}) %collective-permute-start.13) | collective-permute-done | bytes 262176 | tf_op jit(solution)/shard_map/ppermute | solution.py:418
  80.6 4.5 %collective-permute-start.12 = (f32[64,8,128]{2,1,0:T(8,128)S(1)}, f32[64,8,128]{2,1,0:T(8,128)S(1)}, u32[]{:S(2)}, u32[]{:S(2)}) collective-permute-start(f32[64,8,128]{2,1,0:T(8,128)S(1)} %get-tuple-element.91), channel_id=1, source_target_pairs={{0,24},{4,12},{8,0},{12,20},{16,8},{20,28},{24,16},{28,4},{1,25},{... | collective-permute-start | bytes 786440 | tf_op jit(solution)/shard_map/ppermute | solution.py:423
  86.2 3.6 %collective-permute-done.11.refs_1_ = f32[64,8,128]{2,1,0:T(8,128)S(1)} collective-permute-done((f32[64,8,128]{2,1,0:T(8,128)S(1)}, f32[64,8,128]{2,1,0:T(8,128)S(1)}, u32[]{:S(2)}, u32[]{:S(2)}) %collective-permute-start.11) | collective-permute-done | bytes 262176 | tf_op jit(solution)/shard_map/ppermute | solution.py:418
  89.8 2.0 %collective-permute-done.12.refs_2_ = f32[64,8,128]{2,1,0:T(8,128)S(1)} collective-permute-done((f32[64,8,128]{2,1,0:T(8,128)S(1)}, f32[64,8,128]{2,1,0:T(8,128)S(1)}, u32[]{:S(2)}, u32[]{:S(2)}) %collective-permute-start.12) | collective-permute-done | bytes 262176 | tf_op jit(solution)/shard_map/ppermute | solution.py:423
  91.8 4.3 %collective-permute-done.22.refs_8_ = f32[64,8,128]{2,1,0:T(8,128)S(1)} collective-permute-done((f32[64,8,128]{2,1,0:T(8,128)S(1)}, f32[64,8,128]{2,1,0:T(8,128)S(1)}, u32[]{:S(2)}, u32[]{:S(2)}) %collective-permute-start.22) | collective-permute-done | bytes 262176 | tf_op jit(solution)/shard_map/ppermute | solution.py:423
  96.1 2.8 %collective-permute-done.14.refs_3_ = f32[64,8,128]{2,1,0:T(8,128)S(1)} collective-permute-done((f32[64,8,128]{2,1,0:T(8,128)S(1)}, f32[64,8,128]{2,1,0:T(8,128)S(1)}, u32[]{:S(2)}, u32[]{:S(2)}) %collective-permute-start.14) | collective-permute-done | bytes 262176 | tf_op jit(solution)/shard_map/ppermute | solution.py:423
  99.1 1.9 %collective-permute-start.24 = (f32[16,8,128]{2,1,0:T(8,128)S(1)}, f32[16,8,128]{2,1,0:T(8,128)S(1)}, u32[]{:S(2)}, u32[]{:S(2)}) collective-permute-start(f32[16,8,128]{2,1,0:T(8,128)S(1)} %get-tuple-element.107), channel_id=1, source_target_pairs={{0,4},{4,8},{8,12},{12,16},{16,20},{20,24},{24,28},{28,0},{1,5},{5... | collective-permute-start | bytes 196616 | tf_op jit(solution)/shard_map/ppermute | solution.py:404
  101.0 2.9 %collective-permute-start.25 = (f32[16,8,128]{2,1,0:T(8,128)S(1)}, f32[16,8,128]{2,1,0:T(8,128)S(1)}, u32[]{:S(2)}, u32[]{:S(2)}) collective-permute-start(f32[16,8,128]{2,1,0:T(8,128)S(1)} %get-tuple-element.108), channel_id=1, source_target_pairs={{0,28},{4,0},{8,4},{12,8},{16,12},{20,16},{24,20},{28,24},{1,29},{... | collective-permute-start | bytes 196616 | tf_op jit(solution)/shard_map/ppermute | solution.py:404
  103.9 1.7 collective-permute-start.27
  105.6 6.6 %collective-permute-done.28.refs_5_ = f32[1,8,128]{2,1,0:T(8,128)S(1)} collective-permute-done((f32[1,8,128]{2,1,0:T(8,128)S(1)}, f32[1,8,128]{2,1,0:T(8,128)S(1)}, u32[]{:S(2)}, u32[]{:S(2)}) %collective-permute-start.28) | collective-permute-done | bytes 4128 | tf_op jit(solution)/shard_map/ppermute | solution.py:414
  112.2 5.7 %collective-permute-done.29.refs_6_ = f32[1,8,128]{2,1,0:T(8,128)S(1)} collective-permute-done((f32[1,8,128]{2,1,0:T(8,128)S(1)}, f32[1,8,128]{2,1,0:T(8,128)S(1)}, u32[]{:S(2)}, u32[]{:S(2)}) %collective-permute-start.29) | collective-permute-done | bytes 4128 | tf_op jit(solution)/shard_map/ppermute | solution.py:414
  118.0 3.9 %collective-permute-done.30.refs_7_ = f32[1,8,128]{2,1,0:T(8,128)S(1)} collective-permute-done((f32[1,8,128]{2,1,0:T(8,128)S(1)}, f32[1,8,128]{2,1,0:T(8,128)S(1)}, u32[]{:S(2)}, u32[]{:S(2)}) %collective-permute-start.30) | collective-permute-done | bytes 4128 | tf_op jit(solution)/shard_map/ppermute | solution.py:414
  121.9 2.4 %collective-permute-start.31 = (f32[1,8,128]{2,1,0:T(8,128)S(1)}, f32[1,8,128]{2,1,0:T(8,128)S(1)}, u32[]{:S(2)}, u32[]{:S(2)}) collective-permute-start(f32[1,8,128]{2,1,0:T(8,128)S(1)} %get-tuple-element.114), channel_id=1, source_target_pairs={{0,31},{1,28},{2,29},{3,30},{4,3},{5,0},{6,1},{7,2},{8,7},{9,4},{1... | collective-permute-start | bytes 12296 | tf_op jit(solution)/shard_map/ppermute | solution.py:414
  125.7 6.2 %diffuse_spread_a0.1 = (f32[80,8,128]{2,1,0:T(8,128)S(1)}, f32[81,8,128]{2,1,0:T(8,128)S(1)}, f32[81,8,128]{2,1,0:T(8,128)S(1)}, f32[12,8,128]{2,1,0:T(8,128)S(1)}, f32[176,8,128]{2,1,0:T(8,128)S(1)}) custom-call(f32[128,8,128]{2,1,0:T(8,128)S(1)} %get-tuple-element.106.refs_0_, f32[16,8,128]{2,1,0:T(8,128)S(1)} %collective-permute-done.24.refs_1_, ...), custom_call_target="tpu_custom_call" | custom-call | flops 20000000 | bytes 13320208 | tf_op jit(solution)/shard_map/diffuse_spread_a0/pallas_call | solution.py:20
  131.9 1.7 collective-permute-start.33
  133.7 2.7 %spread_b0.1 = (f32[72,8,128]{2,1,0:T(8,128)S(1)}, f32[73,8,128]{2,1,0:T(8,128)S(1)}, f32[73,8,128]{2,1,0:T(8,128)S(1)}, f32[11,8,128]{2,1,0:T(8,128)S(1)}) custom-call(f32[176,8,128]{2,1,0:T(8,128)S(1)} %get-tuple-element.125.g, f32[12,16,64,128]{3,2,1,0:T(8,128)S(1)} %weights0.1.refs_15_.w, s32[1,1,2]{2,1,0:T(1,128)S(1)} %copy-done.15, ...), custom_call_target="tpu_custom_call" | custom-call | flops 10000000 | bytes 7950352 | tf_op jit(solution)/shard_map/spread_b0/pallas_call | solution.py:20
  136.4 1.7 collective-permute-start.41
  139.0 10.4 %collective-permute-done.42.refs_3_.refs_4_ = f32[11,8,128]{2,1,0:T(8,128)S(1)} collective-permute-done((f32[11,8,128]{2,1,0:T(8,128)S(1)}, f32[11,8,128]{2,1,0:T(8,128)S(1)}, u32[]{:S(2)}, u32[]{:S(2)}) %collective-permute-start.42) | collective-permute-done | bytes 45088 | tf_op jit(solution)/shard_map/ppermute | solution.py:404
  150.2 1.1 gather1_0.1
  151.4 2.1 %collective-permute-done.34.refs_3_.refs_4_ = f32[12,8,128]{2,1,0:T(8,128)S(1)} collective-permute-done((f32[12,8,128]{2,1,0:T(8,128)S(1)}, f32[12,8,128]{2,1,0:T(8,128)S(1)}, u32[]{:S(2)}, u32[]{:S(2)}) %collective-permute-start.34) | collective-permute-done | bytes 49184 | tf_op jit(solution)/shard_map/ppermute | solution.py:404
  153.5 1.2 gather0_0.1
  154.7 2.0 %collective-permute-start.43 = (f32[64,8,128]{2,1,0:T(8,128)S(1)}, f32[64,8,128]{2,1,0:T(8,128)S(1)}, u32[]{:S(2)}, u32[]{:S(2)}) collective-permute-start(f32[64,8,128]{2,1,0:T(8,128)S(1)} %get-tuple-element.131), channel_id=1, source_target_pairs={{0,4},{4,0},{8,12},{12,8},{16,20},{20,16},{24,28},{28,24},{1,5},{5... | collective-permute-start | bytes 786440 | tf_op jit(solution)/shard_map/ppermute | solution.py:418
  156.7 3.8 %collective-permute-start.47 = (f32[8,8,128]{2,1,0:T(8,128)S(1)}, f32[8,8,128]{2,1,0:T(8,128)S(1)}, u32[]{:S(2)}, u32[]{:S(2)}) collective-permute-start(f32[8,8,128]{2,1,0:T(8,128)S(1)} %get-tuple-element.135), channel_id=1, source_target_pairs={{0,20},{4,24},{8,28},{12,0},{16,4},{20,8},{24,12},{28,16},{1,21},{... | collective-permute-start | bytes 98312 | tf_op jit(solution)/shard_map/ppermute | solution.py:404
  161.6 2.7 %collective-permute-start.44 = (f32[64,8,128]{2,1,0:T(8,128)S(1)}, f32[64,8,128]{2,1,0:T(8,128)S(1)}, u32[]{:S(2)}, u32[]{:S(2)}) collective-permute-start(f32[64,8,128]{2,1,0:T(8,128)S(1)} %get-tuple-element.132), channel_id=1, source_target_pairs={{0,24},{4,12},{8,0},{12,20},{16,8},{20,28},{24,16},{28,4},{1,25},{... | collective-permute-start | bytes 786440 | tf_op jit(solution)/shard_map/ppermute | solution.py:423
  164.3 4.0 %collective-permute-done.37 = f32[64,8,128]{2,1,0:T(8,128)S(1)} collective-permute-done((f32[64,8,128]{2,1,0:T(8,128)S(1)}, f32[64,8,128]{2,1,0:T(8,128)S(1)}, u32[]{:S(2)}, u32[]{:S(2)}) %collective-permute-start.37) | collective-permute-done | bytes 262176 | tf_op jit(solution)/shard_map/ppermute | solution.py:418
  168.3 4.7 %collective-permute-start.36 = (f32[64,8,128]{2,1,0:T(8,128)S(1)}, f32[64,8,128]{2,1,0:T(8,128)S(1)}, u32[]{:S(2)}, u32[]{:S(2)}) collective-permute-start(f32[64,8,128]{2,1,0:T(8,128)S(1)} %get-tuple-element.121), channel_id=1, source_target_pairs={{0,24},{4,12},{8,0},{12,20},{16,8},{20,28},{24,16},{28,4},{1,25},{... | collective-permute-start | bytes 786440 | tf_op jit(solution)/shard_map/ppermute | solution.py:423
  173.9 3.1 %collective-permute-done.35.refs_1_ = f32[64,8,128]{2,1,0:T(8,128)S(1)} collective-permute-done((f32[64,8,128]{2,1,0:T(8,128)S(1)}, f32[64,8,128]{2,1,0:T(8,128)S(1)}, u32[]{:S(2)}, u32[]{:S(2)}) %collective-permute-start.35) | collective-permute-done | bytes 262176 | tf_op jit(solution)/shard_map/ppermute | solution.py:418
  177.0 8.6 %collective-permute-done.36.refs_2_ = f32[64,8,128]{2,1,0:T(8,128)S(1)} collective-permute-done((f32[64,8,128]{2,1,0:T(8,128)S(1)}, f32[64,8,128]{2,1,0:T(8,128)S(1)}, u32[]{:S(2)}, u32[]{:S(2)}) %collective-permute-start.36) | collective-permute-done | bytes 262176 | tf_op jit(solution)/shard_map/ppermute | solution.py:423
  185.6 1.1 finish.1
  (102 shorter events, 17.4 us)
Async XLA Ops:
  4.8 28.7 %collective-permute-start = (f32[16,8,128]{2,1,0:T(8,128)S(1)}, f32[16,8,128]{2,1,0:T(8,128)S(1)}, u32[]{:S(2)}, u32[]{:S(2)}) collective-permute-start(f32[16,8,128]{2,1,0:T(8,128)S(1)} %get-tuple-element.70), channel_id=1, source_target_pairs={{0,4},{4,8},{8,12},{12,16},{16,20},{20,24},{24,28},{28,0},{1,5},{5... | collective-permute-start | bytes 196616 | tf_op jit(solution)/shard_map/ppermute | solution.py:404
  7.9 25.6 %collective-permute-start.1 = (f32[16,8,128]{2,1,0:T(8,128)S(1)}, f32[16,8,128]{2,1,0:T(8,128)S(1)}, u32[]{:S(2)}, u32[]{:S(2)}) collective-permute-start(f32[16,8,128]{2,1,0:T(8,128)S(1)} %get-tuple-element.71), channel_id=1, source_target_pairs={{0,28},{4,0},{8,4},{12,8},{16,12},{20,16},{24,20},{28,24},{1,29},{... | collective-permute-start | bytes 196616 | tf_op jit(solution)/shard_map/ppermute | solution.py:404
  11.0 22.6 %collective-permute-start.2 = (f32[16,8,128]{2,1,0:T(8,128)S(1)}, f32[16,8,128]{2,1,0:T(8,128)S(1)}, u32[]{:S(2)}, u32[]{:S(2)}) collective-permute-start(f32[16,8,128]{2,1,0:T(8,128)S(1)} %get-tuple-element.72), channel_id=1, source_target_pairs={{0,1},{1,2},{2,3},{3,0},{4,5},{5,6},{6,7},{7,4},{8,9},{9,10},{10,1... | collective-permute-start | bytes 196616 | tf_op jit(solution)/shard_map/ppermute | solution.py:404
  11.0 22.6 %collective-permute-start.3 = (f32[16,8,128]{2,1,0:T(8,128)S(1)}, f32[16,8,128]{2,1,0:T(8,128)S(1)}, u32[]{:S(2)}, u32[]{:S(2)}) collective-permute-start(f32[16,8,128]{2,1,0:T(8,128)S(1)} %get-tuple-element.73), channel_id=1, source_target_pairs={{0,3},{1,0},{2,1},{3,2},{4,7},{5,4},{6,5},{7,6},{8,11},{9,8},{10,9... | collective-permute-start | bytes 196616 | tf_op jit(solution)/shard_map/ppermute | solution.py:404
  12.7 6.6 %collective-permute-start.4 = (f32[1,8,128]{2,1,0:T(8,128)S(1)}, f32[1,8,128]{2,1,0:T(8,128)S(1)}, u32[]{:S(2)}, u32[]{:S(2)}) collective-permute-start(f32[1,8,128]{2,1,0:T(8,128)S(1)} %get-tuple-element.74), channel_id=1, source_target_pairs={{0,5},{1,6},{2,7},{3,4},{4,9},{5,10},{6,11},{7,8},{8,13},{9,14},{1... | collective-permute-start | bytes 12296 | tf_op jit(solution)/shard_map/ppermute | solution.py:414
  19.3 5.7 %collective-permute-start.5 = (f32[1,8,128]{2,1,0:T(8,128)S(1)}, f32[1,8,128]{2,1,0:T(8,128)S(1)}, u32[]{:S(2)}, u32[]{:S(2)}) collective-permute-start(f32[1,8,128]{2,1,0:T(8,128)S(1)} %get-tuple-element.75), channel_id=1, source_target_pairs={{0,7},{1,4},{2,5},{3,6},{4,11},{5,8},{6,9},{7,10},{8,15},{9,12},{1... | collective-permute-start | bytes 12296 | tf_op jit(solution)/shard_map/ppermute | solution.py:414
  25.1 3.9 %collective-permute-start.6 = (f32[1,8,128]{2,1,0:T(8,128)S(1)}, f32[1,8,128]{2,1,0:T(8,128)S(1)}, u32[]{:S(2)}, u32[]{:S(2)}) collective-permute-start(f32[1,8,128]{2,1,0:T(8,128)S(1)} %get-tuple-element.76), channel_id=1, source_target_pairs={{0,29},{1,30},{2,31},{3,28},{4,1},{5,2},{6,3},{7,0},{8,5},{9,6},{1... | collective-permute-start | bytes 12296 | tf_op jit(solution)/shard_map/ppermute | solution.py:414
  29.0 4.5 %collective-permute-start.7 = (f32[1,8,128]{2,1,0:T(8,128)S(1)}, f32[1,8,128]{2,1,0:T(8,128)S(1)}, u32[]{:S(2)}, u32[]{:S(2)}) collective-permute-start(f32[1,8,128]{2,1,0:T(8,128)S(1)} %get-tuple-element.77), channel_id=1, source_target_pairs={{0,31},{1,28},{2,29},{3,30},{4,3},{5,0},{6,1},{7,2},{8,7},{9,4},{1... | collective-permute-start | bytes 12296 | tf_op jit(solution)/shard_map/ppermute | solution.py:414
  42.7 21.8 %collective-permute-start.8 = (f32[81,8,128]{2,1,0:T(8,128)}, f32[81,8,128]{2,1,0:T(8,128)S(1)}, u32[]{:S(2)}, u32[]{:S(2)}) collective-permute-start(f32[81,8,128]{2,1,0:T(8,128)} %get-tuple-element.86), channel_id=1, source_target_pairs={{0,1},{1,2},{2,3},{3,0},{4,5},{5,6},{6,7},{7,4},{8,9},{9,10},{10,1... | collective-permute-start | bytes 995336 | tf_op jit(solution)/shard_map/ppermute | solution.py:404
  42.7 21.8 %collective-permute-start.9 = (f32[81,8,128]{2,1,0:T(8,128)}, f32[81,8,128]{2,1,0:T(8,128)}, u32[]{:S(2)}, u32[]{:S(2)}) collective-permute-start(f32[81,8,128]{2,1,0:T(8,128)} %get-tuple-element.87), channel_id=1, source_target_pairs={{0,3},{1,0},{2,1},{3,2},{4,7},{5,4},{6,5},{7,6},{8,11},{9,8},{10,9... | collective-permute-start | bytes 995336 | tf_op jit(solution)/shard_map/ppermute | solution.py:404
  48.7 12.1 %collective-permute-start.16 = (f32[73,8,128]{2,1,0:T(8,128)}, f32[73,8,128]{2,1,0:T(8,128)}, u32[]{:S(2)}, u32[]{:S(2)}) collective-permute-start(f32[73,8,128]{2,1,0:T(8,128)} %get-tuple-element.97), channel_id=1, source_target_pairs={{0,1},{1,2},{2,3},{3,0},{4,5},{5,6},{6,7},{7,4},{8,9},{9,10},{10,1... | collective-permute-start | bytes 897032 | tf_op jit(solution)/shard_map/ppermute | solution.py:404
  48.7 12.1 %collective-permute-start.17 = (f32[73,8,128]{2,1,0:T(8,128)}, f32[73,8,128]{2,1,0:T(8,128)}, u32[]{:S(2)}, u32[]{:S(2)}) collective-permute-start(f32[73,8,128]{2,1,0:T(8,128)} %get-tuple-element.98), channel_id=1, source_target_pairs={{0,3},{1,0},{2,1},{3,2},{4,7},{5,4},{6,5},{7,6},{8,11},{9,8},{10,9... | collective-permute-start | bytes 897032 | tf_op jit(solution)/shard_map/ppermute | solution.py:404
  50.4 9.9 %collective-permute-start.18 = (f32[11,8,128]{2,1,0:T(8,128)S(1)}, f32[11,8,128]{2,1,0:T(8,128)S(1)}, u32[]{:S(2)}, u32[]{:S(2)}) collective-permute-start(f32[11,8,128]{2,1,0:T(8,128)S(1)} %get-tuple-element.99), channel_id=1, source_target_pairs={{0,2},{1,3},{2,0},{3,1},{4,6},{5,7},{6,4},{7,5},{8,10},{9,11},{10,... | collective-permute-start | bytes 135176 | tf_op jit(solution)/shard_map/ppermute | solution.py:404
  60.4 4.1 %collective-permute-start.10 = (f32[12,8,128]{2,1,0:T(8,128)S(1)}, f32[12,8,128]{2,1,0:T(8,128)S(1)}, u32[]{:S(2)}, u32[]{:S(2)}) collective-permute-start(f32[12,8,128]{2,1,0:T(8,128)S(1)} %get-tuple-element.88), channel_id=1, source_target_pairs={{0,2},{1,3},{2,0},{3,1},{4,6},{5,7},{6,4},{7,5},{8,10},{9,11},{10,... | collective-permute-start | bytes 147464 | tf_op jit(solution)/shard_map/ppermute | solution.py:404
  63.6 10.3 %collective-permute-start.21 = (f32[64,8,128]{2,1,0:T(8,128)S(1)}, f32[64,8,128]{2,1,0:T(8,128)S(1)}, u32[]{:S(2)}, u32[]{:S(2)}) collective-permute-start(f32[64,8,128]{2,1,0:T(8,128)S(1)} %get-tuple-element.104), channel_id=1, source_target_pairs={{0,4},{4,0},{8,12},{12,8},{16,20},{20,16},{24,28},{28,24},{1,5},{5... | collective-permute-start | bytes 786440 | tf_op jit(solution)/shard_map/ppermute | solution.py:418
  67.0 13.5 %collective-permute-start.13 = (f32[64,8,128]{2,1,0:T(8,128)S(1)}, f32[64,8,128]{2,1,0:T(8,128)S(1)}, u32[]{:S(2)}, u32[]{:S(2)}) collective-permute-start(f32[64,8,128]{2,1,0:T(8,128)S(1)} %get-tuple-element.93), channel_id=1, source_target_pairs={{0,4},{4,0},{8,12},{12,8},{16,20},{20,16},{24,28},{28,24},{1,5},{5... | collective-permute-start | bytes 786440 | tf_op jit(solution)/shard_map/ppermute | solution.py:418
  68.3 17.8 %collective-permute-start.19 = (f32[64,8,128]{2,1,0:T(8,128)S(1)}, f32[64,8,128]{2,1,0:T(8,128)S(1)}, u32[]{:S(2)}, u32[]{:S(2)}) collective-permute-start(f32[64,8,128]{2,1,0:T(8,128)S(1)} %get-tuple-element.101), channel_id=1, source_target_pairs={{0,4},{4,0},{8,12},{12,8},{16,20},{20,16},{24,28},{28,24},{1,5},{5... | collective-permute-start | bytes 786440 | tf_op jit(solution)/shard_map/ppermute | solution.py:418
  69.1 16.0 %collective-permute-start.15 = (f32[16,8,128]{2,1,0:T(8,128)S(1)}, f32[16,8,128]{2,1,0:T(8,128)S(1)}, u32[]{:S(2)}, u32[]{:S(2)}) collective-permute-start(f32[16,8,128]{2,1,0:T(8,128)S(1)} %get-tuple-element.94), channel_id=1, source_target_pairs={{0,12},{4,16},{8,20},{12,24},{16,28},{20,0},{24,4},{28,8},{1,13},{... | collective-permute-start | bytes 196616 | tf_op jit(solution)/shard_map/ppermute | solution.py:404
  69.1 11.4 %collective-permute-start.23 = (f32[8,8,128]{2,1,0:T(8,128)S(1)}, f32[8,8,128]{2,1,0:T(8,128)S(1)}, u32[]{:S(2)}, u32[]{:S(2)}) collective-permute-start(f32[8,8,128]{2,1,0:T(8,128)S(1)} %get-tuple-element.105), channel_id=1, source_target_pairs={{0,20},{4,24},{8,28},{12,0},{16,4},{20,8},{24,12},{28,16},{1,21},{... | collective-permute-start | bytes 98312 | tf_op jit(solution)/shard_map/ppermute | solution.py:404
  73.9 12.3 %collective-permute-start.20 = (f32[64,8,128]{2,1,0:T(8,128)S(1)}, f32[64,8,128]{2,1,0:T(8,128)S(1)}, u32[]{:S(2)}, u32[]{:S(2)}) collective-permute-start(f32[64,8,128]{2,1,0:T(8,128)S(1)} %get-tuple-element.102), channel_id=1, source_target_pairs={{0,24},{4,12},{8,0},{12,20},{16,8},{20,28},{24,16},{28,4},{1,25},{... | collective-permute-start | bytes 786440 | tf_op jit(solution)/shard_map/ppermute | solution.py:423
  80.5 9.3 %collective-permute-start.11 = (f32[64,8,128]{2,1,0:T(8,128)S(1)}, f32[64,8,128]{2,1,0:T(8,128)S(1)}, u32[]{:S(2)}, u32[]{:S(2)}) collective-permute-start(f32[64,8,128]{2,1,0:T(8,128)S(1)} %get-tuple-element.90), channel_id=1, source_target_pairs={{0,4},{4,0},{8,12},{12,8},{16,20},{20,16},{24,28},{28,24},{1,5},{5... | collective-permute-start | bytes 786440 | tf_op jit(solution)/shard_map/ppermute | solution.py:418
  80.6 11.2 %collective-permute-start.12 = (f32[64,8,128]{2,1,0:T(8,128)S(1)}, f32[64,8,128]{2,1,0:T(8,128)S(1)}, u32[]{:S(2)}, u32[]{:S(2)}) collective-permute-start(f32[64,8,128]{2,1,0:T(8,128)S(1)} %get-tuple-element.91), channel_id=1, source_target_pairs={{0,24},{4,12},{8,0},{12,20},{16,8},{20,28},{24,16},{28,4},{1,25},{... | collective-permute-start | bytes 786440 | tf_op jit(solution)/shard_map/ppermute | solution.py:423
  85.1 11.0 %collective-permute-start.22 = (f32[64,8,128]{2,1,0:T(8,128)S(1)}, f32[64,8,128]{2,1,0:T(8,128)S(1)}, u32[]{:S(2)}, u32[]{:S(2)}) collective-permute-start(f32[64,8,128]{2,1,0:T(8,128)S(1)} %add.19), channel_id=1, source_target_pairs={{0,8},{4,28},{8,16},{12,4},{16,24},{20,12},{24,0},{28,20},{1,9},{5... | collective-permute-start | bytes 786440 | tf_op jit(solution)/shard_map/ppermute | solution.py:423
  86.1 12.7 %collective-permute-start.14 = (f32[64,8,128]{2,1,0:T(8,128)S(1)}, f32[64,8,128]{2,1,0:T(8,128)S(1)}, u32[]{:S(2)}, u32[]{:S(2)}) collective-permute-start(f32[64,8,128]{2,1,0:T(8,128)S(1)} %add.18), channel_id=1, source_target_pairs={{0,8},{4,28},{8,16},{12,4},{16,24},{20,12},{24,0},{28,20},{1,9},{5... | collective-permute-start | bytes 786440 | tf_op jit(solution)/shard_map/ppermute | solution.py:423
  99.1 26.6 %collective-permute-start.24 = (f32[16,8,128]{2,1,0:T(8,128)S(1)}, f32[16,8,128]{2,1,0:T(8,128)S(1)}, u32[]{:S(2)}, u32[]{:S(2)}) collective-permute-start(f32[16,8,128]{2,1,0:T(8,128)S(1)} %get-tuple-element.107), channel_id=1, source_target_pairs={{0,4},{4,8},{8,12},{12,16},{16,20},{20,24},{24,28},{28,0},{1,5},{5... | collective-permute-start | bytes 196616 | tf_op jit(solution)/shard_map/ppermute | solution.py:404
  101.0 24.7 %collective-permute-start.25 = (f32[16,8,128]{2,1,0:T(8,128)S(1)}, f32[16,8,128]{2,1,0:T(8,128)S(1)}, u32[]{:S(2)}, u32[]{:S(2)}) collective-permute-start(f32[16,8,128]{2,1,0:T(8,128)S(1)} %get-tuple-element.108), channel_id=1, source_target_pairs={{0,28},{4,0},{8,4},{12,8},{16,12},{20,16},{24,20},{28,24},{1,29},{... | collective-permute-start | bytes 196616 | tf_op jit(solution)/shard_map/ppermute | solution.py:404
  103.9 21.8 %collective-permute-start.26 = (f32[16,8,128]{2,1,0:T(8,128)S(1)}, f32[16,8,128]{2,1,0:T(8,128)S(1)}, u32[]{:S(2)}, u32[]{:S(2)}) collective-permute-start(f32[16,8,128]{2,1,0:T(8,128)S(1)} %get-tuple-element.109), channel_id=1, source_target_pairs={{0,1},{1,2},{2,3},{3,0},{4,5},{5,6},{6,7},{7,4},{8,9},{9,10},{10,1... | collective-permute-start | bytes 196616 | tf_op jit(solution)/shard_map/ppermute | solution.py:404
  103.9 21.8 %collective-permute-start.27 = (f32[16,8,128]{2,1,0:T(8,128)S(1)}, f32[16,8,128]{2,1,0:T(8,128)S(1)}, u32[]{:S(2)}, u32[]{:S(2)}) collective-permute-start(f32[16,8,128]{2,1,0:T(8,128)S(1)} %get-tuple-element.110), channel_id=1, source_target_pairs={{0,3},{1,0},{2,1},{3,2},{4,7},{5,4},{6,5},{7,6},{8,11},{9,8},{10,9... | collective-permute-start | bytes 196616 | tf_op jit(solution)/shard_map/ppermute | solution.py:404
  105.6 6.6 %collective-permute-start.28 = (f32[1,8,128]{2,1,0:T(8,128)S(1)}, f32[1,8,128]{2,1,0:T(8,128)S(1)}, u32[]{:S(2)}, u32[]{:S(2)}) collective-permute-start(f32[1,8,128]{2,1,0:T(8,128)S(1)} %get-tuple-element.111), channel_id=1, source_target_pairs={{0,5},{1,6},{2,7},{3,4},{4,9},{5,10},{6,11},{7,8},{8,13},{9,14},{1... | collective-permute-start | bytes 12296 | tf_op jit(solution)/shard_map/ppermute | solution.py:414
  112.2 5.7 %collective-permute-start.29 = (f32[1,8,128]{2,1,0:T(8,128)S(1)}, f32[1,8,128]{2,1,0:T(8,128)S(1)}, u32[]{:S(2)}, u32[]{:S(2)}) collective-permute-start(f32[1,8,128]{2,1,0:T(8,128)S(1)} %get-tuple-element.112), channel_id=1, source_target_pairs={{0,7},{1,4},{2,5},{3,6},{4,11},{5,8},{6,9},{7,10},{8,15},{9,12},{1... | collective-permute-start | bytes 12296 | tf_op jit(solution)/shard_map/ppermute | solution.py:414
  118.0 3.9 %collective-permute-start.30 = (f32[1,8,128]{2,1,0:T(8,128)S(1)}, f32[1,8,128]{2,1,0:T(8,128)S(1)}, u32[]{:S(2)}, u32[]{:S(2)}) collective-permute-start(f32[1,8,128]{2,1,0:T(8,128)S(1)} %get-tuple-element.113), channel_id=1, source_target_pairs={{0,29},{1,30},{2,31},{3,28},{4,1},{5,2},{6,3},{7,0},{8,5},{9,6},{1... | collective-permute-start | bytes 12296 | tf_op jit(solution)/shard_map/ppermute | solution.py:414
  121.9 3.7 %collective-permute-start.31 = (f32[1,8,128]{2,1,0:T(8,128)S(1)}, f32[1,8,128]{2,1,0:T(8,128)S(1)}, u32[]{:S(2)}, u32[]{:S(2)}) collective-permute-start(f32[1,8,128]{2,1,0:T(8,128)S(1)} %get-tuple-element.114), channel_id=1, source_target_pairs={{0,31},{1,28},{2,29},{3,30},{4,3},{5,0},{6,1},{7,2},{8,7},{9,4},{1... | collective-permute-start | bytes 12296 | tf_op jit(solution)/shard_map/ppermute | solution.py:414
  131.9 21.6 %collective-permute-start.32 = (f32[81,8,128]{2,1,0:T(8,128)S(1)}, f32[81,8,128]{2,1,0:T(8,128)S(1)}, u32[]{:S(2)}, u32[]{:S(2)}) collective-permute-start(f32[81,8,128]{2,1,0:T(8,128)S(1)} %get-tuple-element.116), channel_id=1, source_target_pairs={{0,1},{1,2},{2,3},{3,0},{4,5},{5,6},{6,7},{7,4},{8,9},{9,10},{10,1... | collective-permute-start | bytes 995336 | tf_op jit(solution)/shard_map/ppermute | solution.py:404
  131.9 21.6 %collective-permute-start.33 = (f32[81,8,128]{2,1,0:T(8,128)S(1)}, f32[81,8,128]{2,1,0:T(8,128)S(1)}, u32[]{:S(2)}, u32[]{:S(2)}) collective-permute-start(f32[81,8,128]{2,1,0:T(8,128)S(1)} %get-tuple-element.117), channel_id=1, source_target_pairs={{0,3},{1,0},{2,1},{3,2},{4,7},{5,4},{6,5},{7,6},{8,11},{9,8},{10,9... | collective-permute-start | bytes 995336 | tf_op jit(solution)/shard_map/ppermute | solution.py:404
  136.3 13.9 %collective-permute-start.40 = (f32[73,8,128]{2,1,0:T(8,128)S(1)}, f32[73,8,128]{2,1,0:T(8,128)S(1)}, u32[]{:S(2)}, u32[]{:S(2)}) collective-permute-start(f32[73,8,128]{2,1,0:T(8,128)S(1)} %get-tuple-element.127), channel_id=1, source_target_pairs={{0,1},{1,2},{2,3},{3,0},{4,5},{5,6},{6,7},{7,4},{8,9},{9,10},{10,1... | collective-permute-start | bytes 897032 | tf_op jit(solution)/shard_map/ppermute | solution.py:404
  136.4 13.8 %collective-permute-start.41 = (f32[73,8,128]{2,1,0:T(8,128)S(1)}, f32[73,8,128]{2,1,0:T(8,128)S(1)}, u32[]{:S(2)}, u32[]{:S(2)}) collective-permute-start(f32[73,8,128]{2,1,0:T(8,128)S(1)} %get-tuple-element.128), channel_id=1, source_target_pairs={{0,3},{1,0},{2,1},{3,2},{4,7},{5,4},{6,5},{7,6},{8,11},{9,8},{10,9... | collective-permute-start | bytes 897032 | tf_op jit(solution)/shard_map/ppermute | solution.py:404
  138.1 11.2 %collective-permute-start.42 = (f32[11,8,128]{2,1,0:T(8,128)S(1)}, f32[11,8,128]{2,1,0:T(8,128)S(1)}, u32[]{:S(2)}, u32[]{:S(2)}) collective-permute-start(f32[11,8,128]{2,1,0:T(8,128)S(1)} %get-tuple-element.129), channel_id=1, source_target_pairs={{0,2},{1,3},{2,0},{3,1},{4,6},{5,7},{6,4},{7,5},{8,10},{9,11},{10,... | collective-permute-start | bytes 135176 | tf_op jit(solution)/shard_map/ppermute | solution.py:404
  149.4 4.1 %collective-permute-start.34 = (f32[12,8,128]{2,1,0:T(8,128)S(1)}, f32[12,8,128]{2,1,0:T(8,128)S(1)}, u32[]{:S(2)}, u32[]{:S(2)}) collective-permute-start(f32[12,8,128]{2,1,0:T(8,128)S(1)} %get-tuple-element.118), channel_id=1, source_target_pairs={{0,2},{1,3},{2,0},{3,1},{4,6},{5,7},{6,4},{7,5},{8,10},{9,11},{10,... | collective-permute-start | bytes 147464 | tf_op jit(solution)/shard_map/ppermute | solution.py:404
  151.3 10.3 %collective-permute-start.45 = (f32[64,8,128]{2,1,0:T(8,128)S(1)}, f32[64,8,128]{2,1,0:T(8,128)S(1)}, u32[]{:S(2)}, u32[]{:S(2)}) collective-permute-start(f32[64,8,128]{2,1,0:T(8,128)S(1)} %get-tuple-element.134), channel_id=1, source_target_pairs={{0,4},{4,0},{8,12},{12,8},{16,20},{20,16},{24,28},{28,24},{1,5},{5... | collective-permute-start | bytes 786440 | tf_op jit(solution)/shard_map/ppermute | solution.py:418
  154.6 13.6 %collective-permute-start.37 = (f32[64,8,128]{2,1,0:T(8,128)S(1)}, f32[64,8,128]{2,1,0:T(8,128)S(1)}, u32[]{:S(2)}, u32[]{:S(2)}) collective-permute-start(f32[64,8,128]{2,1,0:T(8,128)S(1)} %get-tuple-element.123), channel_id=1, source_target_pairs={{0,4},{4,0},{8,12},{12,8},{16,20},{20,16},{24,28},{28,24},{1,5},{5... | collective-permute-start | bytes 786440 | tf_op jit(solution)/shard_map/ppermute | solution.py:418
  154.7 19.2 %collective-permute-start.43 = (f32[64,8,128]{2,1,0:T(8,128)S(1)}, f32[64,8,128]{2,1,0:T(8,128)S(1)}, u32[]{:S(2)}, u32[]{:S(2)}) collective-permute-start(f32[64,8,128]{2,1,0:T(8,128)S(1)} %get-tuple-element.131), channel_id=1, source_target_pairs={{0,4},{4,0},{8,12},{12,8},{16,20},{20,16},{24,28},{28,24},{1,5},{5... | collective-permute-start | bytes 786440 | tf_op jit(solution)/shard_map/ppermute | solution.py:418
  156.7 16.3 %collective-permute-start.39 = (f32[16,8,128]{2,1,0:T(8,128)S(1)}, f32[16,8,128]{2,1,0:T(8,128)S(1)}, u32[]{:S(2)}, u32[]{:S(2)}) collective-permute-start(f32[16,8,128]{2,1,0:T(8,128)S(1)} %get-tuple-element.124), channel_id=1, source_target_pairs={{0,12},{4,16},{8,20},{12,24},{16,28},{20,0},{24,4},{28,8},{1,13},{... | collective-permute-start | bytes 196616 | tf_op jit(solution)/shard_map/ppermute | solution.py:404
  156.7 11.6 %collective-permute-start.47 = (f32[8,8,128]{2,1,0:T(8,128)S(1)}, f32[8,8,128]{2,1,0:T(8,128)S(1)}, u32[]{:S(2)}, u32[]{:S(2)}) collective-permute-start(f32[8,8,128]{2,1,0:T(8,128)S(1)} %get-tuple-element.135), channel_id=1, source_target_pairs={{0,20},{4,24},{8,28},{12,0},{16,4},{20,8},{24,12},{28,16},{1,21},{... | collective-permute-start | bytes 98312 | tf_op jit(solution)/shard_map/ppermute | solution.py:404
  161.6 12.3 %collective-permute-start.44 = (f32[64,8,128]{2,1,0:T(8,128)S(1)}, f32[64,8,128]{2,1,0:T(8,128)S(1)}, u32[]{:S(2)}, u32[]{:S(2)}) collective-permute-start(f32[64,8,128]{2,1,0:T(8,128)S(1)} %get-tuple-element.132), channel_id=1, source_target_pairs={{0,24},{4,12},{8,0},{12,20},{16,8},{20,28},{24,16},{28,4},{1,25},{... | collective-permute-start | bytes 786440 | tf_op jit(solution)/shard_map/ppermute | solution.py:423
  168.3 8.7 %collective-permute-start.35 = (f32[64,8,128]{2,1,0:T(8,128)S(1)}, f32[64,8,128]{2,1,0:T(8,128)S(1)}, u32[]{:S(2)}, u32[]{:S(2)}) collective-permute-start(f32[64,8,128]{2,1,0:T(8,128)S(1)} %get-tuple-element.120), channel_id=1, source_target_pairs={{0,4},{4,0},{8,12},{12,8},{16,20},{20,16},{24,28},{28,24},{1,5},{5... | collective-permute-start | bytes 786440 | tf_op jit(solution)/shard_map/ppermute | solution.py:418
  168.3 17.3 %collective-permute-start.36 = (f32[64,8,128]{2,1,0:T(8,128)S(1)}, f32[64,8,128]{2,1,0:T(8,128)S(1)}, u32[]{:S(2)}, u32[]{:S(2)}) collective-permute-start(f32[64,8,128]{2,1,0:T(8,128)S(1)} %get-tuple-element.121), channel_id=1, source_target_pairs={{0,24},{4,12},{8,0},{12,20},{16,8},{20,28},{24,16},{28,4},{1,25},{... | collective-permute-start | bytes 786440 | tf_op jit(solution)/shard_map/ppermute | solution.py:423
  173.1 12.5 %collective-permute-start.46 = (f32[64,8,128]{2,1,0:T(8,128)S(1)}, f32[64,8,128]{2,1,0:T(8,128)S(1)}, u32[]{:S(2)}, u32[]{:S(2)}) collective-permute-start(f32[64,8,128]{2,1,0:T(8,128)S(1)} %add.21), channel_id=1, source_target_pairs={{0,8},{4,28},{8,16},{12,4},{16,24},{20,12},{24,0},{28,20},{1,9},{5... | collective-permute-start | bytes 786440 | tf_op jit(solution)/shard_map/ppermute | solution.py:423
  173.9 11.7 %collective-permute-start.38 = (f32[64,8,128]{2,1,0:T(8,128)S(1)}, f32[64,8,128]{2,1,0:T(8,128)S(1)}, u32[]{:S(2)}, u32[]{:S(2)}) collective-permute-start(f32[64,8,128]{2,1,0:T(8,128)S(1)} %add.20), channel_id=1, source_target_pairs={{0,8},{4,28},{8,16},{12,4},{16,24},{20,12},{24,0},{28,20},{1,9},{5... | collective-permute-start | bytes 786440 | tf_op jit(solution)/shard_map/ppermute | solution.py:423
  (18 other events, 381.6 us)

commit v2 on v1

--- a/solution.py
+++ b/solution.py
@@ -7,6 +7,7 @@
 from jax.experimental.pallas import tpu as pltpu
 from jax.sharding import PartitionSpec as P
 
+
 STEPS = 2
 BUOYANCY = 0.8
 FIELDS = 4
@@ -15,7 +16,7 @@
 SMEM = pl.BlockSpec(memory_space=pltpu.SMEM)
 
 
-def call(body, outs, args, specs, scratch=(), flops=1000000, name=None):
+def call(body, outs, args, specs, scratch=(), flops=1000000):
     moved = sum(a.size for a in args) * 4 + sum(o.size for o in outs) * 4
     return pl.pallas_call(
         body,
@@ -23,9 +24,8 @@
         in_specs=list(specs),
         out_specs=tuple(VMEM for _ in outs),
         scratch_shapes=list(scratch),
-        compiler_params=pltpu.CompilerParams(vmem_limit_bytes=40 * 1024 * 1024),
+        compiler_params=pltpu.CompilerParams(vmem_limit_bytes=8 * 1024 * 1024),
         cost_estimate=pl.CostEstimate(flops=flops, bytes_accessed=moved, transcendentals=0),
-        name=name,
     )(*args)
 
 
@@ -52,8 +52,15 @@
     )
 
 
-def prep_body(cx, cy, level, vel, labels, rates, state, rate, top, bot, left, right, c00, c01, c10, c11):
+def prep_body(cx, cy, *refs):
+    hbm, (state, rate, left, right), local, sem = refs[:4], refs[4:8], refs[8:12], refs[12]
     pairs = cy // 2
+    copies = [pltpu.make_async_copy(a, b, sem.at[n]) for n, (a, b) in enumerate(zip(hbm, local))]
+    for copy in copies:
+        copy.start()
+    for copy in copies:
+        copy.wait()
+    level, vel, labels, rates = local
 
     def row(x, _):
         state[x, pl.ds(0, cy, stride=FIELDS), :] = level[x]
@@ -71,17 +78,24 @@
         is_level = sublane(state[x, at, :].shape) % FIELDS == 0
         return jnp.where(is_level, rate[x, at, :], state[x, at, :])
 
-    for k in range(2):
-        for q in range(pairs):
-            top[k * pairs + q] = mixed(k, q)
-            bot[k * pairs + q] = mixed(cx - 2 + k, q)
     for x in range(cx):
         left[x] = mixed(x, 0)
         right[x] = mixed(x, pairs - 1)
-    c00[0] = left[0]
-    c01[0] = right[0]
-    c10[0] = left[cx - 1]
-    c11[0] = right[cx - 1]
+
+
+def edge_rows_body(cx, pairs, mix, *refs):
+    sources, (top, bot) = refs[:-2], refs[-2:]
+    state, ym, yp = sources[0], sources[-2], sources[-1]
+    wide = pairs + 2
+    for out, rows in ((top, (0, 1)), (bot, (cx - 2, cx - 1))):
+        for k, x in enumerate(rows):
+            out[k * wide] = ym[x]
+            out[k * wide + pairs + 1] = yp[x]
+            for q in range(pairs):
+                v = state[x * pairs + q]
+                if mix:
+                    v = jnp.where(sublane(v.shape) % FIELDS == 0, sources[1][x * pairs + q], v)
+                out[k * wide + q + 1] = v
 
 
 def weights_body(cx, cy, step, fraction, out):
@@ -95,7 +109,7 @@
     lax.fori_loop(0, cx, row, 0)
 
 
-def fill(pad, cx, pairs, own, xm, xp, ym, yp, c00, c01, c10, c11, change):
+def fill(pad, cx, pairs, own, xm, xp, ym, yp, change):
     wide = pairs + 2
 
     def row(x, _):
@@ -106,17 +120,12 @@
         return 0
 
     lax.fori_loop(0, cx, row, 0)
-    for k in range(2):
-        for q in range(pairs):
-            pad[k * wide + q + 1] = change(xm[k * pairs + q])
-            pad[(cx + 2 + k) * wide + q + 1] = change(xp[k * pairs + q])
-    pad[wide] = change(c00[0])
-    pad[wide + pairs + 1] = change(c01[0])
-    pad[(cx + 2) * wide] = change(c10[0])
-    pad[(cx + 2) * wide + pairs + 1] = change(c11[0])
-
-
-def coef_body(cx, pairs, rate, xm, xp, ym, yp, c00, c01, c10, c11, ax, yu, yd, zu, zd, c0, pad):
+    for k in range(2 * wide):
+        pad[k] = change(xm[k])
+        pad[(cx + 2) * wide + k] = change(xp[k])
+
+
+def coef_body(cx, pairs, rate, xm, xp, ym, yp, ax, yu, yd, zu, zd, c0, pad):
     wide = pairs + 2
     shape = pad.shape[1:]
     field = sublane(shape) % FIELDS
@@ -128,10 +137,7 @@
         v = v + turn(v, 1, 0)
         return v + turn(v, 2, 0)
 
-    for k in (0, cx + 3):
-        pad[k * wide] = jnp.zeros(shape, jnp.float32)
-        pad[k * wide + pairs + 1] = jnp.zeros(shape, jnp.float32)
-    fill(pad, cx, pairs, lambda x, q: rate[x * pairs + q], xm, xp, ym, yp, c00, c01, c10, c11, spread_rate)
+    fill(pad, cx, pairs, lambda x, q: rate[x * pairs + q], xm, xp, ym, yp, spread_rate)
 
     def faces(x, _):
         for j in range(wide):
@@ -210,7 +216,6 @@
     shape = g.shape[1:]
     half = sublane(shape) < FIELDS
     rows = [(at + 1 - a + 3, jnp.clip(at + 1 - a, 0, cx - 1)) for a in range(4)]
-    before = None
     out = []
     zero = jnp.zeros(shape, jnp.float32)
 
@@ -283,8 +288,8 @@
 
 
 def diffuse_spread_body(cx, pairs, step, rows_of, count, *refs):
-    own, halos, coefs, w, sx, sy = refs[0], refs[1:9], refs[9:15], refs[15], refs[16], refs[17]
-    o, r, l, far, g, pad, mid = refs[18:]
+    own, halos, coefs, w, sx, sy = refs[0], refs[1:5], refs[5:11], refs[11], refs[12], refs[13]
+    o, r, l, far, g, pad, mid = refs[14:]
     diffuse(cx, pairs, own, halos, coefs, pad, mid, g)
     spread(cx, pairs, rows_of, count, g, w, sx, sy, step, o, r, l, far)
 
@@ -294,15 +299,15 @@
 
 
 def gather_body(pairs, step, main, rim_at, edge_of, has_high, has_low, *refs):
-    own, right, left, far_low, far_high, sx, parity = refs[:7]
-    e1, e0, f, k, t0, x3 = refs[7:]
+    own, right, left, far_low, far_high, sx = refs[:6]
+    e1, e0, f, k, t0, x3 = refs[6:]
     shape = own.shape[1:]
     count = own.shape[0] // pairs
     mine = jnp.full(shape, sx[0, 0, step].astype(jnp.float32))
     moves = (mine, right[count * pairs], left[count * pairs])
     far_moves = (far_low[count], far_high[count])
     far_gates = (far_low[count + 1] == 1.0, far_high[count + 1] == -1.0)
-    side = parity[0]
+    side = 2 * lax.rem(lax.axis_index("gx"), 2) - 1
     targets = (side, -side, 2 * side, -2 * side, 0)
     outs = (e1, e0, f, k, t0)
 
@@ -342,6 +347,15 @@
             x3[n * pairs + q] = total(masks, fars, source, q)
 
 
+def add_body(a, b, out):
+    def rows(i, _):
+        for j in range(8):
+            out[i * 8 + j] = a[i * 8 + j] + b[i * 8 + j]
+        return 0
+
+    lax.fori_loop(0, out.shape[0] // 8, rows, 0)
+
+
 def merge(cx, pairs, main, parts, state):
     (t0a, e0a, fa, da, xa), (t0b, e0b, fb, db, xb) = parts
     for base, (t0, e0, f, d) in ((0, (t0a, e0a, fa, da)), (main[0], (t0b, e0b, fb, db))):
@@ -361,23 +375,16 @@
 
 def merge_body(cx, pairs, main, *refs):
     parts = (refs[0:5], refs[5:10])
-    out, top, bot, left, right, c00, c01, c10, c11 = refs[10:]
+    out, left, right = refs[10:]
 
     def put(x, q, v, add):
         at = x * pairs + q
         out[at] = out[at] + v if add else v
 
     merge(cx, pairs, main, parts, put)
-    for k in range(2 * pairs):
-        top[k] = out[k]
-        bot[k] = out[(cx - 2) * pairs + k]
     for x in range(cx):
         left[x] = out[x * pairs]
         right[x] = out[x * pairs + pairs - 1]
-    c00[0] = left[0]
-    c01[0] = right[0]
-    c10[0] = left[cx - 1]
-    c11[0] = right[cx - 1]
 
 
 def finish_body(cx, cy, pairs, main, *refs):
@@ -404,16 +411,6 @@
     return lax.ppermute(value, axis, [(i, (i + steps) % count) for i in range(count)])
 
 
-def moved_both(value, step_x, step_y):
-    nx, ny = lax.axis_size("gx"), lax.axis_size("gy")
-    pairs = [
-        (x * ny + y, ((x + step_x) % nx) * ny + (y + step_y) % ny)
-        for x in range(nx)
-        for y in range(ny)
-    ]
-    return lax.ppermute(value, ("gx", "gy"), pairs)
-
-
 def swapped(value):
     return lax.ppermute(value, "gx", [(i, i ^ 1) for i in range(lax.axis_size("gx"))])
 
@@ -425,16 +422,19 @@
     )
 
 
-def exchange(top, bot, left, right, c00, c01, c10, c11):
+def exchange(cx, pairs, states, left, right):
+    ym = moved(right, "gy", 1)
+    yp = moved(left, "gy", -1)
+    shape = f32(2 * (pairs + 2), *left.shape[1:])
+    top, bot = call(
+        functools.partial(edge_rows_body, cx, pairs, len(states) == 2),
+        [shape] * 2,
+        (*states, ym, yp),
+        [VMEM] * (len(states) + 2),
+    )
     xm = moved(bot, "gx", 1)
     xp = moved(top, "gx", -1)
-    ym = moved(right, "gy", 1)
-    yp = moved(left, "gy", -1)
-    mm = moved_both(c11, 1, 1)
-    mp = moved_both(c10, 1, -1)
-    pm = moved_both(c01, -1, 1)
-    pp = moved_both(c00, -1, -1)
-    return xm, xp, ym, yp, mm, mp, pm, pp
+    return xm, xp, ym, yp
 
 
 def on_device(level, vel, fraction, shift_x, shift_y, labels, rates):
@@ -442,7 +442,6 @@
     pairs = cy // 2
     wide = pairs + 2
     ny = lax.axis_size("gy")
-    parity = (2 * (lax.axis_index("gx") % 2) - 1).astype(jnp.int32).reshape(1)
     first = cx // 2
     main = (first, cx - first)
 
@@ -452,26 +451,24 @@
     def scratch(n):
         return pltpu.VMEM((n, SUB, cz), jnp.float32)
 
-    halo_outs = (
-        [plane(2 * pairs)] * 2 + [plane(cx)] * 2 + [plane(1)] * 4
-    )
+    halo_outs = [plane(cx)] * 2
+    local = [pltpu.VMEM(a.shape, a.dtype) for a in (level, vel, labels)]
     state, rate, *edges = call(
         functools.partial(prep_body, cx, cy),
         [f32(cx, FIELDS * cy, cz)] * 2 + halo_outs,
         (level, vel, labels, rates),
-        [VMEM, VMEM, VMEM, SMEM],
-        name="prep",
+        [pl.BlockSpec(memory_space=pltpu.HBM)] * 4,
+        local + [pltpu.SMEM(rates.shape, rates.dtype), pltpu.SemaphoreType.DMA((4,))],
     )
     state = state.reshape(cx * pairs, SUB, cz)
     rate = rate.reshape(cx * pairs, SUB, cz)
-    halos = exchange(*edges)
+    halos = exchange(cx, pairs, (state, rate), *edges)
     weights = [
         call(
             functools.partial(weights_body, cx, cy, s),
             [f32(12, cx, FIELDS * cy, cz)],
             (fraction,),
             [VMEM],
-            name="weights%d" % s,
         )[0]
         for s in range(STEPS)
     ]
@@ -479,9 +476,8 @@
         functools.partial(coef_body, cx, pairs),
         [plane((cx + 3) * wide)] + [plane((cx + 2) * wide)] * 5,
         (rate, *halos),
-        [VMEM] * 9,
+        [VMEM] * 5,
         [scratch((cx + 4) * wide)],
-        name="coefs",
     )
 
     def rows_a(i):
@@ -502,10 +498,9 @@
             functools.partial(diffuse_spread_body, cx, pairs, step, rows_a, counts[0]),
             outs(counts[0]) + [plane((cx + 6) * pairs)],
             (state, *halos, *coefs, weights[step], shift_x, shift_y),
-            [VMEM] * 15 + spec_tail,
+            [VMEM] * 11 + spec_tail,
             [scratch((cx + 4) * wide), scratch((cx + 2) * wide)],
             flops=20000000,
-            name="diffuse_spread_a%d" % step,
         )
         sent_b = call(
             functools.partial(spread_body, cx, pairs, step, rows_b, counts[1]),
@@ -513,9 +508,10 @@
             (g, weights[step], shift_x, shift_y),
             [VMEM] + spec_tail,
             flops=10000000,
-            name="spread_b%d" % step,
         )
         for n, (own, right, left, far) in enumerate((sent_a, sent_b)):
+            if n:
+                own, _ = lax.optimization_barrier((own, chunks[0]))
             right = moved(right, "gy", 1)
             left = moved(left, "gy", -1)
             far_low = moved(far, "gy", 2)
@@ -527,16 +523,16 @@
             e1, e0, f, k, t0, x3 = call(
                 functools.partial(gather_body, pairs, step, main[n], *args),
                 [plane(main[n] * pairs)] * 5 + [plane((2 if n == 0 else 1) * pairs)],
-                (own, right, left, far_low, far_high, shift_x, parity),
-                [VMEM] * 5 + [SMEM] * 2,
+                (own, right, left, far_low, far_high, shift_x),
+                [VMEM] * 5 + [SMEM],
                 flops=3000000,
-                name="gather%d_%d" % (n, step),
             )
             e1 = swapped(e1)
             f = crossed(f, 1)
+            e0 = swapped(e0)
             x3 = moved(x3, "gx", 3 if n == 0 else -3)
-            e0 = swapped(e0)
-            d = crossed(k + e1, -1)
+            (d,) = call(add_body, [plane(main[n] * pairs)], (k, e1), [VMEM] * 2)
+            d = crossed(d, -1)
             chunks += [t0, e0, f, d, x3]
         if step:
             state, *edges = call(
@@ -544,9 +540,8 @@
                 [plane(cx * pairs)] + halo_outs,
                 chunks,
                 [VMEM] * 10,
-                name="merge%d" % step,
             )
-            halos = exchange(*edges)
+            halos = exchange(cx, pairs, (state,), *edges)
         else:
             return call(
                 functools.partial(finish_body, cx, cy, pairs, main),
@@ -554,7 +549,6 @@
                 chunks,
                 [VMEM] * 10,
                 [pltpu.VMEM((cx, FIELDS * cy, cz), jnp.float32)],
-                name="finish",
             )
 
 

time: 187 us -> 164 us (0.88)
  waiting for transfers between devices: 92.2 us -> 71.7 us
  starting transfers between devices: 56 us -> 58.9 us
  local copies, waits for them, and re-layouts: 7.27 us -> 4.59 us
  Pallas kernels: 30 us -> 28 us
    ppermute x8 -> x0, waiting for transfers between devices: 33.4 us -> none  [moved_both(): return lax.ppermute(value, ('gx', 'gy'), pairs)]
    ppermute x24, waiting for transfers between devices: 22.8 us -> 31.6 us  [moved(): lax.ppermute(value, axis, [(i, (i + steps) % count) for i in range(count)])]
    ppermute x8, waiting for transfers between devices: 17.7 us -> 23.1 us  [crossed(): lax.ppermute(value, 'gx', [(i, (i + (2 if i % 2 else -2) * sign) % count)...]
    ppermute x8 -> x0, starting transfers between devices: 5.25 us -> none  [moved_both(): return lax.ppermute(value, ('gx', 'gy'), pairs)]
    ppermute x8, starting transfers between devices: 4.33 us -> 8.58 us  [swapped(): lax.ppermute(value, 'gx', [(i, i ^ 1) for i in range(lax.axis_size('gx'))])]
    ppermute x24, starting transfers between devices: 31.7 us -> 34.5 us  [moved(): lax.ppermute(value, axis, [(i, (i + steps) % count) for i in range(count)])]
    unnamed x36 -> x16, local copies, waits for them, and re-layouts: 7.27 us -> 4.59 us
    pallas_call x14 -> x20, Pallas kernels: 30 us -> 28 us  [call(): pl.pallas_call(body, out_shape=tuple(outs), in_specs=list(specs), out_spe...]
  transfers between devices with their start and end apart: 48 -> 40, of which waited for: 23 -> 22; matrix products, arithmetic and copies ran while one was open for 0% -> 0% of each run, Pallas kernels for 7% -> 5%
where the time goes in v2:
time: 164 us
  waiting for transfers between devices  71.7 us (44%)
  starting transfers between devices  58.9 us (36%)
  Pallas kernels  28 us (17%)
  local copies, waits for them, and re-layouts  4.59 us (3%)
    ppermute x24, starting transfers between devices, moved(): lax.ppermute(value, axis, [(i, (i + steps) % count) for i in range(count)])  34.5 us
    ppermute x24, waiting for transfers between devices, moved(): lax.ppermute(value, axis, [(i, (i + steps) % count) for i in range(count)])  31.6 us
    pallas_call x20, Pallas kernels, call(): pl.pallas_call(body, out_shape=tuple(outs), in_specs=list(specs), out_spe...  28 us
    ppermute x8, waiting for transfers between devices, crossed(): lax.ppermute(value, 'gx', [(i, (i + (2 if i % 2 else -2) * sign) % count)...  23.1 us
    ppermute x8, waiting for transfers between devices, swapped(): lax.ppermute(value, 'gx', [(i, i ^ 1) for i in range(lax.axis_size('gx'))])  17 us
    ppermute x8, starting transfers between devices, crossed(): lax.ppermute(value, 'gx', [(i, (i + (2 if i % 2 else -2) * sign) % count)...  15.9 us
    ppermute x8, starting transfers between devices, swapped(): lax.ppermute(value, 'gx', [(i, i ^ 1) for i in range(lax.axis_size('gx'))])  8.58 us
    unnamed x16, local copies, waits for them, and re-layouts  4.59 us
  transfers between devices with their start and end apart: 40, of which 22 were waited for; matrix products, arithmetic and copies ran while one was open for 0% of the time, Pallas kernels for 5%

profile of v2, /device:TPU:0, one launch (start us, length us, event | category | flops | bytes accessed | tf_op | source)
XLA Modules:
  0.0 164.1 jit_solution(5664067189150040181)
XLA Ops:
  4.1 1.2 shard_map.86
  5.9 2.0 %collective-permute-start.1 = (f32[16,8,128]{2,1,0:T(8,128)S(1)}, f32[16,8,128]{2,1,0:T(8,128)S(1)}, u32[]{:S(2)}, u32[]{:S(2)}) collective-permute-start(f32[16,8,128]{2,1,0:T(8,128)S(1)} %get-tuple-element.66), channel_id=1, source_target_pairs={{0,3},{1,0},{2,1},{3,2},{4,7},{5,4},{6,5},{7,6},{8,11},{9,8},{10,9... | collective-permute-start | bytes 196616 | tf_op jit(solution)/shard_map/ppermute | solution.py:411
  7.9 1.9 %collective-permute-done.refs_2_.ym.refs_3_ = f32[16,8,128]{2,1,0:T(8,128)S(1)} collective-permute-done((f32[16,8,128]{2,1,0:T(8,128)S(1)}, f32[16,8,128]{2,1,0:T(8,128)S(1)}, u32[]{:S(2)}, u32[]{:S(2)}) %collective-permute-start) | collective-permute-done | bytes 65568 | tf_op jit(solution)/shard_map/ppermute | solution.py:411
  10.3 1.9 %collective-permute-start.2 = (f32[20,8,128]{2,1,0:T(8,128)S(1)}, f32[20,8,128]{2,1,0:T(8,128)S(1)}, u32[]{:S(2)}, u32[]{:S(2)}) collective-permute-start(f32[20,8,128]{2,1,0:T(8,128)S(1)} %get-tuple-element.67), channel_id=1, source_target_pairs={{0,4},{4,8},{8,12},{12,16},{16,20},{20,24},{24,28},{28,0},{1,5},{5... | collective-permute-start | bytes 245768 | tf_op jit(solution)/shard_map/ppermute | solution.py:411
  12.2 3.1 %collective-permute-start.3 = (f32[20,8,128]{2,1,0:T(8,128)S(1)}, f32[20,8,128]{2,1,0:T(8,128)S(1)}, u32[]{:S(2)}, u32[]{:S(2)}) collective-permute-start(f32[20,8,128]{2,1,0:T(8,128)S(1)} %get-tuple-element.68), channel_id=1, source_target_pairs={{0,28},{4,0},{8,4},{12,8},{16,12},{20,16},{24,20},{28,24},{1,29},{... | collective-permute-start | bytes 245768 | tf_op jit(solution)/shard_map/ppermute | solution.py:411
  18.9 2.0 %shard_map.88 = (f32[190,8,128]{2,1,0:T(8,128)S(1)}, f32[180,8,128]{2,1,0:T(8,128)S(1)}, f32[180,8,128]{2,1,0:T(8,128)S(1)}, f32[180,8,128]{2,1,0:T(8,128)S(1)},...) custom-call(f32[128,8,128]{2,1,0:T(8,128)S(1)} %bitcast.3, f32[20,8,128]{2,1,0:T(8,128)S(1)} %collective-permute-done.2.xm.refs_1_, ...), custom_call_target="tpu_custom_call" | custom-call | flops 1000000 | bytes 5283840 | tf_op jit(solution)/shard_map/pallas_call | solution.py:21
  20.9 6.2 %shard_map.90 = (f32[80,8,128]{2,1,0:T(8,128)S(1)}, f32[81,8,128]{2,1,0:T(8,128)S(1)}, f32[81,8,128]{2,1,0:T(8,128)S(1)}, f32[12,8,128]{2,1,0:T(8,128)S(1)}, f32[176,8,128]{2,1,0:T(8,128)S(1)}) custom-call(f32[128,8,128]{2,1,0:T(8,128)S(1)} %bitcast.5, f32[20,8,128]{2,1,0:T(8,128)S(1)} %collective-permute-done.2.xm.refs_1_, ...), custom_call_target="tpu_custom_call" | custom-call | flops 20000000 | bytes 13336592 | tf_op jit(solution)/shard_map/pallas_call | solution.py:21
  27.3 1.6 collective-permute-start.5
  28.9 2.7 %shard_map.93 = (f32[72,8,128]{2,1,0:T(8,128)S(1)}, f32[73,8,128]{2,1,0:T(8,128)S(1)}, f32[73,8,128]{2,1,0:T(8,128)S(1)}, f32[11,8,128]{2,1,0:T(8,128)S(1)}) custom-call(f32[176,8,128]{2,1,0:T(8,128)S(1)} %get-tuple-element.85.g, f32[12,16,64,128]{3,2,1,0:T(8,128)S(1)} %shard_map.89.refs_11_.w, s32[1,1,2]{2,1,0:T(1,128)S(1)} %copy-done.5, ...), custom_call_target="tpu_custom_call" | custom-call | flops 10000000 | bytes 7950352 | tf_op jit(solution)/shard_map/pallas_call | solution.py:21
  31.6 1.7 %collective-permute-start.13 = (f32[73,8,128]{2,1,0:T(8,128)S(1)}, f32[73,8,128]{2,1,0:T(8,128)S(1)}, u32[]{:S(2)}, u32[]{:S(2)}) collective-permute-start(f32[73,8,128]{2,1,0:T(8,128)S(1)} %get-tuple-element.89), channel_id=1, source_target_pairs={{0,3},{1,0},{2,1},{3,2},{4,7},{5,4},{6,5},{7,6},{8,11},{9,8},{10,9... | collective-permute-start | bytes 897032 | tf_op jit(solution)/shard_map/ppermute | solution.py:411
  33.4 1.2 collective-permute-start.6
  34.6 10.1 %collective-permute-done.6.refs_3_.refs_4_ = f32[12,8,128]{2,1,0:T(8,128)S(1)} collective-permute-done((f32[12,8,128]{2,1,0:T(8,128)S(1)}, f32[12,8,128]{2,1,0:T(8,128)S(1)}, u32[]{:S(2)}, u32[]{:S(2)}) %collective-permute-start.6) | collective-permute-done | bytes 49184 | tf_op jit(solution)/shard_map/ppermute | solution.py:411
  44.7 1.2 collective-permute-start.14
  47.1 1.6 %collective-permute-done.14.refs_3_.refs_4_ = f32[11,8,128]{2,1,0:T(8,128)S(1)} collective-permute-done((f32[11,8,128]{2,1,0:T(8,128)S(1)}, f32[11,8,128]{2,1,0:T(8,128)S(1)}, u32[]{:S(2)}, u32[]{:S(2)}) %collective-permute-start.14) | collective-permute-done | bytes 45088 | tf_op jit(solution)/shard_map/ppermute | solution.py:411
  50.6 1.4 collective-permute-start.9
  52.6 2.1 %collective-permute-start.11 = (f32[16,8,128]{2,1,0:T(8,128)S(1)}, f32[16,8,128]{2,1,0:T(8,128)S(1)}, u32[]{:S(2)}, u32[]{:S(2)}) collective-permute-start(f32[16,8,128]{2,1,0:T(8,128)S(1)} %get-tuple-element.84), channel_id=1, source_target_pairs={{0,12},{4,16},{8,20},{12,24},{16,28},{20,0},{24,4},{28,8},{1,13},{... | collective-permute-start | bytes 196616 | tf_op jit(solution)/shard_map/ppermute | solution.py:411
  54.7 1.7 %collective-permute-start.19 = (f32[8,8,128]{2,1,0:T(8,128)S(1)}, f32[8,8,128]{2,1,0:T(8,128)S(1)}, u32[]{:S(2)}, u32[]{:S(2)}) collective-permute-start(f32[8,8,128]{2,1,0:T(8,128)S(1)} %get-tuple-element.96), channel_id=1, source_target_pairs={{0,20},{4,24},{8,28},{12,0},{16,4},{20,8},{24,12},{28,16},{1,21},{... | collective-permute-start | bytes 98312 | tf_op jit(solution)/shard_map/ppermute | solution.py:411
  56.5 4.7 %collective-permute-done.17.b = f32[64,8,128]{2,1,0:T(8,128)S(1)} collective-permute-done((f32[64,8,128]{2,1,0:T(8,128)S(1)}, f32[64,8,128]{2,1,0:T(8,128)S(1)}, u32[]{:S(2)}, u32[]{:S(2)}) %collective-permute-start.17) | collective-permute-done | bytes 262176 | tf_op jit(solution)/shard_map/ppermute | solution.py:415
  61.1 3.4 %collective-permute-start.16 = (f32[64,8,128]{2,1,0:T(8,128)S(1)}, f32[64,8,128]{2,1,0:T(8,128)S(1)}, u32[]{:S(2)}, u32[]{:S(2)}) collective-permute-start(f32[64,8,128]{2,1,0:T(8,128)S(1)} %get-tuple-element.93), channel_id=1, source_target_pairs={{0,24},{4,12},{8,0},{12,20},{16,8},{20,28},{24,16},{28,4},{1,25},{... | collective-permute-start | bytes 786440 | tf_op jit(solution)/shard_map/ppermute | solution.py:420
  64.6 2.2 %collective-permute-done.9.b = f32[64,8,128]{2,1,0:T(8,128)S(1)} collective-permute-done((f32[64,8,128]{2,1,0:T(8,128)S(1)}, f32[64,8,128]{2,1,0:T(8,128)S(1)}, u32[]{:S(2)}, u32[]{:S(2)}) %collective-permute-start.9) | collective-permute-done | bytes 262176 | tf_op jit(solution)/shard_map/ppermute | solution.py:415
  67.6 3.7 %collective-permute-start.8 = (f32[64,8,128]{2,1,0:T(8,128)S(1)}, f32[64,8,128]{2,1,0:T(8,128)S(1)}, u32[]{:S(2)}, u32[]{:S(2)}) collective-permute-start(f32[64,8,128]{2,1,0:T(8,128)S(1)} %get-tuple-element.81), channel_id=1, source_target_pairs={{0,24},{4,12},{8,0},{12,20},{16,8},{20,28},{24,16},{28,4},{1,25},{... | collective-permute-start | bytes 786440 | tf_op jit(solution)/shard_map/ppermute | solution.py:420
  71.4 1.3 collective-permute-start.10
  72.8 1.5 collective-permute-done.7.refs_1_
  74.2 3.7 %collective-permute-done.8.refs_2_ = f32[64,8,128]{2,1,0:T(8,128)S(1)} collective-permute-done((f32[64,8,128]{2,1,0:T(8,128)S(1)}, f32[64,8,128]{2,1,0:T(8,128)S(1)}, u32[]{:S(2)}, u32[]{:S(2)}) %collective-permute-start.8) | collective-permute-done | bytes 262176 | tf_op jit(solution)/shard_map/ppermute | solution.py:420
  78.0 5.4 %collective-permute-done.18.refs_8_ = f32[64,8,128]{2,1,0:T(8,128)S(1)} collective-permute-done((f32[64,8,128]{2,1,0:T(8,128)S(1)}, f32[64,8,128]{2,1,0:T(8,128)S(1)}, u32[]{:S(2)}, u32[]{:S(2)}) %collective-permute-start.18) | collective-permute-done | bytes 262176 | tf_op jit(solution)/shard_map/ppermute | solution.py:420
  83.4 2.8 %collective-permute-done.10.refs_3_ = f32[64,8,128]{2,1,0:T(8,128)S(1)} collective-permute-done((f32[64,8,128]{2,1,0:T(8,128)S(1)}, f32[64,8,128]{2,1,0:T(8,128)S(1)}, u32[]{:S(2)}, u32[]{:S(2)}) %collective-permute-start.10) | collective-permute-done | bytes 262176 | tf_op jit(solution)/shard_map/ppermute | solution.py:420
  86.4 1.7 %collective-permute-start.21 = (f32[16,8,128]{2,1,0:T(8,128)S(1)}, f32[16,8,128]{2,1,0:T(8,128)S(1)}, u32[]{:S(2)}, u32[]{:S(2)}) collective-permute-start(f32[16,8,128]{2,1,0:T(8,128)S(1)} %get-tuple-element.99), channel_id=1, source_target_pairs={{0,3},{1,0},{2,1},{3,2},{4,7},{5,4},{6,5},{7,6},{8,11},{9,8},{10,9... | collective-permute-start | bytes 196616 | tf_op jit(solution)/shard_map/ppermute | solution.py:411
  88.2 1.9 %collective-permute-done.20.refs_1_.refs_3_ = f32[16,8,128]{2,1,0:T(8,128)S(1)} collective-permute-done((f32[16,8,128]{2,1,0:T(8,128)S(1)}, f32[16,8,128]{2,1,0:T(8,128)S(1)}, u32[]{:S(2)}, u32[]{:S(2)}) %collective-permute-start.20) | collective-permute-done | bytes 65568 | tf_op jit(solution)/shard_map/ppermute | solution.py:411
  90.2 4.7 %collective-permute-start.23 = (f32[20,8,128]{2,1,0:T(8,128)S(1)}, f32[20,8,128]{2,1,0:T(8,128)S(1)}, u32[]{:S(2)}, u32[]{:S(2)}) collective-permute-start(f32[20,8,128]{2,1,0:T(8,128)S(1)} %get-tuple-element.101), channel_id=1, source_target_pairs={{0,28},{4,0},{8,4},{12,8},{16,12},{20,16},{24,20},{28,24},{1,29},{... | collective-permute-start | bytes 245768 | tf_op jit(solution)/shard_map/ppermute | solution.py:411
  95.4 2.5 %collective-permute-done.22.refs_1_ = f32[20,8,128]{2,1,0:T(8,128)S(1)} collective-permute-done((f32[20,8,128]{2,1,0:T(8,128)S(1)}, f32[20,8,128]{2,1,0:T(8,128)S(1)}, u32[]{:S(2)}, u32[]{:S(2)}) %collective-permute-start.22) | collective-permute-done | bytes 81952 | tf_op jit(solution)/shard_map/ppermute | solution.py:411
  97.9 6.2 %shard_map.99 = (f32[80,8,128]{2,1,0:T(8,128)S(1)}, f32[81,8,128]{2,1,0:T(8,128)S(1)}, f32[81,8,128]{2,1,0:T(8,128)S(1)}, f32[12,8,128]{2,1,0:T(8,128)S(1)}, f32[176,8,128]{2,1,0:T(8,128)S(1)}) custom-call(f32[128,8,128]{2,1,0:T(8,128)S(1)} %get-tuple-element.97.refs_0_, f32[20,8,128]{2,1,0:T(8,128)S(1)} %collective-permute-done.22.refs_1_, ...), custom_call_target="tpu_custom_call" | custom-call | flops 20000000 | bytes 13336592 | tf_op jit(solution)/shard_map/pallas_call | solution.py:21
  104.4 1.5 collective-permute-start.25
  105.9 2.7 %shard_map.102 = (f32[72,8,128]{2,1,0:T(8,128)S(1)}, f32[73,8,128]{2,1,0:T(8,128)S(1)}, f32[73,8,128]{2,1,0:T(8,128)S(1)}, f32[11,8,128]{2,1,0:T(8,128)S(1)}) custom-call(f32[176,8,128]{2,1,0:T(8,128)S(1)} %get-tuple-element.112.g, f32[12,16,64,128]{3,2,1,0:T(8,128)S(1)} %shard_map.98.refs_11_.w, s32[1,1,2]{2,1,0:T(1,128)S(1)} %copy-done.5, ...), custom_call_target="tpu_custom_call" | custom-call | flops 10000000 | bytes 7950352 | tf_op jit(solution)/shard_map/pallas_call | solution.py:21
  108.6 1.7 %collective-permute-start.33 = (f32[73,8,128]{2,1,0:T(8,128)S(1)}, f32[73,8,128]{2,1,0:T(8,128)S(1)}, u32[]{:S(2)}, u32[]{:S(2)}) collective-permute-start(f32[73,8,128]{2,1,0:T(8,128)S(1)} %get-tuple-element.116), channel_id=1, source_target_pairs={{0,3},{1,0},{2,1},{3,2},{4,7},{5,4},{6,5},{7,6},{8,11},{9,8},{10,9... | collective-permute-start | bytes 897032 | tf_op jit(solution)/shard_map/ppermute | solution.py:411
  110.4 1.6 collective-permute-start.26
  112.0 9.8 %collective-permute-done.26.refs_3_.refs_4_ = f32[12,8,128]{2,1,0:T(8,128)S(1)} collective-permute-done((f32[12,8,128]{2,1,0:T(8,128)S(1)}, f32[12,8,128]{2,1,0:T(8,128)S(1)}, u32[]{:S(2)}, u32[]{:S(2)}) %collective-permute-start.26) | collective-permute-done | bytes 49184 | tf_op jit(solution)/shard_map/ppermute | solution.py:411
  121.7 1.6 collective-permute-start.34
  124.5 1.3 collective-permute-done.34.refs_3_.refs_4_
  126.9 1.6 collective-permute-start.37
  129.0 1.5 collective-permute-start.35
  131.1 3.2 %collective-permute-start.39 = (f32[8,8,128]{2,1,0:T(8,128)S(1)}, f32[8,8,128]{2,1,0:T(8,128)S(1)}, u32[]{:S(2)}, u32[]{:S(2)}) collective-permute-start(f32[8,8,128]{2,1,0:T(8,128)S(1)} %get-tuple-element.123), channel_id=1, source_target_pairs={{0,20},{4,24},{8,28},{12,0},{16,4},{20,8},{24,12},{28,16},{1,21},{... | collective-permute-start | bytes 98312 | tf_op jit(solution)/shard_map/ppermute | solution.py:411
  134.3 3.6 %collective-permute-done.37.b = f32[64,8,128]{2,1,0:T(8,128)S(1)} collective-permute-done((f32[64,8,128]{2,1,0:T(8,128)S(1)}, f32[64,8,128]{2,1,0:T(8,128)S(1)}, u32[]{:S(2)}, u32[]{:S(2)}) %collective-permute-start.37) | collective-permute-done | bytes 262176 | tf_op jit(solution)/shard_map/ppermute | solution.py:415
  137.9 3.7 %collective-permute-start.36 = (f32[64,8,128]{2,1,0:T(8,128)S(1)}, f32[64,8,128]{2,1,0:T(8,128)S(1)}, u32[]{:S(2)}, u32[]{:S(2)}) collective-permute-start(f32[64,8,128]{2,1,0:T(8,128)S(1)} %get-tuple-element.120), channel_id=1, source_target_pairs={{0,24},{4,12},{8,0},{12,20},{16,8},{20,28},{24,16},{28,4},{1,25},{... | collective-permute-start | bytes 786440 | tf_op jit(solution)/shard_map/ppermute | solution.py:420
  141.7 2.1 %collective-permute-done.29.b = f32[64,8,128]{2,1,0:T(8,128)S(1)} collective-permute-done((f32[64,8,128]{2,1,0:T(8,128)S(1)}, f32[64,8,128]{2,1,0:T(8,128)S(1)}, u32[]{:S(2)}, u32[]{:S(2)}) %collective-permute-start.29) | collective-permute-done | bytes 262176 | tf_op jit(solution)/shard_map/ppermute | solution.py:415
  143.9 1.5 collective-permute-start.27
  145.4 3.1 %collective-permute-start.28 = (f32[64,8,128]{2,1,0:T(8,128)S(1)}, f32[64,8,128]{2,1,0:T(8,128)S(1)}, u32[]{:S(2)}, u32[]{:S(2)}) collective-permute-start(f32[64,8,128]{2,1,0:T(8,128)S(1)} %get-tuple-element.108), channel_id=1, source_target_pairs={{0,24},{4,12},{8,0},{12,20},{16,8},{20,28},{24,16},{28,4},{1,25},{... | collective-permute-start | bytes 786440 | tf_op jit(solution)/shard_map/ppermute | solution.py:420
  149.7 2.2 %collective-permute-done.27.refs_1_ = f32[64,8,128]{2,1,0:T(8,128)S(1)} collective-permute-done((f32[64,8,128]{2,1,0:T(8,128)S(1)}, f32[64,8,128]{2,1,0:T(8,128)S(1)}, u32[]{:S(2)}, u32[]{:S(2)}) %collective-permute-start.27) | collective-permute-done | bytes 262176 | tf_op jit(solution)/shard_map/ppermute | solution.py:415
  151.9 11.1 %collective-permute-done.28.refs_2_ = f32[64,8,128]{2,1,0:T(8,128)S(1)} collective-permute-done((f32[64,8,128]{2,1,0:T(8,128)S(1)}, f32[64,8,128]{2,1,0:T(8,128)S(1)}, u32[]{:S(2)}, u32[]{:S(2)}) %collective-permute-start.28) | collective-permute-done | bytes 262176 | tf_op jit(solution)/shard_map/ppermute | solution.py:420
  (68 shorter events, 20.1 us)
Async XLA Ops:
  0.6 1.0 copy-start.2
  1.6 0.9 copy-start.3
  2.5 0.9 copy-start.4
  3.4 0.7 copy-start.7
  4.1 16.8 %copy-start.5 = (s32[1,1,2]{2,1,0:T(1,128)S(1)}, s32[1,1,2]{2,1,0:T(1,128)}, u32[]{:S(2)}) copy-start(s32[1,1,2]{2,1,0:T(1,128)} %refs_5_.7) | copy-start | bytes 28
  4.1 16.8 %copy-start.6 = (s32[1,1,2]{2,1,0:T(1,128)S(1)}, s32[1,1,2]{2,1,0:T(1,128)}, u32[]{:S(2)}) copy-start(s32[1,1,2]{2,1,0:T(1,128)} %sy.3) | copy-start | bytes 28
  5.3 4.4 %collective-permute-start = (f32[16,8,128]{2,1,0:T(8,128)S(1)}, f32[16,8,128]{2,1,0:T(8,128)S(1)}, u32[]{:S(2)}, u32[]{:S(2)}) collective-permute-start(f32[16,8,128]{2,1,0:T(8,128)S(1)} %get-tuple-element.65), channel_id=1, source_target_pairs={{0,1},{1,2},{2,3},{3,0},{4,5},{5,6},{6,7},{7,4},{8,9},{9,10},{10,1... | collective-permute-start | bytes 196616 | tf_op jit(solution)/shard_map/ppermute | solution.py:411
  5.9 4.4 %collective-permute-start.1 = (f32[16,8,128]{2,1,0:T(8,128)S(1)}, f32[16,8,128]{2,1,0:T(8,128)S(1)}, u32[]{:S(2)}, u32[]{:S(2)}) collective-permute-start(f32[16,8,128]{2,1,0:T(8,128)S(1)} %get-tuple-element.66), channel_id=1, source_target_pairs={{0,3},{1,0},{2,1},{3,2},{4,7},{5,4},{6,5},{7,6},{8,11},{9,8},{10,9... | collective-permute-start | bytes 196616 | tf_op jit(solution)/shard_map/ppermute | solution.py:411
  10.3 7.4 %collective-permute-start.2 = (f32[20,8,128]{2,1,0:T(8,128)S(1)}, f32[20,8,128]{2,1,0:T(8,128)S(1)}, u32[]{:S(2)}, u32[]{:S(2)}) collective-permute-start(f32[20,8,128]{2,1,0:T(8,128)S(1)} %get-tuple-element.67), channel_id=1, source_target_pairs={{0,4},{4,8},{8,12},{12,16},{16,20},{20,24},{24,28},{28,0},{1,5},{5... | collective-permute-start | bytes 245768 | tf_op jit(solution)/shard_map/ppermute | solution.py:411
  12.2 6.7 %collective-permute-start.3 = (f32[20,8,128]{2,1,0:T(8,128)S(1)}, f32[20,8,128]{2,1,0:T(8,128)S(1)}, u32[]{:S(2)}, u32[]{:S(2)}) collective-permute-start(f32[20,8,128]{2,1,0:T(8,128)S(1)} %get-tuple-element.68), channel_id=1, source_target_pairs={{0,28},{4,0},{8,4},{12,8},{16,12},{20,16},{24,20},{28,24},{1,29},{... | collective-permute-start | bytes 245768 | tf_op jit(solution)/shard_map/ppermute | solution.py:411
  15.3 1.1 copy-start
  27.1 18.9 %collective-permute-start.4 = (f32[81,8,128]{2,1,0:T(8,128)S(1)}, f32[81,8,128]{2,1,0:T(8,128)S(1)}, u32[]{:S(2)}, u32[]{:S(2)}) collective-permute-start(f32[81,8,128]{2,1,0:T(8,128)S(1)} %get-tuple-element.76), channel_id=1, source_target_pairs={{0,1},{1,2},{2,3},{3,0},{4,5},{5,6},{6,7},{7,4},{8,9},{9,10},{10,1... | collective-permute-start | bytes 995336 | tf_op jit(solution)/shard_map/ppermute | solution.py:411
  27.3 18.6 %collective-permute-start.5 = (f32[81,8,128]{2,1,0:T(8,128)S(1)}, f32[81,8,128]{2,1,0:T(8,128)S(1)}, u32[]{:S(2)}, u32[]{:S(2)}) collective-permute-start(f32[81,8,128]{2,1,0:T(8,128)S(1)} %get-tuple-element.77), channel_id=1, source_target_pairs={{0,3},{1,0},{2,1},{3,2},{4,7},{5,4},{6,5},{7,6},{8,11},{9,8},{10,9... | collective-permute-start | bytes 995336 | tf_op jit(solution)/shard_map/ppermute | solution.py:411
  28.9 66.0 %copy-start.1 = (f32[2,3,16,16,128]{4,3,2,1,0:T(8,128)S(1)}, f32[2,3,16,16,128]{4,3,2,1,0:T(8,128)}, u32[]{:S(2)}) copy-start(f32[2,3,16,16,128]{4,3,2,1,0:T(8,128)} %fraction.3) | copy-start | bytes 2359300
  31.6 17.2 %collective-permute-start.12 = (f32[73,8,128]{2,1,0:T(8,128)S(1)}, f32[73,8,128]{2,1,0:T(8,128)S(1)}, u32[]{:S(2)}, u32[]{:S(2)}) collective-permute-start(f32[73,8,128]{2,1,0:T(8,128)S(1)} %get-tuple-element.88), channel_id=1, source_target_pairs={{0,1},{1,2},{2,3},{3,0},{4,5},{5,6},{6,7},{7,4},{8,9},{9,10},{10,1... | collective-permute-start | bytes 897032 | tf_op jit(solution)/shard_map/ppermute | solution.py:411
  31.6 17.1 %collective-permute-start.13 = (f32[73,8,128]{2,1,0:T(8,128)S(1)}, f32[73,8,128]{2,1,0:T(8,128)S(1)}, u32[]{:S(2)}, u32[]{:S(2)}) collective-permute-start(f32[73,8,128]{2,1,0:T(8,128)S(1)} %get-tuple-element.89), channel_id=1, source_target_pairs={{0,3},{1,0},{2,1},{3,2},{4,7},{5,4},{6,5},{7,6},{8,11},{9,8},{10,9... | collective-permute-start | bytes 897032 | tf_op jit(solution)/shard_map/ppermute | solution.py:411
  33.4 11.3 %collective-permute-start.6 = (f32[12,8,128]{2,1,0:T(8,128)S(1)}, f32[12,8,128]{2,1,0:T(8,128)S(1)}, u32[]{:S(2)}, u32[]{:S(2)}) collective-permute-start(f32[12,8,128]{2,1,0:T(8,128)S(1)} %get-tuple-element.78), channel_id=1, source_target_pairs={{0,2},{1,3},{2,0},{3,1},{4,6},{5,7},{6,4},{7,5},{8,10},{9,11},{10,... | collective-permute-start | bytes 147464 | tf_op jit(solution)/shard_map/ppermute | solution.py:411
  44.7 4.0 %collective-permute-start.14 = (f32[11,8,128]{2,1,0:T(8,128)S(1)}, f32[11,8,128]{2,1,0:T(8,128)S(1)}, u32[]{:S(2)}, u32[]{:S(2)}) collective-permute-start(f32[11,8,128]{2,1,0:T(8,128)S(1)} %get-tuple-element.90), channel_id=1, source_target_pairs={{0,2},{1,3},{2,0},{3,1},{4,6},{5,7},{6,4},{7,5},{8,10},{9,11},{10,... | collective-permute-start | bytes 135176 | tf_op jit(solution)/shard_map/ppermute | solution.py:411
  49.9 11.3 %collective-permute-start.17 = (f32[64,8,128]{2,1,0:T(8,128)S(1)}, f32[64,8,128]{2,1,0:T(8,128)S(1)}, u32[]{:S(2)}, u32[]{:S(2)}) collective-permute-start(f32[64,8,128]{2,1,0:T(8,128)S(1)} %get-tuple-element.95), channel_id=1, source_target_pairs={{0,4},{4,0},{8,12},{12,8},{16,20},{20,16},{24,28},{28,24},{1,5},{5... | collective-permute-start | bytes 786440 | tf_op jit(solution)/shard_map/ppermute | solution.py:415
  50.6 16.1 %collective-permute-start.9 = (f32[64,8,128]{2,1,0:T(8,128)S(1)}, f32[64,8,128]{2,1,0:T(8,128)S(1)}, u32[]{:S(2)}, u32[]{:S(2)}) collective-permute-start(f32[64,8,128]{2,1,0:T(8,128)S(1)} %get-tuple-element.83), channel_id=1, source_target_pairs={{0,4},{4,0},{8,12},{12,8},{16,20},{20,16},{24,28},{28,24},{1,5},{5... | collective-permute-start | bytes 786440 | tf_op jit(solution)/shard_map/ppermute | solution.py:415
  52.0 19.5 %collective-permute-start.15 = (f32[64,8,128]{2,1,0:T(8,128)S(1)}, f32[64,8,128]{2,1,0:T(8,128)S(1)}, u32[]{:S(2)}, u32[]{:S(2)}) collective-permute-start(f32[64,8,128]{2,1,0:T(8,128)S(1)} %get-tuple-element.92), channel_id=1, source_target_pairs={{0,4},{4,0},{8,12},{12,8},{16,20},{20,16},{24,28},{28,24},{1,5},{5... | collective-permute-start | bytes 786440 | tf_op jit(solution)/shard_map/ppermute | solution.py:415
  52.6 18.7 %collective-permute-start.11 = (f32[16,8,128]{2,1,0:T(8,128)S(1)}, f32[16,8,128]{2,1,0:T(8,128)S(1)}, u32[]{:S(2)}, u32[]{:S(2)}) collective-permute-start(f32[16,8,128]{2,1,0:T(8,128)S(1)} %get-tuple-element.84), channel_id=1, source_target_pairs={{0,12},{4,16},{8,20},{12,24},{16,28},{20,0},{24,4},{28,8},{1,13},{... | collective-permute-start | bytes 196616 | tf_op jit(solution)/shard_map/ppermute | solution.py:411
  54.7 12.9 %collective-permute-start.19 = (f32[8,8,128]{2,1,0:T(8,128)S(1)}, f32[8,8,128]{2,1,0:T(8,128)S(1)}, u32[]{:S(2)}, u32[]{:S(2)}) collective-permute-start(f32[8,8,128]{2,1,0:T(8,128)S(1)} %get-tuple-element.96), channel_id=1, source_target_pairs={{0,20},{4,24},{8,28},{12,0},{16,4},{20,8},{24,12},{28,16},{1,21},{... | collective-permute-start | bytes 98312 | tf_op jit(solution)/shard_map/ppermute | solution.py:411
  61.1 11.6 %collective-permute-start.16 = (f32[64,8,128]{2,1,0:T(8,128)S(1)}, f32[64,8,128]{2,1,0:T(8,128)S(1)}, u32[]{:S(2)}, u32[]{:S(2)}) collective-permute-start(f32[64,8,128]{2,1,0:T(8,128)S(1)} %get-tuple-element.93), channel_id=1, source_target_pairs={{0,24},{4,12},{8,0},{12,20},{16,8},{20,28},{24,16},{28,4},{1,25},{... | collective-permute-start | bytes 786440 | tf_op jit(solution)/shard_map/ppermute | solution.py:420
  66.8 7.5 %collective-permute-start.7 = (f32[64,8,128]{2,1,0:T(8,128)S(1)}, f32[64,8,128]{2,1,0:T(8,128)S(1)}, u32[]{:S(2)}, u32[]{:S(2)}) collective-permute-start(f32[64,8,128]{2,1,0:T(8,128)S(1)} %get-tuple-element.80), channel_id=1, source_target_pairs={{0,4},{4,0},{8,12},{12,8},{16,20},{20,16},{24,28},{28,24},{1,5},{5... | collective-permute-start | bytes 786440 | tf_op jit(solution)/shard_map/ppermute | solution.py:415
  67.6 10.4 %collective-permute-start.8 = (f32[64,8,128]{2,1,0:T(8,128)S(1)}, f32[64,8,128]{2,1,0:T(8,128)S(1)}, u32[]{:S(2)}, u32[]{:S(2)}) collective-permute-start(f32[64,8,128]{2,1,0:T(8,128)S(1)} %get-tuple-element.81), channel_id=1, source_target_pairs={{0,24},{4,12},{8,0},{12,20},{16,8},{20,28},{24,16},{28,4},{1,25},{... | collective-permute-start | bytes 786440 | tf_op jit(solution)/shard_map/ppermute | solution.py:420
  71.3 12.1 %collective-permute-start.18 = (f32[64,8,128]{2,1,0:T(8,128)S(1)}, f32[64,8,128]{2,1,0:T(8,128)S(1)}, u32[]{:S(2)}, u32[]{:S(2)}) collective-permute-start(f32[64,8,128]{2,1,0:T(8,128)S(1)} %shard_map.95), channel_id=1, source_target_pairs={{0,8},{4,28},{8,16},{12,4},{16,24},{20,12},{24,0},{28,20},{1,9},{5... | collective-permute-start | bytes 786440 | tf_op jit(solution)/shard_map/ppermute | solution.py:420
  71.4 14.7 %collective-permute-start.10 = (f32[64,8,128]{2,1,0:T(8,128)S(1)}, f32[64,8,128]{2,1,0:T(8,128)S(1)}, u32[]{:S(2)}, u32[]{:S(2)}) collective-permute-start(f32[64,8,128]{2,1,0:T(8,128)S(1)} %shard_map.92), channel_id=1, source_target_pairs={{0,8},{4,28},{8,16},{12,4},{16,24},{20,12},{24,0},{28,20},{1,9},{5... | collective-permute-start | bytes 786440 | tf_op jit(solution)/shard_map/ppermute | solution.py:420
  86.4 3.7 %collective-permute-start.20 = (f32[16,8,128]{2,1,0:T(8,128)S(1)}, f32[16,8,128]{2,1,0:T(8,128)S(1)}, u32[]{:S(2)}, u32[]{:S(2)}) collective-permute-start(f32[16,8,128]{2,1,0:T(8,128)S(1)} %get-tuple-element.98), channel_id=1, source_target_pairs={{0,1},{1,2},{2,3},{3,0},{4,5},{5,6},{6,7},{7,4},{8,9},{9,10},{10,1... | collective-permute-start | bytes 196616 | tf_op jit(solution)/shard_map/ppermute | solution.py:411
  86.4 3.7 %collective-permute-start.21 = (f32[16,8,128]{2,1,0:T(8,128)S(1)}, f32[16,8,128]{2,1,0:T(8,128)S(1)}, u32[]{:S(2)}, u32[]{:S(2)}) collective-permute-start(f32[16,8,128]{2,1,0:T(8,128)S(1)} %get-tuple-element.99), channel_id=1, source_target_pairs={{0,3},{1,0},{2,1},{3,2},{4,7},{5,4},{6,5},{7,6},{8,11},{9,8},{10,9... | collective-permute-start | bytes 196616 | tf_op jit(solution)/shard_map/ppermute | solution.py:411
  90.1 7.8 %collective-permute-start.22 = (f32[20,8,128]{2,1,0:T(8,128)S(1)}, f32[20,8,128]{2,1,0:T(8,128)S(1)}, u32[]{:S(2)}, u32[]{:S(2)}) collective-permute-start(f32[20,8,128]{2,1,0:T(8,128)S(1)} %get-tuple-element.100), channel_id=1, source_target_pairs={{0,4},{4,8},{8,12},{12,16},{16,20},{20,24},{24,28},{28,0},{1,5},{5... | collective-permute-start | bytes 245768 | tf_op jit(solution)/shard_map/ppermute | solution.py:411
  90.2 7.7 %collective-permute-start.23 = (f32[20,8,128]{2,1,0:T(8,128)S(1)}, f32[20,8,128]{2,1,0:T(8,128)S(1)}, u32[]{:S(2)}, u32[]{:S(2)}) collective-permute-start(f32[20,8,128]{2,1,0:T(8,128)S(1)} %get-tuple-element.101), channel_id=1, source_target_pairs={{0,28},{4,0},{8,4},{12,8},{16,12},{20,16},{24,20},{28,24},{1,29},{... | collective-permute-start | bytes 245768 | tf_op jit(solution)/shard_map/ppermute | solution.py:411
  104.1 19.2 %collective-permute-start.24 = (f32[81,8,128]{2,1,0:T(8,128)S(1)}, f32[81,8,128]{2,1,0:T(8,128)S(1)}, u32[]{:S(2)}, u32[]{:S(2)}) collective-permute-start(f32[81,8,128]{2,1,0:T(8,128)S(1)} %get-tuple-element.103), channel_id=1, source_target_pairs={{0,1},{1,2},{2,3},{3,0},{4,5},{5,6},{6,7},{7,4},{8,9},{9,10},{10,1... | collective-permute-start | bytes 995336 | tf_op jit(solution)/shard_map/ppermute | solution.py:411
  104.4 18.9 %collective-permute-start.25 = (f32[81,8,128]{2,1,0:T(8,128)S(1)}, f32[81,8,128]{2,1,0:T(8,128)S(1)}, u32[]{:S(2)}, u32[]{:S(2)}) collective-permute-start(f32[81,8,128]{2,1,0:T(8,128)S(1)} %get-tuple-element.104), channel_id=1, source_target_pairs={{0,3},{1,0},{2,1},{3,2},{4,7},{5,4},{6,5},{7,6},{8,11},{9,8},{10,9... | collective-permute-start | bytes 995336 | tf_op jit(solution)/shard_map/ppermute | solution.py:411
  108.6 17.2 %collective-permute-start.32 = (f32[73,8,128]{2,1,0:T(8,128)S(1)}, f32[73,8,128]{2,1,0:T(8,128)S(1)}, u32[]{:S(2)}, u32[]{:S(2)}) collective-permute-start(f32[73,8,128]{2,1,0:T(8,128)S(1)} %get-tuple-element.115), channel_id=1, source_target_pairs={{0,1},{1,2},{2,3},{3,0},{4,5},{5,6},{6,7},{7,4},{8,9},{9,10},{10,1... | collective-permute-start | bytes 897032 | tf_op jit(solution)/shard_map/ppermute | solution.py:411
  108.6 17.1 %collective-permute-start.33 = (f32[73,8,128]{2,1,0:T(8,128)S(1)}, f32[73,8,128]{2,1,0:T(8,128)S(1)}, u32[]{:S(2)}, u32[]{:S(2)}) collective-permute-start(f32[73,8,128]{2,1,0:T(8,128)S(1)} %get-tuple-element.116), channel_id=1, source_target_pairs={{0,3},{1,0},{2,1},{3,2},{4,7},{5,4},{6,5},{7,6},{8,11},{9,8},{10,9... | collective-permute-start | bytes 897032 | tf_op jit(solution)/shard_map/ppermute | solution.py:411
  110.4 11.3 %collective-permute-start.26 = (f32[12,8,128]{2,1,0:T(8,128)S(1)}, f32[12,8,128]{2,1,0:T(8,128)S(1)}, u32[]{:S(2)}, u32[]{:S(2)}) collective-permute-start(f32[12,8,128]{2,1,0:T(8,128)S(1)} %get-tuple-element.105), channel_id=1, source_target_pairs={{0,2},{1,3},{2,0},{3,1},{4,6},{5,7},{6,4},{7,5},{8,10},{9,11},{10,... | collective-permute-start | bytes 147464 | tf_op jit(solution)/shard_map/ppermute | solution.py:411
  121.7 4.0 %collective-permute-start.34 = (f32[11,8,128]{2,1,0:T(8,128)S(1)}, f32[11,8,128]{2,1,0:T(8,128)S(1)}, u32[]{:S(2)}, u32[]{:S(2)}) collective-permute-start(f32[11,8,128]{2,1,0:T(8,128)S(1)} %get-tuple-element.117), channel_id=1, source_target_pairs={{0,2},{1,3},{2,0},{3,1},{4,6},{5,7},{6,4},{7,5},{8,10},{9,11},{10,... | collective-permute-start | bytes 135176 | tf_op jit(solution)/shard_map/ppermute | solution.py:411
  126.9 11.0 %collective-permute-start.37 = (f32[64,8,128]{2,1,0:T(8,128)S(1)}, f32[64,8,128]{2,1,0:T(8,128)S(1)}, u32[]{:S(2)}, u32[]{:S(2)}) collective-permute-start(f32[64,8,128]{2,1,0:T(8,128)S(1)} %get-tuple-element.122), channel_id=1, source_target_pairs={{0,4},{4,0},{8,12},{12,8},{16,20},{20,16},{24,28},{28,24},{1,5},{5... | collective-permute-start | bytes 786440 | tf_op jit(solution)/shard_map/ppermute | solution.py:415
  128.5 15.4 %collective-permute-start.29 = (f32[64,8,128]{2,1,0:T(8,128)S(1)}, f32[64,8,128]{2,1,0:T(8,128)S(1)}, u32[]{:S(2)}, u32[]{:S(2)}) collective-permute-start(f32[64,8,128]{2,1,0:T(8,128)S(1)} %get-tuple-element.110), channel_id=1, source_target_pairs={{0,4},{4,0},{8,12},{12,8},{16,20},{20,16},{24,28},{28,24},{1,5},{5... | collective-permute-start | bytes 786440 | tf_op jit(solution)/shard_map/ppermute | solution.py:415
  129.0 20.1 %collective-permute-start.35 = (f32[64,8,128]{2,1,0:T(8,128)S(1)}, f32[64,8,128]{2,1,0:T(8,128)S(1)}, u32[]{:S(2)}, u32[]{:S(2)}) collective-permute-start(f32[64,8,128]{2,1,0:T(8,128)S(1)} %get-tuple-element.119), channel_id=1, source_target_pairs={{0,4},{4,0},{8,12},{12,8},{16,20},{20,16},{24,28},{28,24},{1,5},{5... | collective-permute-start | bytes 786440 | tf_op jit(solution)/shard_map/ppermute | solution.py:415
  130.5 18.0 %collective-permute-start.31 = (f32[16,8,128]{2,1,0:T(8,128)S(1)}, f32[16,8,128]{2,1,0:T(8,128)S(1)}, u32[]{:S(2)}, u32[]{:S(2)}) collective-permute-start(f32[16,8,128]{2,1,0:T(8,128)S(1)} %get-tuple-element.111), channel_id=1, source_target_pairs={{0,12},{4,16},{8,20},{12,24},{16,28},{20,0},{24,4},{28,8},{1,13},{... | collective-permute-start | bytes 196616 | tf_op jit(solution)/shard_map/ppermute | solution.py:411
  131.1 14.3 %collective-permute-start.39 = (f32[8,8,128]{2,1,0:T(8,128)S(1)}, f32[8,8,128]{2,1,0:T(8,128)S(1)}, u32[]{:S(2)}, u32[]{:S(2)}) collective-permute-start(f32[8,8,128]{2,1,0:T(8,128)S(1)} %get-tuple-element.123), channel_id=1, source_target_pairs={{0,20},{4,24},{8,28},{12,0},{16,4},{20,8},{24,12},{28,16},{1,21},{... | collective-permute-start | bytes 98312 | tf_op jit(solution)/shard_map/ppermute | solution.py:411
  137.9 11.7 %collective-permute-start.36 = (f32[64,8,128]{2,1,0:T(8,128)S(1)}, f32[64,8,128]{2,1,0:T(8,128)S(1)}, u32[]{:S(2)}, u32[]{:S(2)}) collective-permute-start(f32[64,8,128]{2,1,0:T(8,128)S(1)} %get-tuple-element.120), channel_id=1, source_target_pairs={{0,24},{4,12},{8,0},{12,20},{16,8},{20,28},{24,16},{28,4},{1,25},{... | collective-permute-start | bytes 786440 | tf_op jit(solution)/shard_map/ppermute | solution.py:420
  143.9 8.0 %collective-permute-start.27 = (f32[64,8,128]{2,1,0:T(8,128)S(1)}, f32[64,8,128]{2,1,0:T(8,128)S(1)}, u32[]{:S(2)}, u32[]{:S(2)}) collective-permute-start(f32[64,8,128]{2,1,0:T(8,128)S(1)} %get-tuple-element.107), channel_id=1, source_target_pairs={{0,4},{4,0},{8,12},{12,8},{16,20},{20,16},{24,28},{28,24},{1,5},{5... | collective-permute-start | bytes 786440 | tf_op jit(solution)/shard_map/ppermute | solution.py:415
  145.4 17.6 %collective-permute-start.28 = (f32[64,8,128]{2,1,0:T(8,128)S(1)}, f32[64,8,128]{2,1,0:T(8,128)S(1)}, u32[]{:S(2)}, u32[]{:S(2)}) collective-permute-start(f32[64,8,128]{2,1,0:T(8,128)S(1)} %get-tuple-element.108), channel_id=1, source_target_pairs={{0,24},{4,12},{8,0},{12,20},{16,8},{20,28},{24,16},{28,4},{1,25},{... | collective-permute-start | bytes 786440 | tf_op jit(solution)/shard_map/ppermute | solution.py:420
  148.5 14.5 %collective-permute-start.38 = (f32[64,8,128]{2,1,0:T(8,128)S(1)}, f32[64,8,128]{2,1,0:T(8,128)S(1)}, u32[]{:S(2)}, u32[]{:S(2)}) collective-permute-start(f32[64,8,128]{2,1,0:T(8,128)S(1)} %shard_map.104), channel_id=1, source_target_pairs={{0,8},{4,28},{8,16},{12,4},{16,24},{20,12},{24,0},{28,20},{1,9},{5... | collective-permute-start | bytes 786440 | tf_op jit(solution)/shard_map/ppermute | solution.py:420
  149.1 13.9 %collective-permute-start.30 = (f32[64,8,128]{2,1,0:T(8,128)S(1)}, f32[64,8,128]{2,1,0:T(8,128)S(1)}, u32[]{:S(2)}, u32[]{:S(2)}) collective-permute-start(f32[64,8,128]{2,1,0:T(8,128)S(1)} %shard_map.101), channel_id=1, source_target_pairs={{0,8},{4,28},{8,16},{12,4},{16,24},{20,12},{24,0},{28,20},{1,9},{5... | collective-permute-start | bytes 786440 | tf_op jit(solution)/shard_map/ppermute | solution.py:420

commit v3 on v2

v3 whole, which is shorter than its diff:
```python
import functools

import jax
import jax.numpy as jnp
from jax import lax
from jax.experimental import pallas as pl
from jax.experimental.pallas import tpu as pltpu
from jax.sharding import PartitionSpec as P


STEPS = 2
BUOYANCY = 0.8
FIELDS = 4
SUB = 8
VMEM = pl.BlockSpec(memory_space=pltpu.VMEM)
SMEM = pl.BlockSpec(memory_space=pltpu.SMEM)


def call(body, outs, args, specs, scratch=(), flops=1000000):
    moved = sum(a.size for a in args) * 4 + sum(o.size for o in outs) * 4
    return pl.pallas_call(
        body,
        out_shape=tuple(outs),
        in_specs=list(specs),
        out_specs=tuple(VMEM for _ in outs),
        scratch_shapes=list(scratch),
        compiler_params=pltpu.CompilerParams(vmem_limit_bytes=8 * 1024 * 1024),
        cost_estimate=pl.CostEstimate(flops=flops, bytes_accessed=moved, transcendentals=0),
    )(*args)


def f32(*shape):
    return jax.ShapeDtypeStruct(shape, jnp.float32)


def sublane(shape):
    return lax.broadcasted_iota(jnp.int32, shape, 0)


def turn(v, steps, axis):
    return pltpu.roll(v, steps % v.shape[axis], axis)


def cubic_weights(position):
    squared = position * position
    cubed = squared * position
    return (
        (2.0 * squared - cubed - position) * 0.5,
        (3.0 * cubed - 5.0 * squared + 2.0) * 0.5,
        (4.0 * squared - 3.0 * cubed + position) * 0.5,
        (cubed - squared) * 0.5,
    )


def columns_body(cy, vel, labels, rates, left, right):
    for out, y0 in ((left, 0), (right, cy - 2)):
        for k in range(2):
            cell = jnp.where(labels[:, y0 + k, :] == 1, rates[1], rates[0])
            out[:, FIELDS * k, :] = cell
            for f in range(3):
                out[:, FIELDS * k + f + 1, :] = vel[f, :, y0 + k, :]


def prep_body(cx, cy, level, vel, labels, rates, state, rate):
    def row(x, _):
        state[x, pl.ds(0, cy, stride=FIELDS), :] = level[x]
        for f in range(3):
            state[x, pl.ds(f + 1, cy, stride=FIELDS), :] = vel[f, x]
        cell = jnp.where(labels[x] == 1, rates[1], rates[0])
        for f in range(FIELDS):
            rate[x, pl.ds(f, cy, stride=FIELDS), :] = cell
        return 0

    lax.fori_loop(0, cx, row, 0)


def edge_rows_body(cx, pairs, mix, *refs):
    sources, (top, bot) = refs[:-2], refs[-2:]
    state, ym, yp = sources[0], sources[-2], sources[-1]
    wide = pairs + 2
    for out, rows in ((top, (0, 1)), (bot, (cx - 2, cx - 1))):
        for k, x in enumerate(rows):
            out[k * wide] = ym[x]
            out[k * wide + pairs + 1] = yp[x]
            for q in range(pairs):
                v = state[x * pairs + q]
                if mix:
                    v = jnp.where(sublane(v.shape) % FIELDS == 0, sources[1][x * pairs + q], v)
                out[k * wide + q + 1] = v


def weights_body(cx, cy, step, fraction, out):
    def row(x, _):
        for d in range(3):
            for k, w in enumerate(cubic_weights(fraction[step, d, x])):
                for f in range(FIELDS):
                    out[4 * d + k, x, pl.ds(f, cy, stride=FIELDS), :] = w
        return 0

    lax.fori_loop(0, cx, row, 0)


def fill_rows(pad, at, rows, pairs, own, ym, yp, change):
    wide = pairs + 2
    for n, x in enumerate(rows):
        pad[(at + n) * wide] = change(ym[x])
        pad[(at + n) * wide + pairs + 1] = change(yp[x])
        for q in range(pairs):
            pad[(at + n) * wide + q + 1] = own[x * pairs + q]


def spread_rate(v):
    v = jnp.where(sublane(v.shape) % FIELDS == 0, v, 0.0)
    v = v + turn(v, 1, 0)
    return v + turn(v, 2, 0)


def same(v):
    return v


def coef_row(pad, base, ax, yu, yd, zu, zd, c0, r, wide):
    shape = pad.shape[1:]
    half = sublane(shape) < FIELDS
    scale = jnp.where(sublane(shape) % FIELDS == 0, 0.0, 0.5)
    flipped = [turn(pad[base + j], FIELDS, 0) for j in range(wide)]
    for j in range(wide):
        own = pad[base + j]
        up = jnp.where(half, flipped[j], flipped[min(j + 1, wide - 1)])
        down = jnp.where(half, flipped[max(j - 1, 0)], flipped[j])
        at = r * wide + j
        cyu = (own + up) * scale
        cyd = (own + down) * scale
        czu = (own + turn(own, -1, 1)) * scale
        czd = (own + turn(own, 1, 1)) * scale
        yu[at] = cyu
        yd[at] = cyd
        zu[at] = czu
        zd[at] = czd
        c0[at] = 1.0 - (ax[at] + ax[at + wide] + cyu + cyd + czu + czd)


def face_row(pad, base, ax, r, wide):
    scale = jnp.where(sublane(pad.shape[1:]) % FIELDS == 0, 0.0, 0.5)
    for j in range(wide):
        ax[r * wide + j] = (pad[base - wide + j] + pad[base + j]) * scale


def coef_inner_body(cx, pairs, rate, ym, yp, ax, yu, yd, zu, zd, c0, pad):
    wide = pairs + 2

    def copy(x, _):
        pad[x * wide] = spread_rate(ym[x])
        pad[x * wide + pairs + 1] = spread_rate(yp[x])
        for q in range(pairs):
            pad[x * wide + q + 1] = rate[x * pairs + q]
        return 0

    lax.fori_loop(0, cx, copy, 0)

    def faces(r, _):
        face_row(pad, (r - 1) * wide, ax, r, wide)
        return 0

    lax.fori_loop(2, cx + 1, faces, 0)

    def row(r, _):
        coef_row(pad, (r - 1) * wide, ax, yu, yd, zu, zd, c0, r, wide)
        return 0

    lax.fori_loop(2, cx, row, 0)


def coef_outer_body(cx, pairs, rate, xm, xp, ym, yp, ax_inner, *refs):
    outs, pad = refs[:6], refs[6]
    ax, yu, yd, zu, zd, c0 = outs
    wide = pairs + 2
    outer_pad(pad, cx, pairs, rate, xm, xp, ym, yp, spread_rate)
    for half_at, faces in ((0, (0, 1)), (1, (4, 5))):
        base = 4 * half_at * wide
        for n in faces:
            face_row(pad, base + (1 + n - (3 if half_at else 0)) * wide, ax, n, wide)
    for j in range(wide):
        ax[2 * wide + j] = ax_inner[2 * wide + j]
        ax[3 * wide + j] = ax_inner[cx * wide + j]
    for n in range(2):
        coef_row(pad, (1 + n) * wide, ax, yu, yd, zu, zd, c0, n, wide)
    shifted = ax.at[pl.ds(wide, 5 * wide)]
    for n in range(2):
        coef_row(pad, (5 + n) * wide, shifted, yu, yd, zu, zd, c0, 2 + n, wide)


def outer_pad(pad, cx, pairs, own, xm, xp, ym, yp, change):
    wide = pairs + 2
    for k in range(2 * wide):
        pad[k] = change(xm[k])
        pad[6 * wide + k] = change(xp[k])
    fill_rows(pad, 2, (0, 1), pairs, own, ym, yp, change)
    fill_rows(pad, 4, (cx - 2, cx - 1), pairs, own, ym, yp, change)


def sweep_row(src, base, lo, hi, coefs, at, half):
    ax, yu, yd, zu, zd, c0, wide = coefs
    own = {j: src[base + j] for j in range(max(lo - 1, 0), min(hi + 1, wide))}
    flipped = {j: turn(v, FIELDS, 0) for j, v in own.items()}
    for j in range(lo, hi):
        up = jnp.where(half, flipped[j], flipped.get(j + 1, flipped[j]))
        down = jnp.where(half, flipped.get(j - 1, flipped[j]), flipped[j])
        v = own[j]
        k = at + j
        total = c0[k] * v + ax[k] * src[base - wide + j] + ax[k + wide] * src[base + wide + j]
        total = total + yu[k] * up + yd[k] * down
        total = total + zu[k] * turn(v, -1, 1) + zd[k] * turn(v, 1, 1)
        yield j, total


def lifts(shape):
    return jnp.where(sublane(shape) % FIELDS == 0, BUOYANCY, 0.0)


def diffuse_inner(cx, pairs, own, ym, yp, coefs, pad, mid, g):
    wide = pairs + 2
    half = sublane(pad.shape[1:]) < FIELDS
    lift = lifts(pad.shape[1:])
    coefs = tuple(coefs) + (wide,)

    def copy(x, _):
        pad[x * wide] = ym[x]
        pad[x * wide + pairs + 1] = yp[x]
        for q in range(pairs):
            pad[x * wide + q + 1] = own[x * pairs + q]
        return 0

    lax.fori_loop(0, cx, copy, 0)

    def first(x, _):
        for j, v in sweep_row(pad, x * wide, 0, wide, coefs, (x + 1) * wide, half):
            mid[x * wide + j] = v
        return 0

    lax.fori_loop(1, cx - 1, first, 0)

    def second(x, _):
        for j, v in sweep_row(mid, x * wide, 1, pairs + 1, coefs, (x + 1) * wide, half):
            g[x * pairs + j - 1] = v + lift * turn(v, -3, 0)
        return 0

    lax.fori_loop(2, cx - 2, second, 0)


def diffuse_outer(cx, pairs, own, xm, xp, ym, yp, coefs, outer, mid_inner, g_inner, pad, mid, g):
    wide = pairs + 2
    shape = pad.shape[1:]
    half = sublane(shape) < FIELDS
    lift = lifts(shape)
    zero = jnp.zeros(shape, jnp.float32)
    for k in range(3 * pairs):
        g[k] = zero
        g[(cx + 3) * pairs + k] = zero

    def copy(x, _):
        for q in range(pairs):
            g[(x + 3) * pairs + q] = g_inner[x * pairs + q]
        return 0

    lax.fori_loop(2, cx - 2, copy, 0)
    outer_pad(pad, cx, pairs, own, xm, xp, ym, yp, same)
    for j in range(wide):
        mid[2 * wide + j] = mid_inner[wide + j]
        mid[3 * wide + j] = mid_inner[2 * wide + j]
        mid[4 * wide + j] = mid_inner[(cx - 3) * wide + j]
        mid[5 * wide + j] = mid_inner[(cx - 2) * wide + j]
    low = tuple(outer) + (wide,)
    high = (outer[0].at[pl.ds(wide, 5 * wide)],) + tuple(outer[1:]) + (wide,)
    for n, (src, to, table) in enumerate(((1, 0, low), (2, 1, low), (5, 6, high), (6, 7, high))):
        lo, hi = (1, pairs + 1) if n in (0, 3) else (0, wide)
        for j, v in sweep_row(pad, src * wide, lo, hi, table, n * wide, half):
            mid[to * wide + j] = v
    inner = tuple(coefs) + (wide,)
    for src, x, table, at in (
        (1, 0, low, 1),
        (2, 1, inner, 2),
        (5, cx - 2, inner, cx - 1),
        (6, cx - 1, high, 2),
    ):
        for j, v in sweep_row(mid, src * wide, 1, pairs + 1, table, at * wide, half):
            g[(x + 3) * pairs + j - 1] = v + lift * turn(v, -3, 0)


def patch_row(g, w, cx, pairs, at, lead):
    shape = g.shape[1:]
    half = sublane(shape) < FIELDS
    rows = [(at + 1 - a + lead, jnp.clip(at + 1 - a, 0, cx - 1)) for a in range(4)]
    out = []
    zero = jnp.zeros(shape, jnp.float32)

    def finish(acc0, acc1, acc1_before):
        flipped = turn(acc1, FIELDS, 0) if acc1 is not None else zero
        flipped_before = turn(acc1_before, FIELDS, 0) if acc1_before is not None else zero
        value = jnp.where(half, flipped_before, flipped)
        return value if acc0 is None else acc0 + value

    p1 = p2 = p3 = p3_old = acc1_old = None
    for q in range(pairs):
        sums = [[None] * 4 for _ in range(4)]
        for a in range(4):
            padded, row = rows[a]
            k = pl.ds(SUB * q, SUB)
            h = g[padded * pairs + q] * w[a, row, k, :]
            wy = [w[4 + b, row, k, :] for b in range(4)]
            for c in range(4):
                hc = h * w[8 + c, row, k, :]
                for b in range(4):
                    t = hc * wy[b]
                    sums[b][c] = t if sums[b][c] is None else sums[b][c] + t
        p = []
        for b in range(4):
            s = sums[b]
            p.append((turn(s[0], -1, 1) + s[1]) + (turn(s[2], 1, 1) + turn(s[3], 2, 1)))
        acc1 = p[0] if p2 is None else p2 + p[0]
        acc0 = p1 if p3_old is None else p1 + p3_old
        out.append(finish(acc0, acc1, acc1_old))
        p3_old = p3
        p1, p2, p3 = p[1], p[2], p[3]
        acc1_old = acc1
    out.append(finish(p1 if p3_old is None else p1 + p3_old, p2, acc1_old))
    out.append(finish(p3, None, p2))
    return out


def spread(cx, pairs, rows_of, count, lead, g, w, shift_x, shift_y, step, own, right, left, far):
    shape = g.shape[1:]
    move_x = shift_x[0, 0, step]
    move_y = shift_y[0, 0, step]
    here = jnp.where(move_y == 0, 1.0, 0.0)
    up = jnp.where(move_y == 1, 1.0, 0.0)
    down = jnp.where(move_y == -1, 1.0, 0.0)

    def row(i, _):
        out = patch_row(g, w, cx, pairs, rows_of(i), lead)
        low, high = out[0], out[pairs + 1]
        for q in range(pairs):
            v = out[q + 1]
            o, r, l = v * here, v * up, v * down
            if q == 0:
                o = o + high * down
                r = r + high * here
            if q == pairs - 1:
                o = o + low * up
                l = l + low * here
            own[i * pairs + q] = o
            right[i * pairs + q] = r
            left[i * pairs + q] = l
        far[i] = high * up + low * down
        return 0

    lax.fori_loop(0, count, row, 0)
    mx = jnp.full(shape, move_x.astype(jnp.float32))
    right[count * pairs] = mx
    left[count * pairs] = mx
    far[count] = mx
    far[count + 1] = jnp.full(shape, move_y.astype(jnp.float32))


def inner_body(cx, pairs, step, rows_of, count, *refs):
    own, ym, yp, coefs, w, sx, sy = refs[0], refs[1], refs[2], refs[3:9], refs[9], refs[10], refs[11]
    o, r, l, far, mid, g, pad = refs[12:]
    diffuse_inner(cx, pairs, own, ym, yp, coefs, pad, mid, g)
    spread(cx, pairs, rows_of, count, 0, g, w, sx, sy, step, o, r, l, far)


def outer_body(cx, pairs, step, rows_of, count, *refs):
    own, halos, coefs, outer = refs[0], refs[1:5], refs[5:11], refs[11:17]
    mid_inner, g_inner, w, sx, sy = refs[17:22]
    o, r, l, far, pad, mid, g = refs[22:]
    diffuse_outer(cx, pairs, own, *halos, coefs, outer, mid_inner, g_inner, pad, mid, g)
    spread(cx, pairs, rows_of, count, 3, g, w, sx, sy, step, o, r, l, far)


def gather_body(pairs, step, main, rims, *refs):
    own, right, left, far_low, far_high, sx = refs[:6]
    outs = refs[6:11]
    shape = own.shape[1:]
    count = own.shape[0] // pairs
    skip = 3 if rims else 0
    mine = jnp.full(shape, sx[0, 0, step].astype(jnp.float32))
    moves = (mine, right[count * pairs], left[count * pairs])
    far_moves = (far_low[count], far_high[count])
    far_gates = (far_low[count + 1] == 1.0, far_high[count + 1] == -1.0)
    side = 2 * lax.rem(lax.axis_index("gx"), 2) - 1
    targets = (side, -side, 2 * side, -2 * side, jnp.int32(0))

    def hit(move, t):
        return jnp.where(move == t.astype(jnp.float32), 1.0, 0.0)

    def total(masks, fars, i, q):
        v = masks[0] * own[i * pairs + q] + masks[1] * right[i * pairs + q] + masks[2] * left[i * pairs + q]
        if q == 0:
            v = v + fars[0] * far_low[i]
        if q == pairs - 1:
            v = v + fars[1] * far_high[i]
        return v

    def masks_of(t):
        masks = [hit(m, t) for m in moves]
        fars = [jnp.where(gate, hit(m, t), 0.0) for gate, m in zip(far_gates, far_moves)]
        return masks, fars

    for out, t in zip(outs, targets):
        masks, fars = masks_of(t)

        def row(i, _, out=out, masks=masks, fars=fars):
            for q in range(pairs):
                out[i * pairs + q] = total(masks, fars, i + skip, q)
            return 0

        lax.fori_loop(0, main, row, 0)
        if rims:
            for source, row_at, step_to in ((0, 0, -1), (1, 1, -1), (2, main - 1, 1)):
                masks, fars = masks_of(t + step_to)
                for q in range(pairs):
                    out[row_at * pairs + q] = out[row_at * pairs + q] + total(masks, fars, source, q)
    if rims:
        high, low = refs[11:]
        masks, fars = masks_of(jnp.int32(2))
        for k in range(2):
            for q in range(pairs):
                high[k * pairs + q] = total(masks, fars, k, q)
        masks, fars = masks_of(jnp.int32(-2))
        for q in range(pairs):
            low[q] = total(masks, fars, 2, q)


def add_body(a, b, out):
    group = 8 if out.shape[0] % 8 == 0 else 1

    def rows(i, _):
        for j in range(group):
            out[i * group + j] = a[i * group + j] + b[i * group + j]
        return 0

    lax.fori_loop(0, out.shape[0] // group, rows, 0)


def merge(cx, pairs, chunks, parts, put):
    for runs, (t0, e0, f, d) in zip(chunks, (parts[0:4], parts[4:8])):
        for local, base, rows in runs:

            def row(i, _, t0=t0, e0=e0, f=f, d=d, local=local, base=base):
                for q in range(pairs):
                    at = (i + local) * pairs + q
                    put(i + base, q, (t0[at] + e0[at]) + (f[at] + d[at]), False)
                return 0

            lax.fori_loop(0, rows, row, 0)
    high, low = parts[8:10]
    for q in range(pairs):
        for k in range(2):
            put(k, q, high[k * pairs + q], True)
        put(cx - 1, q, low[q], True)


def merge_body(cx, pairs, chunks, *refs):
    parts = refs[:10]
    out, left, right = refs[10:]

    def put(x, q, v, add):
        at = x * pairs + q
        out[at] = out[at] + v if add else v

    merge(cx, pairs, chunks, parts, put)
    for x in range(cx):
        left[x] = out[x * pairs]
        right[x] = out[x * pairs + pairs - 1]


def finish_body(cx, cy, pairs, chunks, *refs):
    parts = refs[:10]
    level, vel, out = refs[10:]

    def put(x, q, v, add):
        at = pl.ds(SUB * q, SUB)
        out[x, at, :] = out[x, at, :] + v if add else v

    merge(cx, pairs, chunks, parts, put)

    def row(x, _):
        level[x] = out[x, pl.ds(0, cy, stride=FIELDS), :]
        for f in range(3):
            vel[f, x] = out[x, pl.ds(f + 1, cy, stride=FIELDS), :]
        return 0

    lax.fori_loop(0, cx, row, 0)


def moved(value, axis, steps):
    count = lax.axis_size(axis)
    return lax.ppermute(value, axis, [(i, (i + steps) % count) for i in range(count)])


def swapped(value):
    return lax.ppermute(value, "gx", [(i, i ^ 1) for i in range(lax.axis_size("gx"))])


def crossed(value, sign):
    count = lax.axis_size("gx")
    return lax.ppermute(
        value, "gx", [(i, (i + (2 if i % 2 else -2) * sign) % count) for i in range(count)]
    )


def on_device(level, vel, fraction, shift_x, shift_y, labels, rates):
    cx, cy, cz = level.shape
    pairs = cy // 2
    wide = pairs + 2
    ny = lax.axis_size("gy")

    def plane(n):
        return f32(n, SUB, cz)

    def scratch(n):
        return pltpu.VMEM((n, SUB, cz), jnp.float32)

    left, right = call(
        functools.partial(columns_body, cy),
        [plane(cx)] * 2,
        (vel, labels, rates),
        [VMEM, VMEM, SMEM],
    )
    state, rate = call(
        functools.partial(prep_body, cx, cy),
        [f32(cx, FIELDS * cy, cz)] * 2,
        (level, vel, labels, rates),
        [VMEM, VMEM, VMEM, SMEM],
    )
    state = state.reshape(cx * pairs, SUB, cz)
    rate = rate.reshape(cx * pairs, SUB, cz)
    weights = [
        call(
            functools.partial(weights_body, cx, cy, s),
            [f32(12, cx, FIELDS * cy, cz)],
            (fraction,),
            [VMEM],
        )[0]
        for s in range(STEPS)
    ]
    coefs = outer = None

    inner = 4
    count_a = cx - 2 * inner + 1
    main = (count_a, cx - count_a)
    chunk_runs = (
        ((0, inner, count_a),),
        ((0, 0, inner), (inner, inner + count_a, cx - inner - count_a)),
    )

    def rows_a(i):
        return i + inner

    def rows_b(i):
        k = i - 3
        body = jnp.where(k < inner, k, k + count_a)
        return jnp.where(i < 2, cx + i, jnp.where(i < 3, -1, body))

    counts = (main[0], main[1] + 3)

    def outs(n):
        return [plane(n * pairs), plane(n * pairs + 1), plane(n * pairs + 1), plane(n + 2)]

    for step in range(STEPS - 1, -1, -1):
        first = coefs is None
        ym = moved(right, "gy", 1)
        yp = moved(left, "gy", -1)
        states = (state, rate) if first else (state,)
        top, bot = call(
            functools.partial(edge_rows_body, cx, pairs, first),
            [plane(2 * wide)] * 2,
            (*states, ym, yp),
            [VMEM] * (len(states) + 2),
        )
        xm = moved(bot, "gx", 1)
        xp = moved(top, "gx", -1)
        if first:
            coefs = call(
                functools.partial(coef_inner_body, cx, pairs),
                [plane((cx + 3) * wide)] + [plane((cx + 2) * wide)] * 5,
                (rate, ym, yp),
                [VMEM] * 3,
                [scratch(cx * wide)],
            )
        *sent_a, mid, g = call(
            functools.partial(inner_body, cx, pairs, step, rows_a, counts[0]),
            outs(counts[0]) + [plane(cx * wide), plane(cx * pairs)],
            (state, ym, yp, *coefs, weights[step], shift_x, shift_y),
            [VMEM] * 10 + [SMEM] * 2,
            [scratch(cx * wide)],
            flops=20000000,
        )
        if first:
            outer = call(
                functools.partial(coef_outer_body, cx, pairs),
                [plane(6 * wide)] + [plane(4 * wide)] * 5,
                (rate, xm, xp, ym, yp, coefs[0]),
                [VMEM] * 6,
                [scratch(8 * wide)],
            )
        sent_b = call(
            functools.partial(outer_body, cx, pairs, step, rows_b, counts[1]),
            outs(counts[1]),
            (state, xm, xp, ym, yp, *coefs, *outer, mid, g, weights[step], shift_x, shift_y),
            [VMEM] * 20 + [SMEM] * 2,
            [scratch(8 * wide), scratch(8 * wide), scratch((cx + 6) * pairs)],
            flops=10000000,
        )
        chunks = []
        for n, (own, right, left, far) in enumerate((sent_a, sent_b)):
            if n:
                own, _ = lax.optimization_barrier((own, chunks[0]))
            right = moved(right, "gy", 1)
            left = moved(left, "gy", -1)
            far_low = moved(far, "gy", 2)
            far_high = far_low if ny == 4 else moved(far, "gy", -2)
            e1, e0, f, k, t0, *rims = call(
                functools.partial(gather_body, pairs, step, main[n], n == 1),
                [plane(main[n] * pairs)] * 5 + ([plane(2 * pairs), plane(pairs)] if n else []),
                (own, right, left, far_low, far_high, shift_x),
                [VMEM] * 5 + [SMEM],
                flops=3000000,
            )
            e1 = swapped(e1)
            f = crossed(f, 1)
            e0 = swapped(e0)
            (d,) = call(add_body, [plane(main[n] * pairs)], (k, e1), [VMEM] * 2)
            d = crossed(d, -1)
            chunks += [t0, e0, f, d]
        high, low = rims
        high = moved(high, "gx", 3)
        low = moved(low, "gx", -3)
        chunks += [high, low]
        if step:
            state, left, right = call(
                functools.partial(merge_body, cx, pairs, chunk_runs),
                [plane(cx * pairs)] + [plane(cx)] * 2,
                chunks,
                [VMEM] * 10,
            )
        else:
            return call(
                functools.partial(finish_body, cx, cy, pairs, chunk_runs),
                [f32(cx, cy, cz), f32(3, cx, cy, cz)],
                chunks,
                [VMEM] * 10,
                [pltpu.VMEM((cx, FIELDS * cy, cz), jnp.float32)],
            )


def solution(mesh):
    in_specs = (
        P("gx", "gy", None),
        P(None, "gx", "gy", None),
        P(None, None, "gx", "gy", None),
        P("gx", "gy", None),
        P("gx", "gy", None),
        P("gx", "gy", None),
        P(),
    )
    out_specs = (P("gx", "gy", None), P(None, "gx", "gy", None))
    return jax.shard_map(
        on_device, mesh=mesh, in_specs=in_specs, out_specs=out_specs, check_vma=False
    )
```

time: 164 us -> 157 us (0.957)
  waiting for transfers between devices: 71.7 us -> 66.2 us
  starting transfers between devices: 58.9 us -> 55.5 us
  local copies, waits for them, and re-layouts: 4.59 us -> 7.15 us
    ppermute x8, waiting for transfers between devices: 23.1 us -> 12.8 us  [crossed(): lax.ppermute(value, 'gx', [(i, (i + (2 if i % 2 else -2) * sign) % count)...]
    ppermute x8, waiting for transfers between devices: 17 us -> 25.4 us  [swapped(): lax.ppermute(value, 'gx', [(i, i ^ 1) for i in range(lax.axis_size('gx'))])]
    ppermute x8, starting transfers between devices: 15.9 us -> 11.6 us  [crossed(): lax.ppermute(value, 'gx', [(i, (i + (2 if i % 2 else -2) * sign) % count)...]
    ppermute x24, waiting for transfers between devices: 31.6 us -> 28 us  [moved(): lax.ppermute(value, axis, [(i, (i + steps) % count) for i in range(count)])]
    ppermute x8, starting transfers between devices: 8.58 us -> 12.1 us  [swapped(): lax.ppermute(value, 'gx', [(i, i ^ 1) for i in range(lax.axis_size('gx'))])]
    ppermute x24, starting transfers between devices: 34.5 us -> 31.8 us  [moved(): lax.ppermute(value, axis, [(i, (i + steps) % count) for i in range(count)])]
    unnamed x16 -> x22, local copies, waits for them, and re-layouts: 4.59 us -> 7.15 us
    pallas_call x20 -> x22, Pallas kernels: 28 us -> 27.2 us  [call(): pl.pallas_call(body, out_shape=tuple(outs), in_specs=list(specs), out_spe...]
  transfers between devices with their start and end apart: 40 -> 40, of which waited for: 22 -> 14; matrix products, arithmetic and copies ran while one was open for 0% -> 0% of each run, Pallas kernels for 5% -> 16%
where the time goes in v3:
time: 157 us
  waiting for transfers between devices  66.2 us (42%)
  starting transfers between devices  55.5 us (35%)
  Pallas kernels  27.2 us (17%)
  local copies, waits for them, and re-layouts  7.15 us (5%)
    ppermute x24, starting transfers between devices, moved(): lax.ppermute(value, axis, [(i, (i + steps) % count) for i in range(count)])  31.8 us
    ppermute x24, waiting for transfers between devices, moved(): lax.ppermute(value, axis, [(i, (i + steps) % count) for i in range(count)])  28 us
    pallas_call x22, Pallas kernels, call(): pl.pallas_call(body, out_shape=tuple(outs), in_specs=list(specs), out_spe...  27.2 us
    ppermute x8, waiting for transfers between devices, swapped(): lax.ppermute(value, 'gx', [(i, i ^ 1) for i in range(lax.axis_size('gx'))])  25.4 us
    ppermute x8, waiting for transfers between devices, crossed(): lax.ppermute(value, 'gx', [(i, (i + (2 if i % 2 else -2) * sign) % count)...  12.8 us
    ppermute x8, starting transfers between devices, swapped(): lax.ppermute(value, 'gx', [(i, i ^ 1) for i in range(lax.axis_size('gx'))])  12.1 us
    ppermute x8, starting transfers between devices, crossed(): lax.ppermute(value, 'gx', [(i, (i + (2 if i % 2 else -2) * sign) % count)...  11.6 us
    unnamed x22, local copies, waits for them, and re-layouts  7.15 us
  transfers between devices with their start and end apart: 40, of which 14 were waited for; matrix products, arithmetic and copies ran while one was open for 0% of the time, Pallas kernels for 16%

profile of v3, /device:TPU:0, one launch (start us, length us, event | category | flops | bytes accessed | tf_op | source)
XLA Modules:
  0.0 156.9 jit_solution(10127888086223395666)
XLA Ops:
  0.6 1.0 copy-done.2
  1.6 0.9 copy-done.4
  4.4 2.0 %collective-permute-start.1 = (f32[16,8,128]{2,1,0:T(8,128)S(1)}, f32[16,8,128]{2,1,0:T(8,128)S(1)}, u32[]{:S(2)}, u32[]{:S(2)}) collective-permute-start(f32[16,8,128]{2,1,0:T(8,128)S(1)} %get-tuple-element.73), channel_id=1, source_target_pairs={{0,3},{1,0},{2,1},{3,2},{4,7},{5,4},{6,5},{7,6},{8,11},{9,8},{10,9... | collective-permute-start | bytes 196616 | tf_op jit(solution)/shard_map/ppermute | solution.py:498
  6.4 1.0 copy-done.3
  10.5 5.4 %collective-permute-start.10 = (f32[20,8,128]{2,1,0:T(8,128)S(1)}, f32[20,8,128]{2,1,0:T(8,128)S(1)}, u32[]{:S(2)}, u32[]{:S(2)}) collective-permute-start(f32[20,8,128]{2,1,0:T(8,128)S(1)} %get-tuple-element.91), channel_id=1, source_target_pairs={{0,28},{4,0},{8,4},{12,8},{16,12},{20,16},{24,20},{28,24},{1,29},{... | collective-permute-start | bytes 245768 | tf_op jit(solution)/shard_map/ppermute | solution.py:498
  15.9 1.1 copy-done
  17.6 1.6 %shard_map.88 = (f32[190,8,128]{2,1,0:T(8,128)S(1)}, f32[180,8,128]{2,1,0:T(8,128)S(1)}, f32[180,8,128]{2,1,0:T(8,128)S(1)}, f32[180,8,128]{2,1,0:T(8,128)S(1)},...) custom-call(f32[128,8,128]{2,1,0:T(8,128)S(1)} %bitcast.6, ...), custom_call_target="tpu_custom_call" | custom-call | flops 1000000 | bytes 5120000 | tf_op jit(solution)/shard_map/pallas_call | solution.py:21
  19.2 5.3 %shard_map.90 = (f32[72,8,128]{2,1,0:T(8,128)S(1)}, f32[73,8,128]{2,1,0:T(8,128)S(1)}, f32[73,8,128]{2,1,0:T(8,128)S(1)}, f32[11,8,128]{2,1,0:T(8,128)S(1)}, f32...) custom-call(f32[128,8,128]{2,1,0:T(8,128)S(1)} %bitcast.3, ...), custom_call_target="tpu_custom_call" | custom-call | flops 20000000 | bytes 13529104 | tf_op jit(solution)/shard_map/pallas_call | solution.py:21
  24.6 1.7 %collective-permute-start.3 = (f32[73,8,128]{2,1,0:T(8,128)S(1)}, f32[73,8,128]{2,1,0:T(8,128)S(1)}, u32[]{:S(2)}, u32[]{:S(2)}) collective-permute-start(f32[73,8,128]{2,1,0:T(8,128)S(1)} %get-tuple-element.83), channel_id=1, source_target_pairs={{0,3},{1,0},{2,1},{3,2},{4,7},{5,4},{6,5},{7,6},{8,11},{9,8},{10,9... | collective-permute-start | bytes 897032 | tf_op jit(solution)/shard_map/ppermute | solution.py:498
  26.5 3.3 %shard_map.95 = (f32[80,8,128]{2,1,0:T(8,128)S(1)}, f32[81,8,128]{2,1,0:T(8,128)S(1)}, f32[81,8,128]{2,1,0:T(8,128)S(1)}, f32[12,8,128]{2,1,0:T(8,128)S(1)}) custom-call(f32[128,8,128]{2,1,0:T(8,128)S(1)} %bitcast.4, f32[20,8,128]{2,1,0:T(8,128)S(1)} %collective-permute-done.9.xm.refs_1_, f32[20,8,128]{2,1,0:T(8,128)S(1)} %collective-permute-done.10.xp.refs_2_, ...), custom_call_target="tpu_custom_call" | custom-call | flops 10000000 | bytes 14860304 | tf_op jit(solution)/shard_map/pallas_call | solution.py:21
  29.9 1.7 %collective-permute-start.12 = (f32[81,8,128]{2,1,0:T(8,128)S(1)}, f32[81,8,128]{2,1,0:T(8,128)S(1)}, u32[]{:S(2)}, u32[]{:S(2)}) collective-permute-start(f32[81,8,128]{2,1,0:T(8,128)S(1)} %get-tuple-element.103), channel_id=1, source_target_pairs={{0,3},{1,0},{2,1},{3,2},{4,7},{5,4},{6,5},{7,6},{8,11},{9,8},{10,9... | collective-permute-start | bytes 995336 | tf_op jit(solution)/shard_map/ppermute | solution.py:498
  31.6 1.5 collective-permute-start.4
  33.1 8.9 %collective-permute-done.4.refs_3_.refs_4_ = f32[11,8,128]{2,1,0:T(8,128)S(1)} collective-permute-done((f32[11,8,128]{2,1,0:T(8,128)S(1)}, f32[11,8,128]{2,1,0:T(8,128)S(1)}, u32[]{:S(2)}, u32[]{:S(2)}) %collective-permute-start.4) | collective-permute-done | bytes 45088 | tf_op jit(solution)/shard_map/ppermute | solution.py:498
  42.0 1.1 shard_map.91
  43.2 1.6 collective-permute-start.13
  44.7 1.9 %collective-permute-start.5 = (f32[72,8,128]{2,1,0:T(8,128)S(1)}, f32[72,8,128]{2,1,0:T(8,128)S(1)}, u32[]{:S(2)}, u32[]{:S(2)}) collective-permute-start(f32[72,8,128]{2,1,0:T(8,128)S(1)} %get-tuple-element.86), channel_id=1, source_target_pairs={{0,4},{4,0},{8,12},{12,8},{16,20},{20,16},{24,28},{28,24},{1,5},{5... | collective-permute-start | bytes 884744 | tf_op jit(solution)/shard_map/ppermute | solution.py:502
  47.4 1.1 shard_map.96
  48.5 2.0 %collective-permute-start.16 = (f32[56,8,128]{2,1,0:T(8,128)S(1)}, f32[56,8,128]{2,1,0:T(8,128)S(1)}, u32[]{:S(2)}, u32[]{:S(2)}) collective-permute-start(f32[56,8,128]{2,1,0:T(8,128)S(1)} %get-tuple-element.109), channel_id=1, source_target_pairs={{0,4},{4,0},{8,12},{12,8},{16,20},{20,16},{24,28},{28,24},{1,5},{5... | collective-permute-start | bytes 688136 | tf_op jit(solution)/shard_map/ppermute | solution.py:502
  51.4 2.5 %collective-permute-start.6 = (f32[72,8,128]{2,1,0:T(8,128)S(1)}, f32[72,8,128]{2,1,0:T(8,128)S(1)}, u32[]{:S(2)}, u32[]{:S(2)}) collective-permute-start(f32[72,8,128]{2,1,0:T(8,128)S(1)} %get-tuple-element.87), channel_id=1, source_target_pairs={{0,24},{4,12},{8,0},{12,20},{16,8},{20,28},{24,16},{28,4},{1,25},{... | collective-permute-start | bytes 884744 | tf_op jit(solution)/shard_map/ppermute | solution.py:507
  54.0 9.4 %collective-permute-done.16.b = f32[56,8,128]{2,1,0:T(8,128)S(1)} collective-permute-done((f32[56,8,128]{2,1,0:T(8,128)S(1)}, f32[56,8,128]{2,1,0:T(8,128)S(1)}, u32[]{:S(2)}, u32[]{:S(2)}) %collective-permute-start.16) | collective-permute-done | bytes 229408 | tf_op jit(solution)/shard_map/ppermute | solution.py:502
  63.4 1.9 %collective-permute-start.19 = (f32[8,8,128]{2,1,0:T(8,128)S(1)}, f32[8,8,128]{2,1,0:T(8,128)S(1)}, u32[]{:S(2)}, u32[]{:S(2)}) collective-permute-start(f32[8,8,128]{2,1,0:T(8,128)S(1)} %get-tuple-element.111), channel_id=1, source_target_pairs={{0,20},{4,24},{8,28},{12,0},{16,4},{20,8},{24,12},{28,16},{1,21},{... | collective-permute-start | bytes 98312 | tf_op jit(solution)/shard_map/ppermute | solution.py:498
  65.4 2.9 %collective-permute-done.19.refs_9_ = f32[8,8,128]{2,1,0:T(8,128)S(1)} collective-permute-done((f32[8,8,128]{2,1,0:T(8,128)S(1)}, f32[8,8,128]{2,1,0:T(8,128)S(1)}, u32[]{:S(2)}, u32[]{:S(2)}) %collective-permute-start.19) | collective-permute-done | bytes 32800 | tf_op jit(solution)/shard_map/ppermute | solution.py:498
  68.2 2.6 %collective-permute-start.14 = (f32[56,8,128]{2,1,0:T(8,128)S(1)}, f32[56,8,128]{2,1,0:T(8,128)S(1)}, u32[]{:S(2)}, u32[]{:S(2)}) collective-permute-start(f32[56,8,128]{2,1,0:T(8,128)S(1)} %get-tuple-element.106), channel_id=1, source_target_pairs={{0,4},{4,0},{8,12},{12,8},{16,20},{20,16},{24,28},{28,24},{1,5},{5... | collective-permute-start | bytes 688136 | tf_op jit(solution)/shard_map/ppermute | solution.py:502
  70.9 3.6 %collective-permute-start.15 = (f32[56,8,128]{2,1,0:T(8,128)S(1)}, f32[56,8,128]{2,1,0:T(8,128)S(1)}, u32[]{:S(2)}, u32[]{:S(2)}) collective-permute-start(f32[56,8,128]{2,1,0:T(8,128)S(1)} %get-tuple-element.107), channel_id=1, source_target_pairs={{0,24},{4,12},{8,0},{12,20},{16,8},{20,28},{24,16},{28,4},{1,25},{... | collective-permute-start | bytes 688136 | tf_op jit(solution)/shard_map/ppermute | solution.py:507
  74.6 2.1 %collective-permute-done.14.refs_5_ = f32[56,8,128]{2,1,0:T(8,128)S(1)} collective-permute-done((f32[56,8,128]{2,1,0:T(8,128)S(1)}, f32[56,8,128]{2,1,0:T(8,128)S(1)}, u32[]{:S(2)}, u32[]{:S(2)}) %collective-permute-start.14) | collective-permute-done | bytes 229408 | tf_op jit(solution)/shard_map/ppermute | solution.py:502
  76.6 6.4 %collective-permute-done.15.refs_6_ = f32[56,8,128]{2,1,0:T(8,128)S(1)} collective-permute-done((f32[56,8,128]{2,1,0:T(8,128)S(1)}, f32[56,8,128]{2,1,0:T(8,128)S(1)}, u32[]{:S(2)}, u32[]{:S(2)}) %collective-permute-start.15) | collective-permute-done | bytes 229408 | tf_op jit(solution)/shard_map/ppermute | solution.py:507
  83.3 1.7 %collective-permute-start.21 = (f32[16,8,128]{2,1,0:T(8,128)S(1)}, f32[16,8,128]{2,1,0:T(8,128)S(1)}, u32[]{:S(2)}, u32[]{:S(2)}) collective-permute-start(f32[16,8,128]{2,1,0:T(8,128)S(1)} %get-tuple-element.114), channel_id=1, source_target_pairs={{0,3},{1,0},{2,1},{3,2},{4,7},{5,4},{6,5},{7,6},{8,11},{9,8},{10,9... | collective-permute-start | bytes 196616 | tf_op jit(solution)/shard_map/ppermute | solution.py:498
  85.0 1.9 %collective-permute-done.20.refs_1_.refs_3_ = f32[16,8,128]{2,1,0:T(8,128)S(1)} collective-permute-done((f32[16,8,128]{2,1,0:T(8,128)S(1)}, f32[16,8,128]{2,1,0:T(8,128)S(1)}, u32[]{:S(2)}, u32[]{:S(2)}) %collective-permute-start.20) | collective-permute-done | bytes 65568 | tf_op jit(solution)/shard_map/ppermute | solution.py:498
  87.5 4.4 %collective-permute-start.30 = (f32[20,8,128]{2,1,0:T(8,128)S(1)}, f32[20,8,128]{2,1,0:T(8,128)S(1)}, u32[]{:S(2)}, u32[]{:S(2)}) collective-permute-start(f32[20,8,128]{2,1,0:T(8,128)S(1)} %get-tuple-element.125), channel_id=1, source_target_pairs={{0,28},{4,0},{8,4},{12,8},{16,12},{20,16},{24,20},{28,24},{1,29},{... | collective-permute-start | bytes 245768 | tf_op jit(solution)/shard_map/ppermute | solution.py:498
  92.4 5.3 %shard_map.100 = (f32[72,8,128]{2,1,0:T(8,128)S(1)}, f32[73,8,128]{2,1,0:T(8,128)S(1)}, f32[73,8,128]{2,1,0:T(8,128)S(1)}, f32[11,8,128]{2,1,0:T(8,128)S(1)}, f3...) custom-call(f32[128,8,128]{2,1,0:T(8,128)S(1)} %get-tuple-element.112.refs_0_, ...), custom_call_target="tpu_custom_call" | custom-call | flops 20000000 | bytes 13529104 | tf_op jit(solution)/shard_map/pallas_call | solution.py:21
  97.7 1.4 collective-permute-start.22
  99.5 3.3 %shard_map.104 = (f32[80,8,128]{2,1,0:T(8,128)S(1)}, f32[81,8,128]{2,1,0:T(8,128)S(1)}, f32[81,8,128]{2,1,0:T(8,128)S(1)}, f32[12,8,128]{2,1,0:T(8,128)S(1)}) custom-call(f32[128,8,128]{2,1,0:T(8,128)S(1)} %get-tuple-element.112.refs_0_, f32[20,8,128]{2,1,0:T(8,128)S(1)} %collective-permute-done.29.refs_1_, ...), custom_call_target="tpu_custom_call" | custom-call | flops 10000000 | bytes 14860304 | tf_op jit(solution)/shard_map/pallas_call | solution.py:21
  103.4 1.2 collective-permute-start.32
  104.6 2.1 %collective-permute-start.24 = (f32[11,8,128]{2,1,0:T(8,128)S(1)}, f32[11,8,128]{2,1,0:T(8,128)S(1)}, u32[]{:S(2)}, u32[]{:S(2)}) collective-permute-start(f32[11,8,128]{2,1,0:T(8,128)S(1)} %get-tuple-element.118), channel_id=1, source_target_pairs={{0,2},{1,3},{2,0},{3,1},{4,6},{5,7},{6,4},{7,5},{8,10},{9,11},{10,... | collective-permute-start | bytes 135176 | tf_op jit(solution)/shard_map/ppermute | solution.py:498
  106.7 8.5 %collective-permute-done.24.refs_3_.refs_4_ = f32[11,8,128]{2,1,0:T(8,128)S(1)} collective-permute-done((f32[11,8,128]{2,1,0:T(8,128)S(1)}, f32[11,8,128]{2,1,0:T(8,128)S(1)}, u32[]{:S(2)}, u32[]{:S(2)}) %collective-permute-start.24) | collective-permute-done | bytes 45088 | tf_op jit(solution)/shard_map/ppermute | solution.py:498
  115.2 1.1 shard_map.101
  116.4 2.2 %collective-permute-start.33 = (f32[12,8,128]{2,1,0:T(8,128)S(1)}, f32[12,8,128]{2,1,0:T(8,128)S(1)}, u32[]{:S(2)}, u32[]{:S(2)}) collective-permute-start(f32[12,8,128]{2,1,0:T(8,128)S(1)} %get-tuple-element.132), channel_id=1, source_target_pairs={{0,2},{1,3},{2,0},{3,1},{4,6},{5,7},{6,4},{7,5},{8,10},{9,11},{10,... | collective-permute-start | bytes 147464 | tf_op jit(solution)/shard_map/ppermute | solution.py:498
  118.6 1.9 %collective-permute-start.25 = (f32[72,8,128]{2,1,0:T(8,128)S(1)}, f32[72,8,128]{2,1,0:T(8,128)S(1)}, u32[]{:S(2)}, u32[]{:S(2)}) collective-permute-start(f32[72,8,128]{2,1,0:T(8,128)S(1)} %get-tuple-element.120), channel_id=1, source_target_pairs={{0,4},{4,0},{8,12},{12,8},{16,20},{20,16},{24,28},{28,24},{1,5},{5... | collective-permute-start | bytes 884744 | tf_op jit(solution)/shard_map/ppermute | solution.py:502
  120.7 1.2 shard_map.105
  121.8 2.0 %collective-permute-start.36 = (f32[56,8,128]{2,1,0:T(8,128)S(1)}, f32[56,8,128]{2,1,0:T(8,128)S(1)}, u32[]{:S(2)}, u32[]{:S(2)}) collective-permute-start(f32[56,8,128]{2,1,0:T(8,128)S(1)} %get-tuple-element.137), channel_id=1, source_target_pairs={{0,4},{4,0},{8,12},{12,8},{16,20},{20,16},{24,28},{28,24},{1,5},{5... | collective-permute-start | bytes 688136 | tf_op jit(solution)/shard_map/ppermute | solution.py:502
  123.8 3.3 %collective-permute-start.26 = (f32[72,8,128]{2,1,0:T(8,128)S(1)}, f32[72,8,128]{2,1,0:T(8,128)S(1)}, u32[]{:S(2)}, u32[]{:S(2)}) collective-permute-start(f32[72,8,128]{2,1,0:T(8,128)S(1)} %get-tuple-element.121), channel_id=1, source_target_pairs={{0,24},{4,12},{8,0},{12,20},{16,8},{20,28},{24,16},{28,4},{1,25},{... | collective-permute-start | bytes 884744 | tf_op jit(solution)/shard_map/ppermute | solution.py:507
  127.3 10.2 %collective-permute-done.36.b = f32[56,8,128]{2,1,0:T(8,128)S(1)} collective-permute-done((f32[56,8,128]{2,1,0:T(8,128)S(1)}, f32[56,8,128]{2,1,0:T(8,128)S(1)}, u32[]{:S(2)}, u32[]{:S(2)}) %collective-permute-start.36) | collective-permute-done | bytes 229408 | tf_op jit(solution)/shard_map/ppermute | solution.py:502
  137.6 4.8 %collective-permute-done.39.refs_9_ = f32[8,8,128]{2,1,0:T(8,128)S(1)} collective-permute-done((f32[8,8,128]{2,1,0:T(8,128)S(1)}, f32[8,8,128]{2,1,0:T(8,128)S(1)}, u32[]{:S(2)}, u32[]{:S(2)}) %collective-permute-start.39) | collective-permute-done | bytes 32800 | tf_op jit(solution)/shard_map/ppermute | solution.py:498
  142.3 1.4 collective-permute-start.34
  143.8 2.0 %collective-permute-start.37 = (f32[56,8,128]{2,1,0:T(8,128)S(1)}, f32[56,8,128]{2,1,0:T(8,128)S(1)}, u32[]{:S(2)}, u32[]{:S(2)}) collective-permute-start(f32[56,8,128]{2,1,0:T(8,128)S(1)} %shard_map.106), channel_id=1, source_target_pairs={{0,8},{4,28},{8,16},{12,4},{16,24},{20,12},{24,0},{28,20},{1,9},{5... | collective-permute-start | bytes 688136 | tf_op jit(solution)/shard_map/ppermute | solution.py:507
  145.8 3.7 %collective-permute-done.34.refs_5_ = f32[56,8,128]{2,1,0:T(8,128)S(1)} collective-permute-done((f32[56,8,128]{2,1,0:T(8,128)S(1)}, f32[56,8,128]{2,1,0:T(8,128)S(1)}, u32[]{:S(2)}, u32[]{:S(2)}) %collective-permute-start.34) | collective-permute-done | bytes 229408 | tf_op jit(solution)/shard_map/ppermute | solution.py:502
  149.4 6.4 %collective-permute-done.35.refs_6_ = f32[56,8,128]{2,1,0:T(8,128)S(1)} collective-permute-done((f32[56,8,128]{2,1,0:T(8,128)S(1)}, f32[56,8,128]{2,1,0:T(8,128)S(1)}, u32[]{:S(2)}, u32[]{:S(2)}) %collective-permute-start.35) | collective-permute-done | bytes 229408 | tf_op jit(solution)/shard_map/ppermute | solution.py:507
  155.8 1.1 shard_map.107
  (76 shorter events, 10.3 us)
Async XLA Ops:
  0.6 1.0 copy-start.2
  1.6 0.9 copy-start.4
  3.2 16.0 %copy-start.7 = (s32[1,1,2]{2,1,0:T(1,128)S(1)}, s32[1,1,2]{2,1,0:T(1,128)}, u32[]{:S(2)}) copy-start(s32[1,1,2]{2,1,0:T(1,128)} %refs_5_.7) | copy-start | bytes 28
  3.2 16.0 %copy-start.8 = (s32[1,1,2]{2,1,0:T(1,128)S(1)}, s32[1,1,2]{2,1,0:T(1,128)}, u32[]{:S(2)}) copy-start(s32[1,1,2]{2,1,0:T(1,128)} %refs_21_.3) | copy-start | bytes 28
  3.8 6.7 %collective-permute-start = (f32[16,8,128]{2,1,0:T(8,128)S(1)}, f32[16,8,128]{2,1,0:T(8,128)S(1)}, u32[]{:S(2)}, u32[]{:S(2)}) collective-permute-start(f32[16,8,128]{2,1,0:T(8,128)S(1)} %get-tuple-element.72), channel_id=1, source_target_pairs={{0,1},{1,2},{2,3},{3,0},{4,5},{5,6},{6,7},{7,4},{8,9},{9,10},{10,1... | collective-permute-start | bytes 196616 | tf_op jit(solution)/shard_map/ppermute | solution.py:498
  4.4 6.1 %collective-permute-start.1 = (f32[16,8,128]{2,1,0:T(8,128)S(1)}, f32[16,8,128]{2,1,0:T(8,128)S(1)}, u32[]{:S(2)}, u32[]{:S(2)}) collective-permute-start(f32[16,8,128]{2,1,0:T(8,128)S(1)} %get-tuple-element.73), channel_id=1, source_target_pairs={{0,3},{1,0},{2,1},{3,2},{4,7},{5,4},{6,5},{7,6},{8,11},{9,8},{10,9... | collective-permute-start | bytes 196616 | tf_op jit(solution)/shard_map/ppermute | solution.py:498
  6.4 1.0 copy-start.3
  7.4 0.9 copy-start.5
  10.5 15.8 %collective-permute-start.10 = (f32[20,8,128]{2,1,0:T(8,128)S(1)}, f32[20,8,128]{2,1,0:T(8,128)S(1)}, u32[]{:S(2)}, u32[]{:S(2)}) collective-permute-start(f32[20,8,128]{2,1,0:T(8,128)S(1)} %get-tuple-element.91), channel_id=1, source_target_pairs={{0,28},{4,0},{8,4},{12,8},{16,12},{20,16},{24,20},{28,24},{1,29},{... | collective-permute-start | bytes 245768 | tf_op jit(solution)/shard_map/ppermute | solution.py:498
  15.9 10.4 %collective-permute-start.9 = (f32[20,8,128]{2,1,0:T(8,128)S(1)}, f32[20,8,128]{2,1,0:T(8,128)S(1)}, u32[]{:S(2)}, u32[]{:S(2)}) collective-permute-start(f32[20,8,128]{2,1,0:T(8,128)S(1)} %get-tuple-element.90), channel_id=1, source_target_pairs={{0,4},{4,8},{8,12},{12,16},{16,20},{20,24},{24,28},{28,0},{1,5},{5... | collective-permute-start | bytes 245768 | tf_op jit(solution)/shard_map/ppermute | solution.py:498
  15.9 1.1 copy-start
  24.5 17.5 %collective-permute-start.2 = (f32[73,8,128]{2,1,0:T(8,128)S(1)}, f32[73,8,128]{2,1,0:T(8,128)S(1)}, u32[]{:S(2)}, u32[]{:S(2)}) collective-permute-start(f32[73,8,128]{2,1,0:T(8,128)S(1)} %get-tuple-element.82), channel_id=1, source_target_pairs={{0,1},{1,2},{2,3},{3,0},{4,5},{5,6},{6,7},{7,4},{8,9},{9,10},{10,1... | collective-permute-start | bytes 897032 | tf_op jit(solution)/shard_map/ppermute | solution.py:498
  24.6 17.5 %collective-permute-start.3 = (f32[73,8,128]{2,1,0:T(8,128)S(1)}, f32[73,8,128]{2,1,0:T(8,128)S(1)}, u32[]{:S(2)}, u32[]{:S(2)}) collective-permute-start(f32[73,8,128]{2,1,0:T(8,128)S(1)} %get-tuple-element.83), channel_id=1, source_target_pairs={{0,3},{1,0},{2,1},{3,2},{4,7},{5,4},{6,5},{7,6},{8,11},{9,8},{10,9... | collective-permute-start | bytes 897032 | tf_op jit(solution)/shard_map/ppermute | solution.py:498
  29.8 62.1 %copy-start.1 = (f32[2,3,16,16,128]{4,3,2,1,0:T(8,128)S(1)}, f32[2,3,16,16,128]{4,3,2,1,0:T(8,128)}, u32[]{:S(2)}) copy-start(f32[2,3,16,16,128]{4,3,2,1,0:T(8,128)} %fraction.3) | copy-start | bytes 2359300
  29.8 17.6 %collective-permute-start.11 = (f32[81,8,128]{2,1,0:T(8,128)S(1)}, f32[81,8,128]{2,1,0:T(8,128)S(1)}, u32[]{:S(2)}, u32[]{:S(2)}) collective-permute-start(f32[81,8,128]{2,1,0:T(8,128)S(1)} %get-tuple-element.102), channel_id=1, source_target_pairs={{0,1},{1,2},{2,3},{3,0},{4,5},{5,6},{6,7},{7,4},{8,9},{9,10},{10,1... | collective-permute-start | bytes 995336 | tf_op jit(solution)/shard_map/ppermute | solution.py:498
  29.9 17.5 %collective-permute-start.12 = (f32[81,8,128]{2,1,0:T(8,128)S(1)}, f32[81,8,128]{2,1,0:T(8,128)S(1)}, u32[]{:S(2)}, u32[]{:S(2)}) collective-permute-start(f32[81,8,128]{2,1,0:T(8,128)S(1)} %get-tuple-element.103), channel_id=1, source_target_pairs={{0,3},{1,0},{2,1},{3,2},{4,7},{5,4},{6,5},{7,6},{8,11},{9,8},{10,9... | collective-permute-start | bytes 995336 | tf_op jit(solution)/shard_map/ppermute | solution.py:498
  31.6 10.4 %collective-permute-start.4 = (f32[11,8,128]{2,1,0:T(8,128)S(1)}, f32[11,8,128]{2,1,0:T(8,128)S(1)}, u32[]{:S(2)}, u32[]{:S(2)}) collective-permute-start(f32[11,8,128]{2,1,0:T(8,128)S(1)} %get-tuple-element.84), channel_id=1, source_target_pairs={{0,2},{1,3},{2,0},{3,1},{4,6},{5,7},{6,4},{7,5},{8,10},{9,11},{10,... | collective-permute-start | bytes 135176 | tf_op jit(solution)/shard_map/ppermute | solution.py:498
  43.1 10.8 %collective-permute-start.7 = (f32[72,8,128]{2,1,0:T(8,128)S(1)}, f32[72,8,128]{2,1,0:T(8,128)S(1)}, u32[]{:S(2)}, u32[]{:S(2)}) collective-permute-start(f32[72,8,128]{2,1,0:T(8,128)S(1)} %get-tuple-element.89), channel_id=1, source_target_pairs={{0,4},{4,0},{8,12},{12,8},{16,20},{20,16},{24,28},{28,24},{1,5},{5... | collective-permute-start | bytes 884744 | tf_op jit(solution)/shard_map/ppermute | solution.py:502
  43.2 4.2 %collective-permute-start.13 = (f32[12,8,128]{2,1,0:T(8,128)S(1)}, f32[12,8,128]{2,1,0:T(8,128)S(1)}, u32[]{:S(2)}, u32[]{:S(2)}) collective-permute-start(f32[12,8,128]{2,1,0:T(8,128)S(1)} %get-tuple-element.104), channel_id=1, source_target_pairs={{0,2},{1,3},{2,0},{3,1},{4,6},{5,7},{6,4},{7,5},{8,10},{9,11},{10,... | collective-permute-start | bytes 147464 | tf_op jit(solution)/shard_map/ppermute | solution.py:498
  44.7 29.8 %collective-permute-start.5 = (f32[72,8,128]{2,1,0:T(8,128)S(1)}, f32[72,8,128]{2,1,0:T(8,128)S(1)}, u32[]{:S(2)}, u32[]{:S(2)}) collective-permute-start(f32[72,8,128]{2,1,0:T(8,128)S(1)} %get-tuple-element.86), channel_id=1, source_target_pairs={{0,4},{4,0},{8,12},{12,8},{16,20},{20,16},{24,28},{28,24},{1,5},{5... | collective-permute-start | bytes 884744 | tf_op jit(solution)/shard_map/ppermute | solution.py:502
  48.5 15.0 %collective-permute-start.16 = (f32[56,8,128]{2,1,0:T(8,128)S(1)}, f32[56,8,128]{2,1,0:T(8,128)S(1)}, u32[]{:S(2)}, u32[]{:S(2)}) collective-permute-start(f32[56,8,128]{2,1,0:T(8,128)S(1)} %get-tuple-element.109), channel_id=1, source_target_pairs={{0,4},{4,0},{8,12},{12,8},{16,20},{20,16},{24,28},{28,24},{1,5},{5... | collective-permute-start | bytes 688136 | tf_op jit(solution)/shard_map/ppermute | solution.py:502
  50.5 20.4 %collective-permute-start.18 = (f32[16,8,128]{2,1,0:T(8,128)S(1)}, f32[16,8,128]{2,1,0:T(8,128)S(1)}, u32[]{:S(2)}, u32[]{:S(2)}) collective-permute-start(f32[16,8,128]{2,1,0:T(8,128)S(1)} %get-tuple-element.110), channel_id=1, source_target_pairs={{0,12},{4,16},{8,20},{12,24},{16,28},{20,0},{24,4},{28,8},{1,13},{... | collective-permute-start | bytes 196616 | tf_op jit(solution)/shard_map/ppermute | solution.py:498
  51.4 23.2 %collective-permute-start.6 = (f32[72,8,128]{2,1,0:T(8,128)S(1)}, f32[72,8,128]{2,1,0:T(8,128)S(1)}, u32[]{:S(2)}, u32[]{:S(2)}) collective-permute-start(f32[72,8,128]{2,1,0:T(8,128)S(1)} %get-tuple-element.87), channel_id=1, source_target_pairs={{0,24},{4,12},{8,0},{12,20},{16,8},{20,28},{24,16},{28,4},{1,25},{... | collective-permute-start | bytes 884744 | tf_op jit(solution)/shard_map/ppermute | solution.py:507
  53.9 29.1 %collective-permute-start.8 = (f32[72,8,128]{2,1,0:T(8,128)S(1)}, f32[72,8,128]{2,1,0:T(8,128)S(1)}, u32[]{:S(2)}, u32[]{:S(2)}) collective-permute-start(f32[72,8,128]{2,1,0:T(8,128)S(1)} %shard_map.92), channel_id=1, source_target_pairs={{0,8},{4,28},{8,16},{12,4},{16,24},{20,12},{24,0},{28,20},{1,9},{5... | collective-permute-start | bytes 884744 | tf_op jit(solution)/shard_map/ppermute | solution.py:507
  63.4 4.8 %collective-permute-start.19 = (f32[8,8,128]{2,1,0:T(8,128)S(1)}, f32[8,8,128]{2,1,0:T(8,128)S(1)}, u32[]{:S(2)}, u32[]{:S(2)}) collective-permute-start(f32[8,8,128]{2,1,0:T(8,128)S(1)} %get-tuple-element.111), channel_id=1, source_target_pairs={{0,20},{4,24},{8,28},{12,0},{16,4},{20,8},{24,12},{28,16},{1,21},{... | collective-permute-start | bytes 98312 | tf_op jit(solution)/shard_map/ppermute | solution.py:498
  68.2 8.4 %collective-permute-start.14 = (f32[56,8,128]{2,1,0:T(8,128)S(1)}, f32[56,8,128]{2,1,0:T(8,128)S(1)}, u32[]{:S(2)}, u32[]{:S(2)}) collective-permute-start(f32[56,8,128]{2,1,0:T(8,128)S(1)} %get-tuple-element.106), channel_id=1, source_target_pairs={{0,4},{4,0},{8,12},{12,8},{16,20},{20,16},{24,28},{28,24},{1,5},{5... | collective-permute-start | bytes 688136 | tf_op jit(solution)/shard_map/ppermute | solution.py:502
  70.9 12.1 %collective-permute-start.15 = (f32[56,8,128]{2,1,0:T(8,128)S(1)}, f32[56,8,128]{2,1,0:T(8,128)S(1)}, u32[]{:S(2)}, u32[]{:S(2)}) collective-permute-start(f32[56,8,128]{2,1,0:T(8,128)S(1)} %get-tuple-element.107), channel_id=1, source_target_pairs={{0,24},{4,12},{8,0},{12,20},{16,8},{20,28},{24,16},{28,4},{1,25},{... | collective-permute-start | bytes 688136 | tf_op jit(solution)/shard_map/ppermute | solution.py:507
  74.5 8.5 %collective-permute-start.17 = (f32[56,8,128]{2,1,0:T(8,128)S(1)}, f32[56,8,128]{2,1,0:T(8,128)S(1)}, u32[]{:S(2)}, u32[]{:S(2)}) collective-permute-start(f32[56,8,128]{2,1,0:T(8,128)S(1)} %shard_map.97), channel_id=1, source_target_pairs={{0,8},{4,28},{8,16},{12,4},{16,24},{20,12},{24,0},{28,20},{1,9},{5... | collective-permute-start | bytes 688136 | tf_op jit(solution)/shard_map/ppermute | solution.py:507
  83.2 3.7 %collective-permute-start.20 = (f32[16,8,128]{2,1,0:T(8,128)S(1)}, f32[16,8,128]{2,1,0:T(8,128)S(1)}, u32[]{:S(2)}, u32[]{:S(2)}) collective-permute-start(f32[16,8,128]{2,1,0:T(8,128)S(1)} %get-tuple-element.113), channel_id=1, source_target_pairs={{0,1},{1,2},{2,3},{3,0},{4,5},{5,6},{6,7},{7,4},{8,9},{9,10},{10,1... | collective-permute-start | bytes 196616 | tf_op jit(solution)/shard_map/ppermute | solution.py:498
  83.3 3.9 %collective-permute-start.21 = (f32[16,8,128]{2,1,0:T(8,128)S(1)}, f32[16,8,128]{2,1,0:T(8,128)S(1)}, u32[]{:S(2)}, u32[]{:S(2)}) collective-permute-start(f32[16,8,128]{2,1,0:T(8,128)S(1)} %get-tuple-element.114), channel_id=1, source_target_pairs={{0,3},{1,0},{2,1},{3,2},{4,7},{5,4},{6,5},{7,6},{8,11},{9,8},{10,9... | collective-permute-start | bytes 196616 | tf_op jit(solution)/shard_map/ppermute | solution.py:498
  87.1 12.4 %collective-permute-start.29 = (f32[20,8,128]{2,1,0:T(8,128)S(1)}, f32[20,8,128]{2,1,0:T(8,128)S(1)}, u32[]{:S(2)}, u32[]{:S(2)}) collective-permute-start(f32[20,8,128]{2,1,0:T(8,128)S(1)} %get-tuple-element.124), channel_id=1, source_target_pairs={{0,4},{4,8},{8,12},{12,16},{16,20},{20,24},{24,28},{28,0},{1,5},{5... | collective-permute-start | bytes 245768 | tf_op jit(solution)/shard_map/ppermute | solution.py:498
  87.5 12.0 %collective-permute-start.30 = (f32[20,8,128]{2,1,0:T(8,128)S(1)}, f32[20,8,128]{2,1,0:T(8,128)S(1)}, u32[]{:S(2)}, u32[]{:S(2)}) collective-permute-start(f32[20,8,128]{2,1,0:T(8,128)S(1)} %get-tuple-element.125), channel_id=1, source_target_pairs={{0,28},{4,0},{8,4},{12,8},{16,12},{20,16},{24,20},{28,24},{1,29},{... | collective-permute-start | bytes 245768 | tf_op jit(solution)/shard_map/ppermute | solution.py:498
  97.7 17.5 %collective-permute-start.22 = (f32[73,8,128]{2,1,0:T(8,128)S(1)}, f32[73,8,128]{2,1,0:T(8,128)S(1)}, u32[]{:S(2)}, u32[]{:S(2)}) collective-permute-start(f32[73,8,128]{2,1,0:T(8,128)S(1)} %get-tuple-element.116), channel_id=1, source_target_pairs={{0,1},{1,2},{2,3},{3,0},{4,5},{5,6},{6,7},{7,4},{8,9},{9,10},{10,1... | collective-permute-start | bytes 897032 | tf_op jit(solution)/shard_map/ppermute | solution.py:498
  99.1 16.1 %collective-permute-start.23 = (f32[73,8,128]{2,1,0:T(8,128)S(1)}, f32[73,8,128]{2,1,0:T(8,128)S(1)}, u32[]{:S(2)}, u32[]{:S(2)}) collective-permute-start(f32[73,8,128]{2,1,0:T(8,128)S(1)} %get-tuple-element.117), channel_id=1, source_target_pairs={{0,3},{1,0},{2,1},{3,2},{4,7},{5,4},{6,5},{7,6},{8,11},{9,8},{10,9... | collective-permute-start | bytes 897032 | tf_op jit(solution)/shard_map/ppermute | solution.py:498
  102.8 17.9 %collective-permute-start.31 = (f32[81,8,128]{2,1,0:T(8,128)S(1)}, f32[81,8,128]{2,1,0:T(8,128)S(1)}, u32[]{:S(2)}, u32[]{:S(2)}) collective-permute-start(f32[81,8,128]{2,1,0:T(8,128)S(1)} %get-tuple-element.130), channel_id=1, source_target_pairs={{0,1},{1,2},{2,3},{3,0},{4,5},{5,6},{6,7},{7,4},{8,9},{9,10},{10,1... | collective-permute-start | bytes 995336 | tf_op jit(solution)/shard_map/ppermute | solution.py:498
  103.4 17.3 %collective-permute-start.32 = (f32[81,8,128]{2,1,0:T(8,128)S(1)}, f32[81,8,128]{2,1,0:T(8,128)S(1)}, u32[]{:S(2)}, u32[]{:S(2)}) collective-permute-start(f32[81,8,128]{2,1,0:T(8,128)S(1)} %get-tuple-element.131), channel_id=1, source_target_pairs={{0,3},{1,0},{2,1},{3,2},{4,7},{5,4},{6,5},{7,6},{8,11},{9,8},{10,9... | collective-permute-start | bytes 995336 | tf_op jit(solution)/shard_map/ppermute | solution.py:498
  104.6 10.6 %collective-permute-start.24 = (f32[11,8,128]{2,1,0:T(8,128)S(1)}, f32[11,8,128]{2,1,0:T(8,128)S(1)}, u32[]{:S(2)}, u32[]{:S(2)}) collective-permute-start(f32[11,8,128]{2,1,0:T(8,128)S(1)} %get-tuple-element.118), channel_id=1, source_target_pairs={{0,2},{1,3},{2,0},{3,1},{4,6},{5,7},{6,4},{7,5},{8,10},{9,11},{10,... | collective-permute-start | bytes 135176 | tf_op jit(solution)/shard_map/ppermute | solution.py:498
  116.3 10.9 %collective-permute-start.27 = (f32[72,8,128]{2,1,0:T(8,128)S(1)}, f32[72,8,128]{2,1,0:T(8,128)S(1)}, u32[]{:S(2)}, u32[]{:S(2)}) collective-permute-start(f32[72,8,128]{2,1,0:T(8,128)S(1)} %get-tuple-element.123), channel_id=1, source_target_pairs={{0,4},{4,0},{8,12},{12,8},{16,20},{20,16},{24,28},{28,24},{1,5},{5... | collective-permute-start | bytes 884744 | tf_op jit(solution)/shard_map/ppermute | solution.py:502
  116.4 4.3 %collective-permute-start.33 = (f32[12,8,128]{2,1,0:T(8,128)S(1)}, f32[12,8,128]{2,1,0:T(8,128)S(1)}, u32[]{:S(2)}, u32[]{:S(2)}) collective-permute-start(f32[12,8,128]{2,1,0:T(8,128)S(1)} %get-tuple-element.132), channel_id=1, source_target_pairs={{0,2},{1,3},{2,0},{3,1},{4,6},{5,7},{6,4},{7,5},{8,10},{9,11},{10,... | collective-permute-start | bytes 147464 | tf_op jit(solution)/shard_map/ppermute | solution.py:498
  118.6 25.2 %collective-permute-start.25 = (f32[72,8,128]{2,1,0:T(8,128)S(1)}, f32[72,8,128]{2,1,0:T(8,128)S(1)}, u32[]{:S(2)}, u32[]{:S(2)}) collective-permute-start(f32[72,8,128]{2,1,0:T(8,128)S(1)} %get-tuple-element.120), channel_id=1, source_target_pairs={{0,4},{4,0},{8,12},{12,8},{16,20},{20,16},{24,28},{28,24},{1,5},{5... | collective-permute-start | bytes 884744 | tf_op jit(solution)/shard_map/ppermute | solution.py:502
  121.8 15.7 %collective-permute-start.36 = (f32[56,8,128]{2,1,0:T(8,128)S(1)}, f32[56,8,128]{2,1,0:T(8,128)S(1)}, u32[]{:S(2)}, u32[]{:S(2)}) collective-permute-start(f32[56,8,128]{2,1,0:T(8,128)S(1)} %get-tuple-element.137), channel_id=1, source_target_pairs={{0,4},{4,0},{8,12},{12,8},{16,20},{20,16},{24,28},{28,24},{1,5},{5... | collective-permute-start | bytes 688136 | tf_op jit(solution)/shard_map/ppermute | solution.py:502
  123.8 19.9 %collective-permute-start.38 = (f32[16,8,128]{2,1,0:T(8,128)S(1)}, f32[16,8,128]{2,1,0:T(8,128)S(1)}, u32[]{:S(2)}, u32[]{:S(2)}) collective-permute-start(f32[16,8,128]{2,1,0:T(8,128)S(1)} %get-tuple-element.138), channel_id=1, source_target_pairs={{0,12},{4,16},{8,20},{12,24},{16,28},{20,0},{24,4},{28,8},{1,13},{... | collective-permute-start | bytes 196616 | tf_op jit(solution)/shard_map/ppermute | solution.py:498
  123.8 21.9 %collective-permute-start.26 = (f32[72,8,128]{2,1,0:T(8,128)S(1)}, f32[72,8,128]{2,1,0:T(8,128)S(1)}, u32[]{:S(2)}, u32[]{:S(2)}) collective-permute-start(f32[72,8,128]{2,1,0:T(8,128)S(1)} %get-tuple-element.121), channel_id=1, source_target_pairs={{0,24},{4,12},{8,0},{12,20},{16,8},{20,28},{24,16},{28,4},{1,25},{... | collective-permute-start | bytes 884744 | tf_op jit(solution)/shard_map/ppermute | solution.py:507
  127.2 28.6 %collective-permute-start.28 = (f32[72,8,128]{2,1,0:T(8,128)S(1)}, f32[72,8,128]{2,1,0:T(8,128)S(1)}, u32[]{:S(2)}, u32[]{:S(2)}) collective-permute-start(f32[72,8,128]{2,1,0:T(8,128)S(1)} %shard_map.102), channel_id=1, source_target_pairs={{0,8},{4,28},{8,16},{12,4},{16,24},{20,12},{24,0},{28,20},{1,9},{5... | collective-permute-start | bytes 884744 | tf_op jit(solution)/shard_map/ppermute | solution.py:507
  137.5 4.8 %collective-permute-start.39 = (f32[8,8,128]{2,1,0:T(8,128)S(1)}, f32[8,8,128]{2,1,0:T(8,128)S(1)}, u32[]{:S(2)}, u32[]{:S(2)}) collective-permute-start(f32[8,8,128]{2,1,0:T(8,128)S(1)} %get-tuple-element.139), channel_id=1, source_target_pairs={{0,20},{4,24},{8,28},{12,0},{16,4},{20,8},{24,12},{28,16},{1,21},{... | collective-permute-start | bytes 98312 | tf_op jit(solution)/shard_map/ppermute | solution.py:498
  142.3 7.1 %collective-permute-start.34 = (f32[56,8,128]{2,1,0:T(8,128)S(1)}, f32[56,8,128]{2,1,0:T(8,128)S(1)}, u32[]{:S(2)}, u32[]{:S(2)}) collective-permute-start(f32[56,8,128]{2,1,0:T(8,128)S(1)} %get-tuple-element.134), channel_id=1, source_target_pairs={{0,4},{4,0},{8,12},{12,8},{16,20},{20,16},{24,28},{28,24},{1,5},{5... | collective-permute-start | bytes 688136 | tf_op jit(solution)/shard_map/ppermute | solution.py:502
  143.7 12.1 %collective-permute-start.35 = (f32[56,8,128]{2,1,0:T(8,128)S(1)}, f32[56,8,128]{2,1,0:T(8,128)S(1)}, u32[]{:S(2)}, u32[]{:S(2)}) collective-permute-start(f32[56,8,128]{2,1,0:T(8,128)S(1)} %get-tuple-element.135), channel_id=1, source_target_pairs={{0,24},{4,12},{8,0},{12,20},{16,8},{20,28},{24,16},{28,4},{1,25},{... | collective-permute-start | bytes 688136 | tf_op jit(solution)/shard_map/ppermute | solution.py:507
  143.8 12.1 %collective-permute-start.37 = (f32[56,8,128]{2,1,0:T(8,128)S(1)}, f32[56,8,128]{2,1,0:T(8,128)S(1)}, u32[]{:S(2)}, u32[]{:S(2)}) collective-permute-start(f32[56,8,128]{2,1,0:T(8,128)S(1)} %shard_map.106), channel_id=1, source_target_pairs={{0,8},{4,28},{8,16},{12,4},{16,24},{20,12},{24,0},{28,20},{1,9},{5... | collective-permute-start | bytes 688136 | tf_op jit(solution)/shard_map/ppermute | solution.py:507
  (3 other events, 2.2 us)

commit v4 on v3

--- a/solution.py
+++ b/solution.py
@@ -52,16 +52,49 @@
     )
 
 
-def columns_body(cy, vel, labels, rates, left, right):
-    for out, y0 in ((left, 0), (right, cy - 2)):
+def columns_body(cy, vel, labels, rates_at, left, right, near_vel, near_labels, rates, sem):
+    copies = [pltpu.make_async_copy(rates_at, rates, sem.at[4])]
+    for n, y0 in enumerate((0, cy - 2)):
+        at = pl.ds(y0, 2)
+        copies.append(pltpu.make_async_copy(vel.at[:, :, at, :], near_vel.at[n], sem.at[2 * n]))
+        copies.append(pltpu.make_async_copy(labels.at[:, at, :], near_labels.at[n], sem.at[2 * n + 1]))
+    for copy in copies:
+        copy.start()
+    for copy in copies:
+        copy.wait()
+    for n, out in enumerate((left, right)):
         for k in range(2):
-            cell = jnp.where(labels[:, y0 + k, :] == 1, rates[1], rates[0])
+            cell = jnp.where(near_labels[n, :, k, :] == 1, rates[1], rates[0])
             out[:, FIELDS * k, :] = cell
             for f in range(3):
-                out[:, FIELDS * k + f + 1, :] = vel[f, :, y0 + k, :]
-
-
-def prep_body(cx, cy, level, vel, labels, rates, state, rate):
+                out[:, FIELDS * k + f + 1, :] = near_vel[n, f, :, k, :]
+
+
+def in_hbm(value):
+    return pltpu.with_memory_space_constraint(value, pltpu.HBM)
+
+
+def prep_body(cx, cy, step, *refs):
+    level_at, vel_at, labels_at, rates_at, sx_at, sy_at, fraction = refs[:7]
+    state, rate, weights, own_moves = refs[7:11]
+    level, vel, labels, rates, sx, sy, near, sem = refs[11:]
+    copies = [
+        pltpu.make_async_copy(a, b, sem.at[n])
+        for n, (a, b) in enumerate(
+            zip(
+                (vel_at, level_at, labels_at, rates_at, sx_at, sy_at, fraction.at[step]),
+                (vel, level, labels, rates, sx, sy, near),
+            )
+        )
+    ]
+    for copy in copies:
+        copy.start()
+    for copy in copies[:6]:
+        copy.wait()
+    for n in range(STEPS):
+        own_moves[n] = jnp.full(own_moves.shape[1:], sx[0, 0, n].astype(jnp.float32))
+        own_moves[STEPS + n] = jnp.full(own_moves.shape[1:], sy[0, 0, n].astype(jnp.float32))
+
     def row(x, _):
         state[x, pl.ds(0, cy, stride=FIELDS), :] = level[x]
         for f in range(3):
@@ -72,6 +105,8 @@
         return 0
 
     lax.fori_loop(0, cx, row, 0)
+    copies[6].wait()
+    fill_weights(cx, cy, near, weights)
 
 
 def edge_rows_body(cx, pairs, mix, *refs):
@@ -89,15 +124,25 @@
                 out[k * wide + q + 1] = v
 
 
-def weights_body(cx, cy, step, fraction, out):
+def fill_weights(cx, cy, near, out):
+    pairs = cy // 2
+
     def row(x, _):
         for d in range(3):
-            for k, w in enumerate(cubic_weights(fraction[step, d, x])):
+            for k, w in enumerate(cubic_weights(near[d, x])):
+                table = out.at[4 * d + k, pl.ds(x * pairs, pairs)].reshape(FIELDS * cy, w.shape[-1])
                 for f in range(FIELDS):
-                    out[4 * d + k, x, pl.ds(f, cy, stride=FIELDS), :] = w
+                    table[pl.ds(f, cy, stride=FIELDS), :] = w
         return 0
 
     lax.fori_loop(0, cx, row, 0)
+
+
+def weights_body(cx, cy, step, fraction, out, near, sem):
+    copy = pltpu.make_async_copy(fraction.at[step], near, sem)
+    copy.start()
+    copy.wait()
+    fill_weights(cx, cy, near, out)
 
 
 def fill_rows(pad, at, rows, pairs, own, ym, yp, change):
@@ -305,11 +350,11 @@
         sums = [[None] * 4 for _ in range(4)]
         for a in range(4):
             padded, row = rows[a]
-            k = pl.ds(SUB * q, SUB)
-            h = g[padded * pairs + q] * w[a, row, k, :]
-            wy = [w[4 + b, row, k, :] for b in range(4)]
+            k = row * pairs + q
+            h = g[padded * pairs + q] * w[a, k]
+            wy = [w[4 + b, k] for b in range(4)]
             for c in range(4):
-                hc = h * w[8 + c, row, k, :]
+                hc = h * w[8 + c, k]
                 for b in range(4):
                     t = hc * wy[b]
                     sums[b][c] = t if sums[b][c] is None else sums[b][c] + t
@@ -328,10 +373,9 @@
     return out
 
 
-def spread(cx, pairs, rows_of, count, lead, g, w, shift_x, shift_y, step, own, right, left, far):
-    shape = g.shape[1:]
-    move_x = shift_x[0, 0, step]
-    move_y = shift_y[0, 0, step]
+def spread(cx, pairs, rows_of, count, lead, g, w, moves, step, own, right, left, far):
+    move_x = moves[step]
+    move_y = moves[STEPS + step]
     here = jnp.where(move_y == 0, 1.0, 0.0)
     up = jnp.where(move_y == 1, 1.0, 0.0)
     down = jnp.where(move_y == -1, 1.0, 0.0)
@@ -355,35 +399,33 @@
         return 0
 
     lax.fori_loop(0, count, row, 0)
-    mx = jnp.full(shape, move_x.astype(jnp.float32))
-    right[count * pairs] = mx
-    left[count * pairs] = mx
-    far[count] = mx
-    far[count + 1] = jnp.full(shape, move_y.astype(jnp.float32))
+    right[count * pairs] = move_x
+    left[count * pairs] = move_x
+    far[count] = move_x
+    far[count + 1] = move_y
 
 
 def inner_body(cx, pairs, step, rows_of, count, *refs):
-    own, ym, yp, coefs, w, sx, sy = refs[0], refs[1], refs[2], refs[3:9], refs[9], refs[10], refs[11]
-    o, r, l, far, mid, g, pad = refs[12:]
+    own, ym, yp, coefs, w, moves = refs[0], refs[1], refs[2], refs[3:9], refs[9], refs[10]
+    o, r, l, far, mid, g, pad = refs[11:]
     diffuse_inner(cx, pairs, own, ym, yp, coefs, pad, mid, g)
-    spread(cx, pairs, rows_of, count, 0, g, w, sx, sy, step, o, r, l, far)
+    spread(cx, pairs, rows_of, count, 0, g, w, moves, step, o, r, l, far)
 
 
 def outer_body(cx, pairs, step, rows_of, count, *refs):
     own, halos, coefs, outer = refs[0], refs[1:5], refs[5:11], refs[11:17]
-    mid_inner, g_inner, w, sx, sy = refs[17:22]
-    o, r, l, far, pad, mid, g = refs[22:]
+    mid_inner, g_inner, w, moves = refs[17:21]
+    o, r, l, far, pad, mid, g = refs[21:]
     diffuse_outer(cx, pairs, own, *halos, coefs, outer, mid_inner, g_inner, pad, mid, g)
-    spread(cx, pairs, rows_of, count, 3, g, w, sx, sy, step, o, r, l, far)
+    spread(cx, pairs, rows_of, count, 3, g, w, moves, step, o, r, l, far)
 
 
 def gather_body(pairs, step, main, rims, *refs):
-    own, right, left, far_low, far_high, sx = refs[:6]
+    own, right, left, far_low, far_high, own_moves = refs[:6]
     outs = refs[6:11]
-    shape = own.shape[1:]
     count = own.shape[0] // pairs
     skip = 3 if rims else 0
-    mine = jnp.full(shape, sx[0, 0, step].astype(jnp.float32))
+    mine = own_moves[step]
     moves = (mine, right[count * pairs], left[count * pairs])
     far_moves = (far_low[count], far_high[count])
     far_gates = (far_low[count + 1] == 1.0, far_high[count + 1] == -1.0)
@@ -521,29 +563,46 @@
     def scratch(n):
         return pltpu.VMEM((n, SUB, cz), jnp.float32)
 
+    level, vel, labels, rates = map(in_hbm, (level, vel, labels, rates))
+    fraction, shift_x, shift_y = map(in_hbm, (fraction, shift_x, shift_y))
+    hbm = pl.BlockSpec(memory_space=pltpu.HBM)
+    rates_here = pltpu.SMEM(rates.shape, rates.dtype)
+    near = pltpu.VMEM(fraction.shape[1:], fraction.dtype)
     left, right = call(
         functools.partial(columns_body, cy),
         [plane(cx)] * 2,
         (vel, labels, rates),
-        [VMEM, VMEM, SMEM],
+        [hbm] * 3,
+        [
+            pltpu.VMEM((2, *vel.shape[:2], 2, cz), vel.dtype),
+            pltpu.VMEM((2, cx, 2, cz), labels.dtype),
+            rates_here,
+            pltpu.SemaphoreType.DMA((5,)),
+        ],
     )
-    state, rate = call(
-        functools.partial(prep_body, cx, cy),
-        [f32(cx, FIELDS * cy, cz)] * 2,
-        (level, vel, labels, rates),
-        [VMEM, VMEM, VMEM, SMEM],
+    last = STEPS - 1
+    table = f32(12, cx * pairs + 1, SUB, cz)
+    state, rate, weights_last, own_moves = call(
+        functools.partial(prep_body, cx, cy, last),
+        [f32(cx, FIELDS * cy, cz)] * 2 + [table, plane(2 * STEPS)],
+        (level, vel, labels, rates, shift_x, shift_y, fraction),
+        [hbm] * 7,
+        [pltpu.VMEM(a.shape, a.dtype) for a in (level, vel, labels)]
+        + [pltpu.SMEM(a.shape, a.dtype) for a in (rates, shift_x, shift_y)]
+        + [near, pltpu.SemaphoreType.DMA((7,))],
     )
     state = state.reshape(cx * pairs, SUB, cz)
     rate = rate.reshape(cx * pairs, SUB, cz)
     weights = [
         call(
             functools.partial(weights_body, cx, cy, s),
-            [f32(12, cx, FIELDS * cy, cz)],
+            [table],
             (fraction,),
-            [VMEM],
+            [hbm],
+            [near, pltpu.SemaphoreType.DMA],
         )[0]
-        for s in range(STEPS)
-    ]
+        for s in range(last)
+    ] + [weights_last]
     coefs = outer = None
 
     inner = 4
@@ -591,8 +650,8 @@
         *sent_a, mid, g = call(
             functools.partial(inner_body, cx, pairs, step, rows_a, counts[0]),
             outs(counts[0]) + [plane(cx * wide), plane(cx * pairs)],
-            (state, ym, yp, *coefs, weights[step], shift_x, shift_y),
-            [VMEM] * 10 + [SMEM] * 2,
+            (state, ym, yp, *coefs, weights[step], own_moves),
+            [VMEM] * 11,
             [scratch(cx * wide)],
             flops=20000000,
         )
@@ -607,8 +666,8 @@
         sent_b = call(
             functools.partial(outer_body, cx, pairs, step, rows_b, counts[1]),
             outs(counts[1]),
-            (state, xm, xp, ym, yp, *coefs, *outer, mid, g, weights[step], shift_x, shift_y),
-            [VMEM] * 20 + [SMEM] * 2,
+            (state, xm, xp, ym, yp, *coefs, *outer, mid, g, weights[step], own_moves),
+            [VMEM] * 21,
             [scratch(8 * wide), scratch(8 * wide), scratch((cx + 6) * pairs)],
             flops=10000000,
         )
@@ -623,8 +682,8 @@
             e1, e0, f, k, t0, *rims = call(
                 functools.partial(gather_body, pairs, step, main[n], n == 1),
                 [plane(main[n] * pairs)] * 5 + ([plane(2 * pairs), plane(pairs)] if n else []),
-                (own, right, left, far_low, far_high, shift_x),
-                [VMEM] * 5 + [SMEM],
+                (own, right, left, far_low, far_high, own_moves),
+                [VMEM] * 6,
                 flops=3000000,
             )
             e1 = swapped(e1)

time: 157 us -> 148 us (0.943)
  local copies, waits for them, and re-layouts: 7.15 us -> 0 us
  Pallas kernels: 27.2 us -> 23.8 us
  waiting for transfers between devices: 66.2 us -> 67.8 us
    unnamed x22 -> x0, local copies, waits for them, and re-layouts: 7.15 us -> none
    pallas_call x22 -> x21, Pallas kernels: 27.2 us -> 23.8 us  [call(): pl.pallas_call(body, out_shape=tuple(outs), in_specs=list(specs), out_spe...]
    ppermute x24, waiting for transfers between devices: 28 us -> 30.1 us  [moved(): lax.ppermute(value, axis, [(i, (i + steps) % count) for i in range(count)])]
  transfers between devices with their start and end apart: 40 -> 40, of which waited for: 14 -> 18; matrix products, arithmetic and copies ran while one was open for 0% -> 0% of each run, Pallas kernels for 16% -> 15%
where the time goes in v4:
time: 148 us
  waiting for transfers between devices  67.8 us (46%)
  starting transfers between devices  55.2 us (37%)
  Pallas kernels  23.8 us (16%)
    ppermute x24, starting transfers between devices, moved(): lax.ppermute(value, axis, [(i, (i + steps) % count) for i in range(count)])  31.7 us
    ppermute x24, waiting for transfers between devices, moved(): lax.ppermute(value, axis, [(i, (i + steps) % count) for i in range(count)])  30.1 us
    ppermute x8, waiting for transfers between devices, swapped(): lax.ppermute(value, 'gx', [(i, i ^ 1) for i in range(lax.axis_size('gx'))])  24.8 us
    pallas_call x21, Pallas kernels, call(): pl.pallas_call(body, out_shape=tuple(outs), in_specs=list(specs), out_spe...  23.8 us
    ppermute x8, waiting for transfers between devices, crossed(): lax.ppermute(value, 'gx', [(i, (i + (2 if i % 2 else -2) * sign) % count)...  12.8 us
    ppermute x8, starting transfers between devices, crossed(): lax.ppermute(value, 'gx', [(i, (i + (2 if i % 2 else -2) * sign) % count)...  11.9 us
    ppermute x8, starting transfers between devices, swapped(): lax.ppermute(value, 'gx', [(i, i ^ 1) for i in range(lax.axis_size('gx'))])  11.6 us
  transfers between devices with their start and end apart: 40, of which 18 were waited for; matrix products, arithmetic and copies ran while one was open for 0% of the time, Pallas kernels for 15%

profile of v4, /device:TPU:0, one launch (start us, length us, event | category | flops | bytes accessed | tf_op | source)
XLA Modules:
  0.0 147.7 jit_solution(13221419886981783255)
XLA Ops:
  0.6 1.0 shard_map.87
  2.2 2.0 %collective-permute-start.1 = (f32[16,8,128]{2,1,0:T(8,128)S(1)}, f32[16,8,128]{2,1,0:T(8,128)S(1)}, u32[]{:S(2)}, u32[]{:S(2)}) collective-permute-start(f32[16,8,128]{2,1,0:T(8,128)S(1)} %get-tuple-element.75), channel_id=1, source_target_pairs={{0,3},{1,0},{2,1},{3,2},{4,7},{5,4},{6,5},{7,6},{8,11},{9,8},{10,9... | collective-permute-start | bytes 196616 | tf_op jit(solution)/shard_map/ppermute | solution.py:540
  4.1 1.8 %shard_map.86 = (f32[16,64,128]{2,1,0:T(8,128)S(1)}, f32[16,64,128]{2,1,0:T(8,128)S(1)}, f32[12,129,8,128]{3,2,1,0:T(8,128)S(1)}, f32[4,8,128]{2,1,0:T(8,128)S(1)}) custom-call(f32[16,16,128]{2,1,0:T(8,128)} %refs_0_.1, f32[3,16,16,128]{3,2,1,0:T(8,128)} %vel.1, s32[16,16,128]{2,1,0:T(8,128)} %labels.1, f32[2]{0:T(128)} %rates_at.1, s32[1,1,2]{2,1,0:T(1,128)} %refs_4_.1, ...), custom_call_target="tpu_custom_call" | custom-call | flops 1000000 | bytes 8847384 | tf_op jit(solution)/shard_map/pallas_call | solution.py:21
  6.6 4.9 %collective-permute-start.10 = (f32[20,8,128]{2,1,0:T(8,128)S(1)}, f32[20,8,128]{2,1,0:T(8,128)S(1)}, u32[]{:S(2)}, u32[]{:S(2)}) collective-permute-start(f32[20,8,128]{2,1,0:T(8,128)S(1)} %get-tuple-element.95), channel_id=1, source_target_pairs={{0,28},{4,0},{8,4},{12,8},{16,12},{20,16},{24,20},{28,24},{1,29},{... | collective-permute-start | bytes 245768 | tf_op jit(solution)/shard_map/ppermute | solution.py:540
  11.5 1.6 %shard_map.88 = (f32[190,8,128]{2,1,0:T(8,128)S(1)}, f32[180,8,128]{2,1,0:T(8,128)S(1)}, f32[180,8,128]{2,1,0:T(8,128)S(1)}, f32[180,8,128]{2,1,0:T(8,128)S(1)},...) custom-call(f32[128,8,128]{2,1,0:T(8,128)S(1)} %bitcast.6, ...), custom_call_target="tpu_custom_call" | custom-call | flops 1000000 | bytes 5120000 | tf_op jit(solution)/shard_map/pallas_call | solution.py:21
  13.1 4.6 %shard_map.89 = (f32[72,8,128]{2,1,0:T(8,128)S(1)}, f32[73,8,128]{2,1,0:T(8,128)S(1)}, f32[73,8,128]{2,1,0:T(8,128)S(1)}, f32[11,8,128]{2,1,0:T(8,128)S(1)}, f32...) custom-call(f32[128,8,128]{2,1,0:T(8,128)S(1)} %bitcast.3, ...), custom_call_target="tpu_custom_call" | custom-call | flops 20000000 | bytes 13594624 | tf_op jit(solution)/shard_map/pallas_call | solution.py:21
  17.6 1.4 collective-permute-start.2
  19.6 2.5 %shard_map.94 = (f32[80,8,128]{2,1,0:T(8,128)S(1)}, f32[81,8,128]{2,1,0:T(8,128)S(1)}, f32[81,8,128]{2,1,0:T(8,128)S(1)}, f32[12,8,128]{2,1,0:T(8,128)S(1)}) custom-call(f32[128,8,128]{2,1,0:T(8,128)S(1)} %bitcast.4, f32[20,8,128]{2,1,0:T(8,128)S(1)} %collective-permute-done.9.xm.refs_1_, f32[20,8,128]{2,1,0:T(8,128)S(1)} %collective-permute-done.10.xp.refs_2_, ...), custom_call_target="tpu_custom_call" | custom-call | flops 10000000 | bytes 14925824 | tf_op jit(solution)/shard_map/pallas_call | solution.py:21
  22.2 1.7 %collective-permute-start.12 = (f32[81,8,128]{2,1,0:T(8,128)S(1)}, f32[81,8,128]{2,1,0:T(8,128)S(1)}, u32[]{:S(2)}, u32[]{:S(2)}) collective-permute-start(f32[81,8,128]{2,1,0:T(8,128)S(1)} %get-tuple-element.107), channel_id=1, source_target_pairs={{0,3},{1,0},{2,1},{3,2},{4,7},{5,4},{6,5},{7,6},{8,11},{9,8},{10,9... | collective-permute-start | bytes 995336 | tf_op jit(solution)/shard_map/ppermute | solution.py:540
  23.9 1.5 %collective-permute-start.4 = (f32[11,8,128]{2,1,0:T(8,128)S(1)}, f32[11,8,128]{2,1,0:T(8,128)S(1)}, u32[]{:S(2)}, u32[]{:S(2)}) collective-permute-start(f32[11,8,128]{2,1,0:T(8,128)S(1)} %get-tuple-element.88), channel_id=1, source_target_pairs={{0,2},{1,3},{2,0},{3,1},{4,6},{5,7},{6,4},{7,5},{8,10},{9,11},{10,... | collective-permute-start | bytes 135176 | tf_op jit(solution)/shard_map/ppermute | solution.py:540
  25.4 9.8 %collective-permute-done.4.refs_3_.refs_4_ = f32[11,8,128]{2,1,0:T(8,128)S(1)} collective-permute-done((f32[11,8,128]{2,1,0:T(8,128)S(1)}, f32[11,8,128]{2,1,0:T(8,128)S(1)}, u32[]{:S(2)}, u32[]{:S(2)}) %collective-permute-start.4) | collective-permute-done | bytes 45088 | tf_op jit(solution)/shard_map/ppermute | solution.py:540
  35.8 1.6 %collective-permute-start.13 = (f32[12,8,128]{2,1,0:T(8,128)S(1)}, f32[12,8,128]{2,1,0:T(8,128)S(1)}, u32[]{:S(2)}, u32[]{:S(2)}) collective-permute-start(f32[12,8,128]{2,1,0:T(8,128)S(1)} %get-tuple-element.108), channel_id=1, source_target_pairs={{0,2},{1,3},{2,0},{3,1},{4,6},{5,7},{6,4},{7,5},{8,10},{9,11},{10,... | collective-permute-start | bytes 147464 | tf_op jit(solution)/shard_map/ppermute | solution.py:540
  37.4 1.9 %collective-permute-start.5 = (f32[72,8,128]{2,1,0:T(8,128)S(1)}, f32[72,8,128]{2,1,0:T(8,128)S(1)}, u32[]{:S(2)}, u32[]{:S(2)}) collective-permute-start(f32[72,8,128]{2,1,0:T(8,128)S(1)} %get-tuple-element.90), channel_id=1, source_target_pairs={{0,4},{4,0},{8,12},{12,8},{16,20},{20,16},{24,28},{28,24},{1,5},{5... | collective-permute-start | bytes 884744 | tf_op jit(solution)/shard_map/ppermute | solution.py:544
  39.3 0.7 collective-permute-done.13.refs_3_.refs_4_
  40.0 0.6 shard_map.95
  40.6 2.0 %collective-permute-start.16 = (f32[56,8,128]{2,1,0:T(8,128)S(1)}, f32[56,8,128]{2,1,0:T(8,128)S(1)}, u32[]{:S(2)}, u32[]{:S(2)}) collective-permute-start(f32[56,8,128]{2,1,0:T(8,128)S(1)} %get-tuple-element.113), channel_id=1, source_target_pairs={{0,4},{4,0},{8,12},{12,8},{16,20},{20,16},{24,28},{28,24},{1,5},{5... | collective-permute-start | bytes 688136 | tf_op jit(solution)/shard_map/ppermute | solution.py:544
  42.6 0.9 collective-permute-start.18
  43.5 2.5 %collective-permute-start.6 = (f32[72,8,128]{2,1,0:T(8,128)S(1)}, f32[72,8,128]{2,1,0:T(8,128)S(1)}, u32[]{:S(2)}, u32[]{:S(2)}) collective-permute-start(f32[72,8,128]{2,1,0:T(8,128)S(1)} %get-tuple-element.91), channel_id=1, source_target_pairs={{0,24},{4,12},{8,0},{12,20},{16,8},{20,28},{24,16},{28,4},{1,25},{... | collective-permute-start | bytes 884744 | tf_op jit(solution)/shard_map/ppermute | solution.py:549
  46.5 9.1 %collective-permute-done.16.b = f32[56,8,128]{2,1,0:T(8,128)S(1)} collective-permute-done((f32[56,8,128]{2,1,0:T(8,128)S(1)}, f32[56,8,128]{2,1,0:T(8,128)S(1)}, u32[]{:S(2)}, u32[]{:S(2)}) %collective-permute-start.16) | collective-permute-done | bytes 229408 | tf_op jit(solution)/shard_map/ppermute | solution.py:544
  55.6 1.9 %collective-permute-start.19 = (f32[8,8,128]{2,1,0:T(8,128)S(1)}, f32[8,8,128]{2,1,0:T(8,128)S(1)}, u32[]{:S(2)}, u32[]{:S(2)}) collective-permute-start(f32[8,8,128]{2,1,0:T(8,128)S(1)} %get-tuple-element.115), channel_id=1, source_target_pairs={{0,20},{4,24},{8,28},{12,0},{16,4},{20,8},{24,12},{28,16},{1,21},{... | collective-permute-start | bytes 98312 | tf_op jit(solution)/shard_map/ppermute | solution.py:540
  57.6 2.9 %collective-permute-done.19.refs_9_ = f32[8,8,128]{2,1,0:T(8,128)S(1)} collective-permute-done((f32[8,8,128]{2,1,0:T(8,128)S(1)}, f32[8,8,128]{2,1,0:T(8,128)S(1)}, u32[]{:S(2)}, u32[]{:S(2)}) %collective-permute-start.19) | collective-permute-done | bytes 32800 | tf_op jit(solution)/shard_map/ppermute | solution.py:540
  60.4 2.4 %collective-permute-start.14 = (f32[56,8,128]{2,1,0:T(8,128)S(1)}, f32[56,8,128]{2,1,0:T(8,128)S(1)}, u32[]{:S(2)}, u32[]{:S(2)}) collective-permute-start(f32[56,8,128]{2,1,0:T(8,128)S(1)} %get-tuple-element.110), channel_id=1, source_target_pairs={{0,4},{4,0},{8,12},{12,8},{16,20},{20,16},{24,28},{28,24},{1,5},{5... | collective-permute-start | bytes 688136 | tf_op jit(solution)/shard_map/ppermute | solution.py:544
  62.8 3.9 %collective-permute-start.15 = (f32[56,8,128]{2,1,0:T(8,128)S(1)}, f32[56,8,128]{2,1,0:T(8,128)S(1)}, u32[]{:S(2)}, u32[]{:S(2)}) collective-permute-start(f32[56,8,128]{2,1,0:T(8,128)S(1)} %get-tuple-element.111), channel_id=1, source_target_pairs={{0,24},{4,12},{8,0},{12,20},{16,8},{20,28},{24,16},{28,4},{1,25},{... | collective-permute-start | bytes 688136 | tf_op jit(solution)/shard_map/ppermute | solution.py:549
  66.7 1.3 collective-permute-done.14.refs_5_
  68.0 3.9 %collective-permute-done.15.refs_6_ = f32[56,8,128]{2,1,0:T(8,128)S(1)} collective-permute-done((f32[56,8,128]{2,1,0:T(8,128)S(1)}, f32[56,8,128]{2,1,0:T(8,128)S(1)}, u32[]{:S(2)}, u32[]{:S(2)}) %collective-permute-start.15) | collective-permute-done | bytes 229408 | tf_op jit(solution)/shard_map/ppermute | solution.py:549
  72.0 2.7 %collective-permute-done.17.refs_7_ = f32[56,8,128]{2,1,0:T(8,128)S(1)} collective-permute-done((f32[56,8,128]{2,1,0:T(8,128)S(1)}, f32[56,8,128]{2,1,0:T(8,128)S(1)}, u32[]{:S(2)}, u32[]{:S(2)}) %collective-permute-start.17) | collective-permute-done | bytes 229408 | tf_op jit(solution)/shard_map/ppermute | solution.py:549
  74.9 1.7 %collective-permute-start.21 = (f32[16,8,128]{2,1,0:T(8,128)S(1)}, f32[16,8,128]{2,1,0:T(8,128)S(1)}, u32[]{:S(2)}, u32[]{:S(2)}) collective-permute-start(f32[16,8,128]{2,1,0:T(8,128)S(1)} %get-tuple-element.118), channel_id=1, source_target_pairs={{0,3},{1,0},{2,1},{3,2},{4,7},{5,4},{6,5},{7,6},{8,11},{9,8},{10,9... | collective-permute-start | bytes 196616 | tf_op jit(solution)/shard_map/ppermute | solution.py:540
  76.7 1.9 %collective-permute-done.20.refs_1_.refs_3_ = f32[16,8,128]{2,1,0:T(8,128)S(1)} collective-permute-done((f32[16,8,128]{2,1,0:T(8,128)S(1)}, f32[16,8,128]{2,1,0:T(8,128)S(1)}, u32[]{:S(2)}, u32[]{:S(2)}) %collective-permute-start.20) | collective-permute-done | bytes 65568 | tf_op jit(solution)/shard_map/ppermute | solution.py:540
  79.2 4.7 %collective-permute-start.30 = (f32[20,8,128]{2,1,0:T(8,128)S(1)}, f32[20,8,128]{2,1,0:T(8,128)S(1)}, u32[]{:S(2)}, u32[]{:S(2)}) collective-permute-start(f32[20,8,128]{2,1,0:T(8,128)S(1)} %get-tuple-element.129), channel_id=1, source_target_pairs={{0,28},{4,0},{8,4},{12,8},{16,12},{20,16},{24,20},{28,24},{1,29},{... | collective-permute-start | bytes 245768 | tf_op jit(solution)/shard_map/ppermute | solution.py:540
  83.9 1.5 %shard_map.98.refs_9_.refs_19_ = f32[12,129,8,128]{3,2,1,0:T(8,128)S(1)} custom-call(f32[2,3,16,16,128]{4,3,2,1,0:T(8,128)} %fraction.1), custom_call_target="tpu_custom_call" | custom-call | flops 1000000 | bytes 7127040 | tf_op jit(solution)/shard_map/pallas_call | solution.py:21
  85.4 4.6 %shard_map.99 = (f32[72,8,128]{2,1,0:T(8,128)S(1)}, f32[73,8,128]{2,1,0:T(8,128)S(1)}, f32[73,8,128]{2,1,0:T(8,128)S(1)}, f32[11,8,128]{2,1,0:T(8,128)S(1)}, f32...) custom-call(f32[128,8,128]{2,1,0:T(8,128)S(1)} %get-tuple-element.116.refs_0_, ...), custom_call_target="tpu_custom_call" | custom-call | flops 20000000 | bytes 13594624 | tf_op jit(solution)/shard_map/pallas_call | solution.py:21
  89.9 1.5 %collective-permute-start.22 = (f32[73,8,128]{2,1,0:T(8,128)S(1)}, f32[73,8,128]{2,1,0:T(8,128)S(1)}, u32[]{:S(2)}, u32[]{:S(2)}) collective-permute-start(f32[73,8,128]{2,1,0:T(8,128)S(1)} %get-tuple-element.120), channel_id=1, source_target_pairs={{0,1},{1,2},{2,3},{3,0},{4,5},{5,6},{6,7},{7,4},{8,9},{9,10},{10,1... | collective-permute-start | bytes 897032 | tf_op jit(solution)/shard_map/ppermute | solution.py:540
  91.8 2.5 %shard_map.103 = (f32[80,8,128]{2,1,0:T(8,128)S(1)}, f32[81,8,128]{2,1,0:T(8,128)S(1)}, f32[81,8,128]{2,1,0:T(8,128)S(1)}, f32[12,8,128]{2,1,0:T(8,128)S(1)}) custom-call(f32[128,8,128]{2,1,0:T(8,128)S(1)} %get-tuple-element.116.refs_0_, f32[20,8,128]{2,1,0:T(8,128)S(1)} %collective-permute-done.29.refs_1_, ...), custom_call_target="tpu_custom_call" | custom-call | flops 10000000 | bytes 14925824 | tf_op jit(solution)/shard_map/pallas_call | solution.py:21
  94.2 1.0 collective-permute-start.31
  95.2 0.8 collective-permute-start.32
  96.0 2.5 %collective-permute-start.24 = (f32[11,8,128]{2,1,0:T(8,128)S(1)}, f32[11,8,128]{2,1,0:T(8,128)S(1)}, u32[]{:S(2)}, u32[]{:S(2)}) collective-permute-start(f32[11,8,128]{2,1,0:T(8,128)S(1)} %get-tuple-element.122), channel_id=1, source_target_pairs={{0,2},{1,3},{2,0},{3,1},{4,6},{5,7},{6,4},{7,5},{8,10},{9,11},{10,... | collective-permute-start | bytes 135176 | tf_op jit(solution)/shard_map/ppermute | solution.py:540
  98.6 8.9 %collective-permute-done.24.refs_3_.refs_4_ = f32[11,8,128]{2,1,0:T(8,128)S(1)} collective-permute-done((f32[11,8,128]{2,1,0:T(8,128)S(1)}, f32[11,8,128]{2,1,0:T(8,128)S(1)}, u32[]{:S(2)}, u32[]{:S(2)}) %collective-permute-start.24) | collective-permute-done | bytes 45088 | tf_op jit(solution)/shard_map/ppermute | solution.py:540
  108.1 2.2 %collective-permute-start.33 = (f32[12,8,128]{2,1,0:T(8,128)S(1)}, f32[12,8,128]{2,1,0:T(8,128)S(1)}, u32[]{:S(2)}, u32[]{:S(2)}) collective-permute-start(f32[12,8,128]{2,1,0:T(8,128)S(1)} %get-tuple-element.136), channel_id=1, source_target_pairs={{0,2},{1,3},{2,0},{3,1},{4,6},{5,7},{6,4},{7,5},{8,10},{9,11},{10,... | collective-permute-start | bytes 147464 | tf_op jit(solution)/shard_map/ppermute | solution.py:540
  110.2 1.9 %collective-permute-start.25 = (f32[72,8,128]{2,1,0:T(8,128)S(1)}, f32[72,8,128]{2,1,0:T(8,128)S(1)}, u32[]{:S(2)}, u32[]{:S(2)}) collective-permute-start(f32[72,8,128]{2,1,0:T(8,128)S(1)} %get-tuple-element.124), channel_id=1, source_target_pairs={{0,4},{4,0},{8,12},{12,8},{16,20},{20,16},{24,28},{28,24},{1,5},{5... | collective-permute-start | bytes 884744 | tf_op jit(solution)/shard_map/ppermute | solution.py:544
  112.9 2.0 %collective-permute-start.36 = (f32[56,8,128]{2,1,0:T(8,128)S(1)}, f32[56,8,128]{2,1,0:T(8,128)S(1)}, u32[]{:S(2)}, u32[]{:S(2)}) collective-permute-start(f32[56,8,128]{2,1,0:T(8,128)S(1)} %get-tuple-element.141), channel_id=1, source_target_pairs={{0,4},{4,0},{8,12},{12,8},{16,20},{20,16},{24,28},{28,24},{1,5},{5... | collective-permute-start | bytes 688136 | tf_op jit(solution)/shard_map/ppermute | solution.py:544
  114.9 3.3 %collective-permute-start.26 = (f32[72,8,128]{2,1,0:T(8,128)S(1)}, f32[72,8,128]{2,1,0:T(8,128)S(1)}, u32[]{:S(2)}, u32[]{:S(2)}) collective-permute-start(f32[72,8,128]{2,1,0:T(8,128)S(1)} %get-tuple-element.125), channel_id=1, source_target_pairs={{0,24},{4,12},{8,0},{12,20},{16,8},{20,28},{24,16},{28,4},{1,25},{... | collective-permute-start | bytes 884744 | tf_op jit(solution)/shard_map/ppermute | solution.py:549
  118.4 11.2 %collective-permute-done.36.b = f32[56,8,128]{2,1,0:T(8,128)S(1)} collective-permute-done((f32[56,8,128]{2,1,0:T(8,128)S(1)}, f32[56,8,128]{2,1,0:T(8,128)S(1)}, u32[]{:S(2)}, u32[]{:S(2)}) %collective-permute-start.36) | collective-permute-done | bytes 229408 | tf_op jit(solution)/shard_map/ppermute | solution.py:544
  129.6 4.8 %collective-permute-done.39.refs_9_ = f32[8,8,128]{2,1,0:T(8,128)S(1)} collective-permute-done((f32[8,8,128]{2,1,0:T(8,128)S(1)}, f32[8,8,128]{2,1,0:T(8,128)S(1)}, u32[]{:S(2)}, u32[]{:S(2)}) %collective-permute-start.39) | collective-permute-done | bytes 32800 | tf_op jit(solution)/shard_map/ppermute | solution.py:540
  134.4 1.2 collective-permute-start.34
  136.2 1.5 collective-permute-start.37
  137.6 2.8 %collective-permute-done.34.refs_5_ = f32[56,8,128]{2,1,0:T(8,128)S(1)} collective-permute-done((f32[56,8,128]{2,1,0:T(8,128)S(1)}, f32[56,8,128]{2,1,0:T(8,128)S(1)}, u32[]{:S(2)}, u32[]{:S(2)}) %collective-permute-start.34) | collective-permute-done | bytes 229408 | tf_op jit(solution)/shard_map/ppermute | solution.py:544
  140.4 6.2 %collective-permute-done.35.refs_6_ = f32[56,8,128]{2,1,0:T(8,128)S(1)} collective-permute-done((f32[56,8,128]{2,1,0:T(8,128)S(1)}, f32[56,8,128]{2,1,0:T(8,128)S(1)}, u32[]{:S(2)}, u32[]{:S(2)}) %collective-permute-start.35) | collective-permute-done | bytes 229408 | tf_op jit(solution)/shard_map/ppermute | solution.py:549
  146.6 1.1 shard_map.106
  (53 shorter events, 6.2 us)
Async XLA Ops:
  1.6 4.4 %collective-permute-start = (f32[16,8,128]{2,1,0:T(8,128)S(1)}, f32[16,8,128]{2,1,0:T(8,128)S(1)}, u32[]{:S(2)}, u32[]{:S(2)}) collective-permute-start(f32[16,8,128]{2,1,0:T(8,128)S(1)} %get-tuple-element.74), channel_id=1, source_target_pairs={{0,1},{1,2},{2,3},{3,0},{4,5},{5,6},{6,7},{7,4},{8,9},{9,10},{10,1... | collective-permute-start | bytes 196616 | tf_op jit(solution)/shard_map/ppermute | solution.py:540
  2.2 4.4 %collective-permute-start.1 = (f32[16,8,128]{2,1,0:T(8,128)S(1)}, f32[16,8,128]{2,1,0:T(8,128)S(1)}, u32[]{:S(2)}, u32[]{:S(2)}) collective-permute-start(f32[16,8,128]{2,1,0:T(8,128)S(1)} %get-tuple-element.75), channel_id=1, source_target_pairs={{0,3},{1,0},{2,1},{3,2},{4,7},{5,4},{6,5},{7,6},{8,11},{9,8},{10,9... | collective-permute-start | bytes 196616 | tf_op jit(solution)/shard_map/ppermute | solution.py:540
  6.6 12.8 %collective-permute-start.10 = (f32[20,8,128]{2,1,0:T(8,128)S(1)}, f32[20,8,128]{2,1,0:T(8,128)S(1)}, u32[]{:S(2)}, u32[]{:S(2)}) collective-permute-start(f32[20,8,128]{2,1,0:T(8,128)S(1)} %get-tuple-element.95), channel_id=1, source_target_pairs={{0,28},{4,0},{8,4},{12,8},{16,12},{20,16},{24,20},{28,24},{1,29},{... | collective-permute-start | bytes 245768 | tf_op jit(solution)/shard_map/ppermute | solution.py:540
  11.5 7.9 %collective-permute-start.9 = (f32[20,8,128]{2,1,0:T(8,128)S(1)}, f32[20,8,128]{2,1,0:T(8,128)S(1)}, u32[]{:S(2)}, u32[]{:S(2)}) collective-permute-start(f32[20,8,128]{2,1,0:T(8,128)S(1)} %get-tuple-element.94), channel_id=1, source_target_pairs={{0,4},{4,8},{8,12},{12,16},{16,20},{20,24},{24,28},{28,0},{1,5},{5... | collective-permute-start | bytes 245768 | tf_op jit(solution)/shard_map/ppermute | solution.py:540
  17.6 17.5 %collective-permute-start.2 = (f32[73,8,128]{2,1,0:T(8,128)S(1)}, f32[73,8,128]{2,1,0:T(8,128)S(1)}, u32[]{:S(2)}, u32[]{:S(2)}) collective-permute-start(f32[73,8,128]{2,1,0:T(8,128)S(1)} %get-tuple-element.86), channel_id=1, source_target_pairs={{0,1},{1,2},{2,3},{3,0},{4,5},{5,6},{6,7},{7,4},{8,9},{9,10},{10,1... | collective-permute-start | bytes 897032 | tf_op jit(solution)/shard_map/ppermute | solution.py:540
  19.0 16.2 %collective-permute-start.3 = (f32[73,8,128]{2,1,0:T(8,128)S(1)}, f32[73,8,128]{2,1,0:T(8,128)S(1)}, u32[]{:S(2)}, u32[]{:S(2)}) collective-permute-start(f32[73,8,128]{2,1,0:T(8,128)S(1)} %get-tuple-element.87), channel_id=1, source_target_pairs={{0,3},{1,0},{2,1},{3,2},{4,7},{5,4},{6,5},{7,6},{8,11},{9,8},{10,9... | collective-permute-start | bytes 897032 | tf_op jit(solution)/shard_map/ppermute | solution.py:540
  22.1 17.9 %collective-permute-start.11 = (f32[81,8,128]{2,1,0:T(8,128)S(1)}, f32[81,8,128]{2,1,0:T(8,128)S(1)}, u32[]{:S(2)}, u32[]{:S(2)}) collective-permute-start(f32[81,8,128]{2,1,0:T(8,128)S(1)} %get-tuple-element.106), channel_id=1, source_target_pairs={{0,1},{1,2},{2,3},{3,0},{4,5},{5,6},{6,7},{7,4},{8,9},{9,10},{10,1... | collective-permute-start | bytes 995336 | tf_op jit(solution)/shard_map/ppermute | solution.py:540
  22.2 17.8 %collective-permute-start.12 = (f32[81,8,128]{2,1,0:T(8,128)S(1)}, f32[81,8,128]{2,1,0:T(8,128)S(1)}, u32[]{:S(2)}, u32[]{:S(2)}) collective-permute-start(f32[81,8,128]{2,1,0:T(8,128)S(1)} %get-tuple-element.107), channel_id=1, source_target_pairs={{0,3},{1,0},{2,1},{3,2},{4,7},{5,4},{6,5},{7,6},{8,11},{9,8},{10,9... | collective-permute-start | bytes 995336 | tf_op jit(solution)/shard_map/ppermute | solution.py:540
  23.9 11.3 %collective-permute-start.4 = (f32[11,8,128]{2,1,0:T(8,128)S(1)}, f32[11,8,128]{2,1,0:T(8,128)S(1)}, u32[]{:S(2)}, u32[]{:S(2)}) collective-permute-start(f32[11,8,128]{2,1,0:T(8,128)S(1)} %get-tuple-element.88), channel_id=1, source_target_pairs={{0,2},{1,3},{2,0},{3,1},{4,6},{5,7},{6,4},{7,5},{8,10},{9,11},{10,... | collective-permute-start | bytes 135176 | tf_op jit(solution)/shard_map/ppermute | solution.py:540
  35.7 10.7 %collective-permute-start.7 = (f32[72,8,128]{2,1,0:T(8,128)S(1)}, f32[72,8,128]{2,1,0:T(8,128)S(1)}, u32[]{:S(2)}, u32[]{:S(2)}) collective-permute-start(f32[72,8,128]{2,1,0:T(8,128)S(1)} %get-tuple-element.93), channel_id=1, source_target_pairs={{0,4},{4,0},{8,12},{12,8},{16,20},{20,16},{24,28},{28,24},{1,5},{5... | collective-permute-start | bytes 884744 | tf_op jit(solution)/shard_map/ppermute | solution.py:544
  35.8 4.2 %collective-permute-start.13 = (f32[12,8,128]{2,1,0:T(8,128)S(1)}, f32[12,8,128]{2,1,0:T(8,128)S(1)}, u32[]{:S(2)}, u32[]{:S(2)}) collective-permute-start(f32[12,8,128]{2,1,0:T(8,128)S(1)} %get-tuple-element.108), channel_id=1, source_target_pairs={{0,2},{1,3},{2,0},{3,1},{4,6},{5,7},{6,4},{7,5},{8,10},{9,11},{10,... | collective-permute-start | bytes 147464 | tf_op jit(solution)/shard_map/ppermute | solution.py:540
  37.4 29.4 %collective-permute-start.5 = (f32[72,8,128]{2,1,0:T(8,128)S(1)}, f32[72,8,128]{2,1,0:T(8,128)S(1)}, u32[]{:S(2)}, u32[]{:S(2)}) collective-permute-start(f32[72,8,128]{2,1,0:T(8,128)S(1)} %get-tuple-element.90), channel_id=1, source_target_pairs={{0,4},{4,0},{8,12},{12,8},{16,20},{20,16},{24,28},{28,24},{1,5},{5... | collective-permute-start | bytes 884744 | tf_op jit(solution)/shard_map/ppermute | solution.py:544
  40.6 15.1 %collective-permute-start.16 = (f32[56,8,128]{2,1,0:T(8,128)S(1)}, f32[56,8,128]{2,1,0:T(8,128)S(1)}, u32[]{:S(2)}, u32[]{:S(2)}) collective-permute-start(f32[56,8,128]{2,1,0:T(8,128)S(1)} %get-tuple-element.113), channel_id=1, source_target_pairs={{0,4},{4,0},{8,12},{12,8},{16,20},{20,16},{24,28},{28,24},{1,5},{5... | collective-permute-start | bytes 688136 | tf_op jit(solution)/shard_map/ppermute | solution.py:544
  42.6 20.3 %collective-permute-start.18 = (f32[16,8,128]{2,1,0:T(8,128)S(1)}, f32[16,8,128]{2,1,0:T(8,128)S(1)}, u32[]{:S(2)}, u32[]{:S(2)}) collective-permute-start(f32[16,8,128]{2,1,0:T(8,128)S(1)} %get-tuple-element.114), channel_id=1, source_target_pairs={{0,12},{4,16},{8,20},{12,24},{16,28},{20,0},{24,4},{28,8},{1,13},{... | collective-permute-start | bytes 196616 | tf_op jit(solution)/shard_map/ppermute | solution.py:540
  43.5 23.3 %collective-permute-start.6 = (f32[72,8,128]{2,1,0:T(8,128)S(1)}, f32[72,8,128]{2,1,0:T(8,128)S(1)}, u32[]{:S(2)}, u32[]{:S(2)}) collective-permute-start(f32[72,8,128]{2,1,0:T(8,128)S(1)} %get-tuple-element.91), channel_id=1, source_target_pairs={{0,24},{4,12},{8,0},{12,20},{16,8},{20,28},{24,16},{28,4},{1,25},{... | collective-permute-start | bytes 884744 | tf_op jit(solution)/shard_map/ppermute | solution.py:549
  46.4 28.2 %collective-permute-start.8 = (f32[72,8,128]{2,1,0:T(8,128)S(1)}, f32[72,8,128]{2,1,0:T(8,128)S(1)}, u32[]{:S(2)}, u32[]{:S(2)}) collective-permute-start(f32[72,8,128]{2,1,0:T(8,128)S(1)} %shard_map.91), channel_id=1, source_target_pairs={{0,8},{4,28},{8,16},{12,4},{16,24},{20,12},{24,0},{28,20},{1,9},{5... | collective-permute-start | bytes 884744 | tf_op jit(solution)/shard_map/ppermute | solution.py:549
  55.6 4.8 %collective-permute-start.19 = (f32[8,8,128]{2,1,0:T(8,128)S(1)}, f32[8,8,128]{2,1,0:T(8,128)S(1)}, u32[]{:S(2)}, u32[]{:S(2)}) collective-permute-start(f32[8,8,128]{2,1,0:T(8,128)S(1)} %get-tuple-element.115), channel_id=1, source_target_pairs={{0,20},{4,24},{8,28},{12,0},{16,4},{20,8},{24,12},{28,16},{1,21},{... | collective-permute-start | bytes 98312 | tf_op jit(solution)/shard_map/ppermute | solution.py:540
  60.4 7.6 %collective-permute-start.14 = (f32[56,8,128]{2,1,0:T(8,128)S(1)}, f32[56,8,128]{2,1,0:T(8,128)S(1)}, u32[]{:S(2)}, u32[]{:S(2)}) collective-permute-start(f32[56,8,128]{2,1,0:T(8,128)S(1)} %get-tuple-element.110), channel_id=1, source_target_pairs={{0,4},{4,0},{8,12},{12,8},{16,20},{20,16},{24,28},{28,24},{1,5},{5... | collective-permute-start | bytes 688136 | tf_op jit(solution)/shard_map/ppermute | solution.py:544
  62.8 9.1 %collective-permute-start.15 = (f32[56,8,128]{2,1,0:T(8,128)S(1)}, f32[56,8,128]{2,1,0:T(8,128)S(1)}, u32[]{:S(2)}, u32[]{:S(2)}) collective-permute-start(f32[56,8,128]{2,1,0:T(8,128)S(1)} %get-tuple-element.111), channel_id=1, source_target_pairs={{0,24},{4,12},{8,0},{12,20},{16,8},{20,28},{24,16},{28,4},{1,25},{... | collective-permute-start | bytes 688136 | tf_op jit(solution)/shard_map/ppermute | solution.py:549
  66.7 7.9 %collective-permute-start.17 = (f32[56,8,128]{2,1,0:T(8,128)S(1)}, f32[56,8,128]{2,1,0:T(8,128)S(1)}, u32[]{:S(2)}, u32[]{:S(2)}) collective-permute-start(f32[56,8,128]{2,1,0:T(8,128)S(1)} %shard_map.96), channel_id=1, source_target_pairs={{0,8},{4,28},{8,16},{12,4},{16,24},{20,12},{24,0},{28,20},{1,9},{5... | collective-permute-start | bytes 688136 | tf_op jit(solution)/shard_map/ppermute | solution.py:549
  74.9 3.7 %collective-permute-start.20 = (f32[16,8,128]{2,1,0:T(8,128)S(1)}, f32[16,8,128]{2,1,0:T(8,128)S(1)}, u32[]{:S(2)}, u32[]{:S(2)}) collective-permute-start(f32[16,8,128]{2,1,0:T(8,128)S(1)} %get-tuple-element.117), channel_id=1, source_target_pairs={{0,1},{1,2},{2,3},{3,0},{4,5},{5,6},{6,7},{7,4},{8,9},{9,10},{10,1... | collective-permute-start | bytes 196616 | tf_op jit(solution)/shard_map/ppermute | solution.py:540
  74.9 4.2 %collective-permute-start.21 = (f32[16,8,128]{2,1,0:T(8,128)S(1)}, f32[16,8,128]{2,1,0:T(8,128)S(1)}, u32[]{:S(2)}, u32[]{:S(2)}) collective-permute-start(f32[16,8,128]{2,1,0:T(8,128)S(1)} %get-tuple-element.118), channel_id=1, source_target_pairs={{0,3},{1,0},{2,1},{3,2},{4,7},{5,4},{6,5},{7,6},{8,11},{9,8},{10,9... | collective-permute-start | bytes 196616 | tf_op jit(solution)/shard_map/ppermute | solution.py:540
  79.1 12.7 %collective-permute-start.29 = (f32[20,8,128]{2,1,0:T(8,128)S(1)}, f32[20,8,128]{2,1,0:T(8,128)S(1)}, u32[]{:S(2)}, u32[]{:S(2)}) collective-permute-start(f32[20,8,128]{2,1,0:T(8,128)S(1)} %get-tuple-element.128), channel_id=1, source_target_pairs={{0,4},{4,8},{8,12},{12,16},{16,20},{20,24},{24,28},{28,0},{1,5},{5... | collective-permute-start | bytes 245768 | tf_op jit(solution)/shard_map/ppermute | solution.py:540
  79.2 12.6 %collective-permute-start.30 = (f32[20,8,128]{2,1,0:T(8,128)S(1)}, f32[20,8,128]{2,1,0:T(8,128)S(1)}, u32[]{:S(2)}, u32[]{:S(2)}) collective-permute-start(f32[20,8,128]{2,1,0:T(8,128)S(1)} %get-tuple-element.129), channel_id=1, source_target_pairs={{0,28},{4,0},{8,4},{12,8},{16,12},{20,16},{24,20},{28,24},{1,29},{... | collective-permute-start | bytes 245768 | tf_op jit(solution)/shard_map/ppermute | solution.py:540
  89.9 17.5 %collective-permute-start.22 = (f32[73,8,128]{2,1,0:T(8,128)S(1)}, f32[73,8,128]{2,1,0:T(8,128)S(1)}, u32[]{:S(2)}, u32[]{:S(2)}) collective-permute-start(f32[73,8,128]{2,1,0:T(8,128)S(1)} %get-tuple-element.120), channel_id=1, source_target_pairs={{0,1},{1,2},{2,3},{3,0},{4,5},{5,6},{6,7},{7,4},{8,9},{9,10},{10,1... | collective-permute-start | bytes 897032 | tf_op jit(solution)/shard_map/ppermute | solution.py:540
  91.4 16.0 %collective-permute-start.23 = (f32[73,8,128]{2,1,0:T(8,128)S(1)}, f32[73,8,128]{2,1,0:T(8,128)S(1)}, u32[]{:S(2)}, u32[]{:S(2)}) collective-permute-start(f32[73,8,128]{2,1,0:T(8,128)S(1)} %get-tuple-element.121), channel_id=1, source_target_pairs={{0,3},{1,0},{2,1},{3,2},{4,7},{5,4},{6,5},{7,6},{8,11},{9,8},{10,9... | collective-permute-start | bytes 897032 | tf_op jit(solution)/shard_map/ppermute | solution.py:540
  94.2 18.1 %collective-permute-start.31 = (f32[81,8,128]{2,1,0:T(8,128)S(1)}, f32[81,8,128]{2,1,0:T(8,128)S(1)}, u32[]{:S(2)}, u32[]{:S(2)}) collective-permute-start(f32[81,8,128]{2,1,0:T(8,128)S(1)} %get-tuple-element.134), channel_id=1, source_target_pairs={{0,1},{1,2},{2,3},{3,0},{4,5},{5,6},{6,7},{7,4},{8,9},{9,10},{10,1... | collective-permute-start | bytes 995336 | tf_op jit(solution)/shard_map/ppermute | solution.py:540
  95.2 17.1 %collective-permute-start.32 = (f32[81,8,128]{2,1,0:T(8,128)S(1)}, f32[81,8,128]{2,1,0:T(8,128)S(1)}, u32[]{:S(2)}, u32[]{:S(2)}) collective-permute-start(f32[81,8,128]{2,1,0:T(8,128)S(1)} %get-tuple-element.135), channel_id=1, source_target_pairs={{0,3},{1,0},{2,1},{3,2},{4,7},{5,4},{6,5},{7,6},{8,11},{9,8},{10,9... | collective-permute-start | bytes 995336 | tf_op jit(solution)/shard_map/ppermute | solution.py:540
  96.0 11.5 %collective-permute-start.24 = (f32[11,8,128]{2,1,0:T(8,128)S(1)}, f32[11,8,128]{2,1,0:T(8,128)S(1)}, u32[]{:S(2)}, u32[]{:S(2)}) collective-permute-start(f32[11,8,128]{2,1,0:T(8,128)S(1)} %get-tuple-element.122), channel_id=1, source_target_pairs={{0,2},{1,3},{2,0},{3,1},{4,6},{5,7},{6,4},{7,5},{8,10},{9,11},{10,... | collective-permute-start | bytes 135176 | tf_op jit(solution)/shard_map/ppermute | solution.py:540
  108.0 10.3 %collective-permute-start.27 = (f32[72,8,128]{2,1,0:T(8,128)S(1)}, f32[72,8,128]{2,1,0:T(8,128)S(1)}, u32[]{:S(2)}, u32[]{:S(2)}) collective-permute-start(f32[72,8,128]{2,1,0:T(8,128)S(1)} %get-tuple-element.127), channel_id=1, source_target_pairs={{0,4},{4,0},{8,12},{12,8},{16,20},{20,16},{24,28},{28,24},{1,5},{5... | collective-permute-start | bytes 884744 | tf_op jit(solution)/shard_map/ppermute | solution.py:544
  108.1 4.2 %collective-permute-start.33 = (f32[12,8,128]{2,1,0:T(8,128)S(1)}, f32[12,8,128]{2,1,0:T(8,128)S(1)}, u32[]{:S(2)}, u32[]{:S(2)}) collective-permute-start(f32[12,8,128]{2,1,0:T(8,128)S(1)} %get-tuple-element.136), channel_id=1, source_target_pairs={{0,2},{1,3},{2,0},{3,1},{4,6},{5,7},{6,4},{7,5},{8,10},{9,11},{10,... | collective-permute-start | bytes 147464 | tf_op jit(solution)/shard_map/ppermute | solution.py:540
  110.2 25.9 %collective-permute-start.25 = (f32[72,8,128]{2,1,0:T(8,128)S(1)}, f32[72,8,128]{2,1,0:T(8,128)S(1)}, u32[]{:S(2)}, u32[]{:S(2)}) collective-permute-start(f32[72,8,128]{2,1,0:T(8,128)S(1)} %get-tuple-element.124), channel_id=1, source_target_pairs={{0,4},{4,0},{8,12},{12,8},{16,20},{20,16},{24,28},{28,24},{1,5},{5... | collective-permute-start | bytes 884744 | tf_op jit(solution)/shard_map/ppermute | solution.py:544
  112.9 16.7 %collective-permute-start.36 = (f32[56,8,128]{2,1,0:T(8,128)S(1)}, f32[56,8,128]{2,1,0:T(8,128)S(1)}, u32[]{:S(2)}, u32[]{:S(2)}) collective-permute-start(f32[56,8,128]{2,1,0:T(8,128)S(1)} %get-tuple-element.141), channel_id=1, source_target_pairs={{0,4},{4,0},{8,12},{12,8},{16,20},{20,16},{24,28},{28,24},{1,5},{5... | collective-permute-start | bytes 688136 | tf_op jit(solution)/shard_map/ppermute | solution.py:544
  114.9 20.7 %collective-permute-start.38 = (f32[16,8,128]{2,1,0:T(8,128)S(1)}, f32[16,8,128]{2,1,0:T(8,128)S(1)}, u32[]{:S(2)}, u32[]{:S(2)}) collective-permute-start(f32[16,8,128]{2,1,0:T(8,128)S(1)} %get-tuple-element.142), channel_id=1, source_target_pairs={{0,12},{4,16},{8,20},{12,24},{16,28},{20,0},{24,4},{28,8},{1,13},{... | collective-permute-start | bytes 196616 | tf_op jit(solution)/shard_map/ppermute | solution.py:540
  114.9 22.7 %collective-permute-start.26 = (f32[72,8,128]{2,1,0:T(8,128)S(1)}, f32[72,8,128]{2,1,0:T(8,128)S(1)}, u32[]{:S(2)}, u32[]{:S(2)}) collective-permute-start(f32[72,8,128]{2,1,0:T(8,128)S(1)} %get-tuple-element.125), channel_id=1, source_target_pairs={{0,24},{4,12},{8,0},{12,20},{16,8},{20,28},{24,16},{28,4},{1,25},{... | collective-permute-start | bytes 884744 | tf_op jit(solution)/shard_map/ppermute | solution.py:549
  118.3 28.3 %collective-permute-start.28 = (f32[72,8,128]{2,1,0:T(8,128)S(1)}, f32[72,8,128]{2,1,0:T(8,128)S(1)}, u32[]{:S(2)}, u32[]{:S(2)}) collective-permute-start(f32[72,8,128]{2,1,0:T(8,128)S(1)} %shard_map.101), channel_id=1, source_target_pairs={{0,8},{4,28},{8,16},{12,4},{16,24},{20,12},{24,0},{28,20},{1,9},{5... | collective-permute-start | bytes 884744 | tf_op jit(solution)/shard_map/ppermute | solution.py:549
  129.6 4.8 %collective-permute-start.39 = (f32[8,8,128]{2,1,0:T(8,128)S(1)}, f32[8,8,128]{2,1,0:T(8,128)S(1)}, u32[]{:S(2)}, u32[]{:S(2)}) collective-permute-start(f32[8,8,128]{2,1,0:T(8,128)S(1)} %get-tuple-element.143), channel_id=1, source_target_pairs={{0,20},{4,24},{8,28},{12,0},{16,4},{20,8},{24,12},{28,16},{1,21},{... | collective-permute-start | bytes 98312 | tf_op jit(solution)/shard_map/ppermute | solution.py:540
  134.4 6.0 %collective-permute-start.34 = (f32[56,8,128]{2,1,0:T(8,128)S(1)}, f32[56,8,128]{2,1,0:T(8,128)S(1)}, u32[]{:S(2)}, u32[]{:S(2)}) collective-permute-start(f32[56,8,128]{2,1,0:T(8,128)S(1)} %get-tuple-element.138), channel_id=1, source_target_pairs={{0,4},{4,0},{8,12},{12,8},{16,20},{20,16},{24,28},{28,24},{1,5},{5... | collective-permute-start | bytes 688136 | tf_op jit(solution)/shard_map/ppermute | solution.py:544
  135.6 11.0 %collective-permute-start.35 = (f32[56,8,128]{2,1,0:T(8,128)S(1)}, f32[56,8,128]{2,1,0:T(8,128)S(1)}, u32[]{:S(2)}, u32[]{:S(2)}) collective-permute-start(f32[56,8,128]{2,1,0:T(8,128)S(1)} %get-tuple-element.139), channel_id=1, source_target_pairs={{0,24},{4,12},{8,0},{12,20},{16,8},{20,28},{24,16},{28,4},{1,25},{... | collective-permute-start | bytes 688136 | tf_op jit(solution)/shard_map/ppermute | solution.py:549
  136.2 10.5 %collective-permute-start.37 = (f32[56,8,128]{2,1,0:T(8,128)S(1)}, f32[56,8,128]{2,1,0:T(8,128)S(1)}, u32[]{:S(2)}, u32[]{:S(2)}) collective-permute-start(f32[56,8,128]{2,1,0:T(8,128)S(1)} %shard_map.105), channel_id=1, source_target_pairs={{0,8},{4,28},{8,16},{12,4},{16,24},{20,12},{24,0},{28,20},{1,9},{5... | collective-permute-start | bytes 688136 | tf_op jit(solution)/shard_map/ppermute | solution.py:549

commit v5 on v4

--- a/solution.py
+++ b/solution.py
@@ -412,19 +412,20 @@
     spread(cx, pairs, rows_of, count, 0, g, w, moves, step, o, r, l, far)
 
 
-def outer_body(cx, pairs, step, rows_of, count, *refs):
+def outer_body(cx, pairs, step, runs, *refs):
     own, halos, coefs, outer = refs[0], refs[1:5], refs[5:11], refs[11:17]
     mid_inner, g_inner, w, moves = refs[17:21]
-    o, r, l, far, pad, mid, g = refs[21:]
+    outs, (pad, mid, g) = refs[21:29], refs[29:]
     diffuse_outer(cx, pairs, own, *halos, coefs, outer, mid_inner, g_inner, pad, mid, g)
-    spread(cx, pairs, rows_of, count, 3, g, w, moves, step, o, r, l, far)
+    for n, (rows_of, count) in enumerate(runs):
+        spread(cx, pairs, rows_of, count, 3, g, w, moves, step, *outs[4 * n : 4 * n + 4])
 
 
 def gather_body(pairs, step, main, rims, *refs):
     own, right, left, far_low, far_high, own_moves = refs[:6]
     outs = refs[6:11]
     count = own.shape[0] // pairs
-    skip = 3 if rims else 0
+    skip = len(rims)
     mine = own_moves[step]
     moves = (mine, right[count * pairs], left[count * pairs])
     far_moves = (far_low[count], far_high[count])
@@ -457,20 +458,14 @@
             return 0
 
         lax.fori_loop(0, main, row, 0)
-        if rims:
-            for source, row_at, step_to in ((0, 0, -1), (1, 1, -1), (2, main - 1, 1)):
-                masks, fars = masks_of(t + step_to)
-                for q in range(pairs):
-                    out[row_at * pairs + q] = out[row_at * pairs + q] + total(masks, fars, source, q)
-    if rims:
-        high, low = refs[11:]
-        masks, fars = masks_of(jnp.int32(2))
-        for k in range(2):
+        for source, (row_at, step_to) in enumerate(rims):
+            masks, fars = masks_of(t + step_to)
             for q in range(pairs):
-                high[k * pairs + q] = total(masks, fars, k, q)
-        masks, fars = masks_of(jnp.int32(-2))
+                out[row_at * pairs + q] = out[row_at * pairs + q] + total(masks, fars, source, q)
+    for source, (_, step_to) in enumerate(rims):
+        masks, fars = masks_of(jnp.int32(-2 * step_to))
         for q in range(pairs):
-            low[q] = total(masks, fars, 2, q)
+            refs[11][source * pairs + q] = total(masks, fars, source, q)
 
 
 def add_body(a, b, out):
@@ -485,7 +480,7 @@
 
 
 def merge(cx, pairs, chunks, parts, put):
-    for runs, (t0, e0, f, d) in zip(chunks, (parts[0:4], parts[4:8])):
+    for runs, (t0, e0, f, d) in zip(chunks, (parts[0:4], parts[4:8], parts[8:12])):
         for local, base, rows in runs:
 
             def row(i, _, t0=t0, e0=e0, f=f, d=d, local=local, base=base):
@@ -495,7 +490,7 @@
                 return 0
 
             lax.fori_loop(0, rows, row, 0)
-    high, low = parts[8:10]
+    high, low = parts[12:14]
     for q in range(pairs):
         for k in range(2):
             put(k, q, high[k * pairs + q], True)
@@ -503,8 +498,8 @@
 
 
 def merge_body(cx, pairs, chunks, *refs):
-    parts = refs[:10]
-    out, left, right = refs[10:]
+    parts = refs[:14]
+    out, left, right = refs[14:]
 
     def put(x, q, v, add):
         at = x * pairs + q
@@ -517,8 +512,8 @@
 
 
 def finish_body(cx, cy, pairs, chunks, *refs):
-    parts = refs[:10]
-    level, vel, out = refs[10:]
+    parts = refs[:14]
+    level, vel, out = refs[14:]
 
     def put(x, q, v, add):
         at = pl.ds(SUB * q, SUB)
@@ -607,21 +602,21 @@
 
     inner = 4
     count_a = cx - 2 * inner + 1
-    main = (count_a, cx - count_a)
-    chunk_runs = (
-        ((0, inner, count_a),),
-        ((0, 0, inner), (inner, inner + count_a, cx - inner - count_a)),
-    )
+    behind = inner + count_a
+    main = (count_a, inner, cx - behind)
+    chunk_runs = (((0, inner, main[0]),), ((0, 0, main[1]),), ((0, behind, main[2]),))
 
     def rows_a(i):
         return i + inner
 
     def rows_b(i):
-        k = i - 3
-        body = jnp.where(k < inner, k, k + count_a)
-        return jnp.where(i < 2, cx + i, jnp.where(i < 3, -1, body))
-
-    counts = (main[0], main[1] + 3)
+        return jnp.where(i < 2, cx + i, i - 2)
+
+    def rows_c(i):
+        return jnp.where(i < 1, -1, i - 1 + behind)
+
+    counts = (main[0], main[1] + 2, main[2] + 1)
+    rims_of = ((), ((0, -1), (1, -1)), ((main[2] - 1, 1),))
 
     def outs(n):
         return [plane(n * pairs), plane(n * pairs + 1), plane(n * pairs + 1), plane(n + 2)]
@@ -664,24 +659,24 @@
                 [scratch(8 * wide)],
             )
         sent_b = call(
-            functools.partial(outer_body, cx, pairs, step, rows_b, counts[1]),
-            outs(counts[1]),
+            functools.partial(outer_body, cx, pairs, step, ((rows_b, counts[1]), (rows_c, counts[2]))),
+            outs(counts[1]) + outs(counts[2]),
             (state, xm, xp, ym, yp, *coefs, *outer, mid, g, weights[step], own_moves),
             [VMEM] * 21,
             [scratch(8 * wide), scratch(8 * wide), scratch((cx + 6) * pairs)],
             flops=10000000,
         )
-        chunks = []
-        for n, (own, right, left, far) in enumerate((sent_a, sent_b)):
+        chunks, rims = [], []
+        for n, (own, right, left, far) in enumerate((sent_a, sent_b[:4], sent_b[4:])):
             if n:
-                own, _ = lax.optimization_barrier((own, chunks[0]))
+                own, _ = lax.optimization_barrier((own, chunks[-4]))
             right = moved(right, "gy", 1)
             left = moved(left, "gy", -1)
             far_low = moved(far, "gy", 2)
             far_high = far_low if ny == 4 else moved(far, "gy", -2)
-            e1, e0, f, k, t0, *rims = call(
-                functools.partial(gather_body, pairs, step, main[n], n == 1),
-                [plane(main[n] * pairs)] * 5 + ([plane(2 * pairs), plane(pairs)] if n else []),
+            e1, e0, f, k, t0, *rim = call(
+                functools.partial(gather_body, pairs, step, main[n], rims_of[n]),
+                [plane(main[n] * pairs)] * 5 + ([plane(len(rims_of[n]) * pairs)] if n else []),
                 (own, right, left, far_low, far_high, own_moves),
                 [VMEM] * 6,
                 flops=3000000,
@@ -692,6 +687,7 @@
             (d,) = call(add_body, [plane(main[n] * pairs)], (k, e1), [VMEM] * 2)
             d = crossed(d, -1)
             chunks += [t0, e0, f, d]
+            rims += rim
         high, low = rims
         high = moved(high, "gx", 3)
         low = moved(low, "gx", -3)
@@ -701,14 +697,14 @@
                 functools.partial(merge_body, cx, pairs, chunk_runs),
                 [plane(cx * pairs)] + [plane(cx)] * 2,
                 chunks,
-                [VMEM] * 10,
+                [VMEM] * 14,
             )
         else:
             return call(
                 functools.partial(finish_body, cx, cy, pairs, chunk_runs),
                 [f32(cx, cy, cz), f32(3, cx, cy, cz)],
                 chunks,
-                [VMEM] * 10,
+                [VMEM] * 14,
                 [pltpu.VMEM((cx, FIELDS * cy, cz), jnp.float32)],
             )
 

time: 148 us -> 162 us (1.095)
  starting transfers between devices: 55.2 us -> 66.9 us
  waiting for transfers between devices: 67.8 us -> 70.1 us
    ppermute x8 -> x12, waiting for transfers between devices: 24.8 us -> 5.84 us  [swapped(): lax.ppermute(value, 'gx', [(i, i ^ 1) for i in range(lax.axis_size('gx'))])]
    ppermute x8 -> x12, waiting for transfers between devices: 12.8 us -> 31.3 us  [crossed(): lax.ppermute(value, 'gx', [(i, (i + (2 if i % 2 else -2) * sign) % count)...]
    ppermute x8 -> x12, starting transfers between devices: 11.6 us -> 19.9 us  [swapped(): lax.ppermute(value, 'gx', [(i, i ^ 1) for i in range(lax.axis_size('gx'))])]
    ppermute x8 -> x12, starting transfers between devices: 11.9 us -> 16.2 us  [crossed(): lax.ppermute(value, 'gx', [(i, (i + (2 if i % 2 else -2) * sign) % count)...]
    ppermute x24 -> x30, waiting for transfers between devices: 30.1 us -> 33 us  [moved(): lax.ppermute(value, axis, [(i, (i + steps) % count) for i in range(count)])]
    ppermute x24 -> x30, starting transfers between devices: 31.7 us -> 30.8 us  [moved(): lax.ppermute(value, axis, [(i, (i + steps) % count) for i in range(count)])]
    pallas_call x21 -> x25, Pallas kernels: 23.8 us -> 23.8 us  [call(): pl.pallas_call(body, out_shape=tuple(outs), in_specs=list(specs), out_spe...]
  transfers between devices with their start and end apart: 40 -> 54, of which waited for: 18 -> 18; matrix products, arithmetic and copies ran while one was open for 0% -> 0% of each run, Pallas kernels for 15% -> 7%
where the time goes in v5:
time: 162 us
  waiting for transfers between devices  70.1 us (43%)
  starting transfers between devices  66.9 us (41%)
  Pallas kernels  23.8 us (15%)
    ppermute x30, waiting for transfers between devices, moved(): lax.ppermute(value, axis, [(i, (i + steps) % count) for i in range(count)])  33 us
    ppermute x12, waiting for transfers between devices, crossed(): lax.ppermute(value, 'gx', [(i, (i + (2 if i % 2 else -2) * sign) % count)...  31.3 us
    ppermute x30, starting transfers between devices, moved(): lax.ppermute(value, axis, [(i, (i + steps) % count) for i in range(count)])  30.8 us
    pallas_call x25, Pallas kernels, call(): pl.pallas_call(body, out_shape=tuple(outs), in_specs=list(specs), out_spe...  23.8 us
    ppermute x12, starting transfers between devices, swapped(): lax.ppermute(value, 'gx', [(i, i ^ 1) for i in range(lax.axis_size('gx'))])  19.9 us
    ppermute x12, starting transfers between devices, crossed(): lax.ppermute(value, 'gx', [(i, (i + (2 if i % 2 else -2) * sign) % count)...  16.2 us
    ppermute x12, waiting for transfers between devices, swapped(): lax.ppermute(value, 'gx', [(i, i ^ 1) for i in range(lax.axis_size('gx'))])  5.84 us
  transfers between devices with their start and end apart: 54, of which 18 were waited for; matrix products, arithmetic and copies ran while one was open for 0% of the time, Pallas kernels for 7%

profile of v5, /device:TPU:0, one launch (start us, length us, event | category | flops | bytes accessed | tf_op | source)
XLA Modules:
  0.0 161.6 jit_solution(8206642920992368071)
XLA Ops:
  2.2 2.0 %collective-permute-start.1 = (f32[16,8,128]{2,1,0:T(8,128)S(1)}, f32[16,8,128]{2,1,0:T(8,128)S(1)}, u32[]{:S(2)}, u32[]{:S(2)}) collective-permute-start(f32[16,8,128]{2,1,0:T(8,128)S(1)} %get-tuple-element.95), channel_id=1, source_target_pairs={{0,3},{1,0},{2,1},{3,2},{4,7},{5,4},{6,5},{7,6},{8,11},{9,8},{10,9... | collective-permute-start | bytes 196616 | tf_op jit(solution)/shard_map/ppermute | solution.py:535
  4.1 1.8 %shard_map.86 = (f32[16,64,128]{2,1,0:T(8,128)S(1)}, f32[16,64,128]{2,1,0:T(8,128)S(1)}, f32[12,129,8,128]{3,2,1,0:T(8,128)S(1)}, f32[4,8,128]{2,1,0:T(8,128)S(1)}) custom-call(f32[16,16,128]{2,1,0:T(8,128)} %refs_0_.1, f32[3,16,16,128]{3,2,1,0:T(8,128)} %vel.1, s32[16,16,128]{2,1,0:T(8,128)} %labels.1, f32[2]{0:T(128)} %rates_at.1, s32[1,1,2]{2,1,0:T(1,128)} %refs_4_.1, ...), custom_call_target="tpu_custom_call" | custom-call | flops 1000000 | bytes 8847384 | tf_op jit(solution)/shard_map/pallas_call | solution.py:21
  6.6 1.6 shard_map.88
  8.1 4.5 %shard_map.89 = (f32[72,8,128]{2,1,0:T(8,128)S(1)}, f32[73,8,128]{2,1,0:T(8,128)S(1)}, f32[73,8,128]{2,1,0:T(8,128)S(1)}, f32[11,8,128]{2,1,0:T(8,128)S(1)}, f32...) custom-call(f32[128,8,128]{2,1,0:T(8,128)S(1)} %bitcast.2, ...), custom_call_target="tpu_custom_call" | custom-call | flops 20000000 | bytes 13594624 | tf_op jit(solution)/shard_map/pallas_call | solution.py:21
  12.7 1.9 %collective-permute-start.2 = (f32[73,8,128]{2,1,0:T(8,128)S(1)}, f32[73,8,128]{2,1,0:T(8,128)S(1)}, u32[]{:S(2)}, u32[]{:S(2)}) collective-permute-start(f32[73,8,128]{2,1,0:T(8,128)S(1)} %get-tuple-element.106), channel_id=1, source_target_pairs={{0,1},{1,2},{2,3},{3,0},{4,5},{5,6},{6,7},{7,4},{8,9},{9,10},{10,1... | collective-permute-start | bytes 897032 | tf_op jit(solution)/shard_map/ppermute | solution.py:535
  14.9 4.5 %collective-permute-start.10 = (f32[20,8,128]{2,1,0:T(8,128)S(1)}, f32[20,8,128]{2,1,0:T(8,128)S(1)}, u32[]{:S(2)}, u32[]{:S(2)}) collective-permute-start(f32[20,8,128]{2,1,0:T(8,128)S(1)} %get-tuple-element.115), channel_id=1, source_target_pairs={{0,28},{4,0},{8,4},{12,8},{16,12},{20,16},{24,20},{28,24},{1,29},{... | collective-permute-start | bytes 245768 | tf_op jit(solution)/shard_map/ppermute | solution.py:535
  19.5 1.5 collective-permute-start.4
  21.0 2.6 %collective-permute-done.4.refs_3_.refs_4_ = f32[11,8,128]{2,1,0:T(8,128)S(1)} collective-permute-done((f32[11,8,128]{2,1,0:T(8,128)S(1)}, f32[11,8,128]{2,1,0:T(8,128)S(1)}, u32[]{:S(2)}, u32[]{:S(2)}) %collective-permute-start.4) | collective-permute-done | bytes 45088 | tf_op jit(solution)/shard_map/ppermute | solution.py:535
  24.1 1.5 collective-permute-start.7
  25.5 1.1 collective-permute-done.9.xm.refs_1_
  26.8 2.5 %shard_map.94 = (f32[48,8,128]{2,1,0:T(8,128)S(1)}, f32[49,8,128]{2,1,0:T(8,128)S(1)}, f32[49,8,128]{2,1,0:T(8,128)S(1)}, f32[8,8,128]{2,1,0:T(8,128)S(1)}, f32[...) custom-call(f32[128,8,128]{2,1,0:T(8,128)S(1)} %bitcast.4, ...), custom_call_target="tpu_custom_call" | custom-call | flops 10000000 | bytes 14942208 | tf_op jit(solution)/shard_map/pallas_call | solution.py:21
  29.4 1.7 %collective-permute-start.12 = (f32[49,8,128]{2,1,0:T(8,128)S(1)}, f32[49,8,128]{2,1,0:T(8,128)S(1)}, u32[]{:S(2)}, u32[]{:S(2)}) collective-permute-start(f32[49,8,128]{2,1,0:T(8,128)S(1)} %get-tuple-element.127), channel_id=1, source_target_pairs={{0,3},{1,0},{2,1},{3,2},{4,7},{5,4},{6,5},{7,6},{8,11},{9,8},{10,9... | collective-permute-start | bytes 602120 | tf_op jit(solution)/shard_map/ppermute | solution.py:535
  31.1 1.4 collective-permute-start.13
  32.5 6.3 %collective-permute-done.13.refs_3_.refs_4_ = f32[8,8,128]{2,1,0:T(8,128)S(1)} collective-permute-done((f32[8,8,128]{2,1,0:T(8,128)S(1)}, f32[8,8,128]{2,1,0:T(8,128)S(1)}, u32[]{:S(2)}, u32[]{:S(2)}) %collective-permute-start.13) | collective-permute-done | bytes 32800 | tf_op jit(solution)/shard_map/ppermute | solution.py:535
  40.0 3.2 %collective-permute-done.20.refs_3_.refs_4_ = f32[6,8,128]{2,1,0:T(8,128)S(1)} collective-permute-done((f32[6,8,128]{2,1,0:T(8,128)S(1)}, f32[6,8,128]{2,1,0:T(8,128)S(1)}, u32[]{:S(2)}, u32[]{:S(2)}) %collective-permute-start.20) | collective-permute-done | bytes 24608 | tf_op jit(solution)/shard_map/ppermute | solution.py:535
  43.4 1.4 collective-permute-start.26
  44.9 2.8 %collective-permute-start.23 = (f32[24,8,128]{2,1,0:T(8,128)S(1)}, f32[24,8,128]{2,1,0:T(8,128)S(1)}, u32[]{:S(2)}, u32[]{:S(2)}) collective-permute-start(f32[24,8,128]{2,1,0:T(8,128)S(1)} %get-tuple-element.143), channel_id=1, source_target_pairs={{0,4},{4,0},{8,12},{12,8},{16,20},{20,16},{24,28},{28,24},{1,5},{5... | collective-permute-start | bytes 294920 | tf_op jit(solution)/shard_map/ppermute | solution.py:539
  47.7 2.0 %collective-permute-start.16 = (f32[32,8,128]{2,1,0:T(8,128)S(1)}, f32[32,8,128]{2,1,0:T(8,128)S(1)}, u32[]{:S(2)}, u32[]{:S(2)}) collective-permute-start(f32[32,8,128]{2,1,0:T(8,128)S(1)} %get-tuple-element.133), channel_id=1, source_target_pairs={{0,4},{4,0},{8,12},{12,8},{16,20},{20,16},{24,28},{28,24},{1,5},{5... | collective-permute-start | bytes 393224 | tf_op jit(solution)/shard_map/ppermute | solution.py:539
  50.0 3.1 %collective-permute-start.22 = (f32[24,8,128]{2,1,0:T(8,128)S(1)}, f32[24,8,128]{2,1,0:T(8,128)S(1)}, u32[]{:S(2)}, u32[]{:S(2)}) collective-permute-start(f32[24,8,128]{2,1,0:T(8,128)S(1)} %get-tuple-element.141), channel_id=1, source_target_pairs={{0,24},{4,12},{8,0},{12,20},{16,8},{20,28},{24,16},{28,4},{1,25},{... | collective-permute-start | bytes 294920 | tf_op jit(solution)/shard_map/ppermute | solution.py:544
  53.1 2.8 %collective-permute-done.25.refs_12_ = f32[16,8,128]{2,1,0:T(8,128)S(1)} collective-permute-done((f32[16,8,128]{2,1,0:T(8,128)S(1)}, f32[16,8,128]{2,1,0:T(8,128)S(1)}, u32[]{:S(2)}, u32[]{:S(2)}) %collective-permute-start.25) | collective-permute-done | bytes 65568 | tf_op jit(solution)/shard_map/ppermute | solution.py:535
  56.8 2.9 %collective-permute-start.6 = (f32[72,8,128]{2,1,0:T(8,128)S(1)}, f32[72,8,128]{2,1,0:T(8,128)S(1)}, u32[]{:S(2)}, u32[]{:S(2)}) collective-permute-start(f32[72,8,128]{2,1,0:T(8,128)S(1)} %get-tuple-element.111), channel_id=1, source_target_pairs={{0,24},{4,12},{8,0},{12,20},{16,8},{20,28},{24,16},{28,4},{1,25},{... | collective-permute-start | bytes 884744 | tf_op jit(solution)/shard_map/ppermute | solution.py:544
  59.7 2.1 %collective-permute-start.14 = (f32[32,8,128]{2,1,0:T(8,128)S(1)}, f32[32,8,128]{2,1,0:T(8,128)S(1)}, u32[]{:S(2)}, u32[]{:S(2)}) collective-permute-start(f32[32,8,128]{2,1,0:T(8,128)S(1)} %get-tuple-element.130), channel_id=1, source_target_pairs={{0,4},{4,0},{8,12},{12,8},{16,20},{20,16},{24,28},{28,24},{1,5},{5... | collective-permute-start | bytes 393224 | tf_op jit(solution)/shard_map/ppermute | solution.py:539
  61.8 2.0 %collective-permute-start.15 = (f32[32,8,128]{2,1,0:T(8,128)S(1)}, f32[32,8,128]{2,1,0:T(8,128)S(1)}, u32[]{:S(2)}, u32[]{:S(2)}) collective-permute-start(f32[32,8,128]{2,1,0:T(8,128)S(1)} %get-tuple-element.131), channel_id=1, source_target_pairs={{0,24},{4,12},{8,0},{12,20},{16,8},{20,28},{24,16},{28,4},{1,25},{... | collective-permute-start | bytes 393224 | tf_op jit(solution)/shard_map/ppermute | solution.py:544
  63.8 1.9 %collective-permute-done.14.refs_5_ = f32[32,8,128]{2,1,0:T(8,128)S(1)} collective-permute-done((f32[32,8,128]{2,1,0:T(8,128)S(1)}, f32[32,8,128]{2,1,0:T(8,128)S(1)}, u32[]{:S(2)}, u32[]{:S(2)}) %collective-permute-start.14) | collective-permute-done | bytes 131104 | tf_op jit(solution)/shard_map/ppermute | solution.py:539
  66.2 8.9 %collective-permute-done.15.refs_6_ = f32[32,8,128]{2,1,0:T(8,128)S(1)} collective-permute-done((f32[32,8,128]{2,1,0:T(8,128)S(1)}, f32[32,8,128]{2,1,0:T(8,128)S(1)}, u32[]{:S(2)}, u32[]{:S(2)}) %collective-permute-start.15) | collective-permute-done | bytes 131104 | tf_op jit(solution)/shard_map/ppermute | solution.py:544
  75.2 6.9 %collective-permute-done.24.refs_11_ = f32[24,8,128]{2,1,0:T(8,128)S(1)} collective-permute-done((f32[24,8,128]{2,1,0:T(8,128)S(1)}, f32[24,8,128]{2,1,0:T(8,128)S(1)}, u32[]{:S(2)}, u32[]{:S(2)}) %collective-permute-start.24) | collective-permute-done | bytes 98336 | tf_op jit(solution)/shard_map/ppermute | solution.py:544
  82.3 1.7 %collective-permute-start.28 = (f32[16,8,128]{2,1,0:T(8,128)S(1)}, f32[16,8,128]{2,1,0:T(8,128)S(1)}, u32[]{:S(2)}, u32[]{:S(2)}) collective-permute-start(f32[16,8,128]{2,1,0:T(8,128)S(1)} %get-tuple-element.148), channel_id=1, source_target_pairs={{0,3},{1,0},{2,1},{3,2},{4,7},{5,4},{6,5},{7,6},{8,11},{9,8},{10,9... | collective-permute-start | bytes 196616 | tf_op jit(solution)/shard_map/ppermute | solution.py:535
  84.0 1.5 shard_map.100.refs_9_.refs_19_
  86.0 4.6 %shard_map.101 = (f32[72,8,128]{2,1,0:T(8,128)S(1)}, f32[73,8,128]{2,1,0:T(8,128)S(1)}, f32[73,8,128]{2,1,0:T(8,128)S(1)}, f32[11,8,128]{2,1,0:T(8,128)S(1)}, f3...) custom-call(f32[128,8,128]{2,1,0:T(8,128)S(1)} %get-tuple-element.146.refs_0_, ...), custom_call_target="tpu_custom_call" | custom-call | flops 20000000 | bytes 13594624 | tf_op jit(solution)/shard_map/pallas_call | solution.py:21
  90.6 1.3 collective-permute-start.29
  93.4 3.8 %collective-permute-start.37 = (f32[20,8,128]{2,1,0:T(8,128)S(1)}, f32[20,8,128]{2,1,0:T(8,128)S(1)}, u32[]{:S(2)}, u32[]{:S(2)}) collective-permute-start(f32[20,8,128]{2,1,0:T(8,128)S(1)} %get-tuple-element.159), channel_id=1, source_target_pairs={{0,28},{4,0},{8,4},{12,8},{16,12},{20,16},{24,20},{28,24},{1,29},{... | collective-permute-start | bytes 245768 | tf_op jit(solution)/shard_map/ppermute | solution.py:535
  97.2 1.2 collective-permute-start.31
  98.4 2.9 %collective-permute-done.31.refs_3_.refs_4_ = f32[11,8,128]{2,1,0:T(8,128)S(1)} collective-permute-done((f32[11,8,128]{2,1,0:T(8,128)S(1)}, f32[11,8,128]{2,1,0:T(8,128)S(1)}, u32[]{:S(2)}, u32[]{:S(2)}) %collective-permute-start.31) | collective-permute-done | bytes 45088 | tf_op jit(solution)/shard_map/ppermute | solution.py:535
  102.5 2.4 %shard_map.105 = (f32[48,8,128]{2,1,0:T(8,128)S(1)}, f32[49,8,128]{2,1,0:T(8,128)S(1)}, f32[49,8,128]{2,1,0:T(8,128)S(1)}, f32[8,8,128]{2,1,0:T(8,128)S(1)}, f32...) custom-call(f32[128,8,128]{2,1,0:T(8,128)S(1)} %get-tuple-element.146., ...), custom_call_target="tpu_custom_call" | custom-call | flops 10000000 | bytes 14942208 | tf_op jit(solution)/shard_map/pallas_call | solution.py:21
  105.0 1.7 %collective-permute-start.39 = (f32[49,8,128]{2,1,0:T(8,128)S(1)}, f32[49,8,128]{2,1,0:T(8,128)S(1)}, u32[]{:S(2)}, u32[]{:S(2)}) collective-permute-start(f32[49,8,128]{2,1,0:T(8,128)S(1)} %get-tuple-element.165), channel_id=1, source_target_pairs={{0,3},{1,0},{2,1},{3,2},{4,7},{5,4},{6,5},{7,6},{8,11},{9,8},{10,9... | collective-permute-start | bytes 602120 | tf_op jit(solution)/shard_map/ppermute | solution.py:535
  106.8 1.2 collective-permute-start.40
  107.9 6.5 %collective-permute-done.40.refs_3_.refs_4_ = f32[8,8,128]{2,1,0:T(8,128)S(1)} collective-permute-done((f32[8,8,128]{2,1,0:T(8,128)S(1)}, f32[8,8,128]{2,1,0:T(8,128)S(1)}, u32[]{:S(2)}, u32[]{:S(2)}) %collective-permute-start.40) | collective-permute-done | bytes 32800 | tf_op jit(solution)/shard_map/ppermute | solution.py:535
  115.7 3.1 %collective-permute-done.47.refs_3_.refs_4_ = f32[6,8,128]{2,1,0:T(8,128)S(1)} collective-permute-done((f32[6,8,128]{2,1,0:T(8,128)S(1)}, f32[6,8,128]{2,1,0:T(8,128)S(1)}, u32[]{:S(2)}, u32[]{:S(2)}) %collective-permute-start.47) | collective-permute-done | bytes 24608 | tf_op jit(solution)/shard_map/ppermute | solution.py:535
  119.9 4.9 %collective-permute-start.50 = (f32[24,8,128]{2,1,0:T(8,128)S(1)}, f32[24,8,128]{2,1,0:T(8,128)S(1)}, u32[]{:S(2)}, u32[]{:S(2)}) collective-permute-start(f32[24,8,128]{2,1,0:T(8,128)S(1)} %get-tuple-element.181), channel_id=1, source_target_pairs={{0,4},{4,0},{8,12},{12,8},{16,20},{20,16},{24,28},{28,24},{1,5},{5... | collective-permute-start | bytes 294920 | tf_op jit(solution)/shard_map/ppermute | solution.py:539
  124.8 2.0 %collective-permute-start.43 = (f32[32,8,128]{2,1,0:T(8,128)S(1)}, f32[32,8,128]{2,1,0:T(8,128)S(1)}, u32[]{:S(2)}, u32[]{:S(2)}) collective-permute-start(f32[32,8,128]{2,1,0:T(8,128)S(1)} %get-tuple-element.171), channel_id=1, source_target_pairs={{0,4},{4,0},{8,12},{12,8},{16,20},{20,16},{24,28},{28,24},{1,5},{5... | collective-permute-start | bytes 393224 | tf_op jit(solution)/shard_map/ppermute | solution.py:539
  126.9 3.4 %collective-permute-start.49 = (f32[24,8,128]{2,1,0:T(8,128)S(1)}, f32[24,8,128]{2,1,0:T(8,128)S(1)}, u32[]{:S(2)}, u32[]{:S(2)}) collective-permute-start(f32[24,8,128]{2,1,0:T(8,128)S(1)} %get-tuple-element.179), channel_id=1, source_target_pairs={{0,24},{4,12},{8,0},{12,20},{16,8},{20,28},{24,16},{28,4},{1,25},{... | collective-permute-start | bytes 294920 | tf_op jit(solution)/shard_map/ppermute | solution.py:544
  130.3 3.4 %collective-permute-done.52.refs_12_ = f32[16,8,128]{2,1,0:T(8,128)S(1)} collective-permute-done((f32[16,8,128]{2,1,0:T(8,128)S(1)}, f32[16,8,128]{2,1,0:T(8,128)S(1)}, u32[]{:S(2)}, u32[]{:S(2)}) %collective-permute-start.52) | collective-permute-done | bytes 65568 | tf_op jit(solution)/shard_map/ppermute | solution.py:535
  134.1 3.0 %collective-permute-start.33 = (f32[72,8,128]{2,1,0:T(8,128)S(1)}, f32[72,8,128]{2,1,0:T(8,128)S(1)}, u32[]{:S(2)}, u32[]{:S(2)}) collective-permute-start(f32[72,8,128]{2,1,0:T(8,128)S(1)} %get-tuple-element.155), channel_id=1, source_target_pairs={{0,24},{4,12},{8,0},{12,20},{16,8},{20,28},{24,16},{28,4},{1,25},{... | collective-permute-start | bytes 884744 | tf_op jit(solution)/shard_map/ppermute | solution.py:544
  137.0 2.6 %collective-permute-start.41 = (f32[32,8,128]{2,1,0:T(8,128)S(1)}, f32[32,8,128]{2,1,0:T(8,128)S(1)}, u32[]{:S(2)}, u32[]{:S(2)}) collective-permute-start(f32[32,8,128]{2,1,0:T(8,128)S(1)} %get-tuple-element.168), channel_id=1, source_target_pairs={{0,4},{4,0},{8,12},{12,8},{16,20},{20,16},{24,28},{28,24},{1,5},{5... | collective-permute-start | bytes 393224 | tf_op jit(solution)/shard_map/ppermute | solution.py:539
  139.6 1.5 collective-permute-start.42
  141.1 3.9 %collective-permute-done.41.refs_5_ = f32[32,8,128]{2,1,0:T(8,128)S(1)} collective-permute-done((f32[32,8,128]{2,1,0:T(8,128)S(1)}, f32[32,8,128]{2,1,0:T(8,128)S(1)}, u32[]{:S(2)}, u32[]{:S(2)}) %collective-permute-start.41) | collective-permute-done | bytes 131104 | tf_op jit(solution)/shard_map/ppermute | solution.py:539
  145.0 9.1 %collective-permute-done.42.refs_6_ = f32[32,8,128]{2,1,0:T(8,128)S(1)} collective-permute-done((f32[32,8,128]{2,1,0:T(8,128)S(1)}, f32[32,8,128]{2,1,0:T(8,128)S(1)}, u32[]{:S(2)}, u32[]{:S(2)}) %collective-permute-start.42) | collective-permute-done | bytes 131104 | tf_op jit(solution)/shard_map/ppermute | solution.py:544
  154.1 6.4 %collective-permute-done.51.refs_11_ = f32[24,8,128]{2,1,0:T(8,128)S(1)} collective-permute-done((f32[24,8,128]{2,1,0:T(8,128)S(1)}, f32[24,8,128]{2,1,0:T(8,128)S(1)}, u32[]{:S(2)}, u32[]{:S(2)}) %collective-permute-start.51) | collective-permute-done | bytes 98336 | tf_op jit(solution)/shard_map/ppermute | solution.py:544
  (85 shorter events, 13.8 us)
Async XLA Ops:
  1.6 4.4 %collective-permute-start = (f32[16,8,128]{2,1,0:T(8,128)S(1)}, f32[16,8,128]{2,1,0:T(8,128)S(1)}, u32[]{:S(2)}, u32[]{:S(2)}) collective-permute-start(f32[16,8,128]{2,1,0:T(8,128)S(1)} %get-tuple-element.94), channel_id=1, source_target_pairs={{0,1},{1,2},{2,3},{3,0},{4,5},{5,6},{6,7},{7,4},{8,9},{9,10},{10,1... | collective-permute-start | bytes 196616 | tf_op jit(solution)/shard_map/ppermute | solution.py:535
  2.2 4.4 %collective-permute-start.1 = (f32[16,8,128]{2,1,0:T(8,128)S(1)}, f32[16,8,128]{2,1,0:T(8,128)S(1)}, u32[]{:S(2)}, u32[]{:S(2)}) collective-permute-start(f32[16,8,128]{2,1,0:T(8,128)S(1)} %get-tuple-element.95), channel_id=1, source_target_pairs={{0,3},{1,0},{2,1},{3,2},{4,7},{5,4},{6,5},{7,6},{8,11},{9,8},{10,9... | collective-permute-start | bytes 196616 | tf_op jit(solution)/shard_map/ppermute | solution.py:535
  12.7 10.8 %collective-permute-start.2 = (f32[73,8,128]{2,1,0:T(8,128)S(1)}, f32[73,8,128]{2,1,0:T(8,128)S(1)}, u32[]{:S(2)}, u32[]{:S(2)}) collective-permute-start(f32[73,8,128]{2,1,0:T(8,128)S(1)} %get-tuple-element.106), channel_id=1, source_target_pairs={{0,1},{1,2},{2,3},{3,0},{4,5},{5,6},{6,7},{7,4},{8,9},{9,10},{10,1... | collective-permute-start | bytes 897032 | tf_op jit(solution)/shard_map/ppermute | solution.py:535
  14.6 8.9 %collective-permute-start.3 = (f32[73,8,128]{2,1,0:T(8,128)S(1)}, f32[73,8,128]{2,1,0:T(8,128)S(1)}, u32[]{:S(2)}, u32[]{:S(2)}) collective-permute-start(f32[73,8,128]{2,1,0:T(8,128)S(1)} %get-tuple-element.107), channel_id=1, source_target_pairs={{0,3},{1,0},{2,1},{3,2},{4,7},{5,4},{6,5},{7,6},{8,11},{9,8},{10,9... | collective-permute-start | bytes 897032 | tf_op jit(solution)/shard_map/ppermute | solution.py:535
  14.9 10.6 %collective-permute-start.10 = (f32[20,8,128]{2,1,0:T(8,128)S(1)}, f32[20,8,128]{2,1,0:T(8,128)S(1)}, u32[]{:S(2)}, u32[]{:S(2)}) collective-permute-start(f32[20,8,128]{2,1,0:T(8,128)S(1)} %get-tuple-element.115), channel_id=1, source_target_pairs={{0,28},{4,0},{8,4},{12,8},{16,12},{20,16},{24,20},{28,24},{1,29},{... | collective-permute-start | bytes 245768 | tf_op jit(solution)/shard_map/ppermute | solution.py:535
  19.5 7.2 %collective-permute-start.9 = (f32[20,8,128]{2,1,0:T(8,128)S(1)}, f32[20,8,128]{2,1,0:T(8,128)S(1)}, u32[]{:S(2)}, u32[]{:S(2)}) collective-permute-start(f32[20,8,128]{2,1,0:T(8,128)S(1)} %get-tuple-element.114), channel_id=1, source_target_pairs={{0,4},{4,8},{8,12},{12,16},{16,20},{20,24},{24,28},{28,0},{1,5},{5... | collective-permute-start | bytes 245768 | tf_op jit(solution)/shard_map/ppermute | solution.py:535
  24.1 25.9 %collective-permute-start.7 = (f32[72,8,128]{2,1,0:T(8,128)S(1)}, f32[72,8,128]{2,1,0:T(8,128)S(1)}, u32[]{:S(2)}, u32[]{:S(2)}) collective-permute-start(f32[72,8,128]{2,1,0:T(8,128)S(1)} %get-tuple-element.113), channel_id=1, source_target_pairs={{0,4},{4,0},{8,12},{12,8},{16,20},{20,16},{24,28},{28,24},{1,5},{5... | collective-permute-start | bytes 884744 | tf_op jit(solution)/shard_map/ppermute | solution.py:539
  29.3 9.5 %collective-permute-start.11 = (f32[49,8,128]{2,1,0:T(8,128)S(1)}, f32[49,8,128]{2,1,0:T(8,128)S(1)}, u32[]{:S(2)}, u32[]{:S(2)}) collective-permute-start(f32[49,8,128]{2,1,0:T(8,128)S(1)} %get-tuple-element.126), channel_id=1, source_target_pairs={{0,1},{1,2},{2,3},{3,0},{4,5},{5,6},{6,7},{7,4},{8,9},{9,10},{10,1... | collective-permute-start | bytes 602120 | tf_op jit(solution)/shard_map/ppermute | solution.py:535
  29.4 10.3 %collective-permute-start.12 = (f32[49,8,128]{2,1,0:T(8,128)S(1)}, f32[49,8,128]{2,1,0:T(8,128)S(1)}, u32[]{:S(2)}, u32[]{:S(2)}) collective-permute-start(f32[49,8,128]{2,1,0:T(8,128)S(1)} %get-tuple-element.127), channel_id=1, source_target_pairs={{0,3},{1,0},{2,1},{3,2},{4,7},{5,4},{6,5},{7,6},{8,11},{9,8},{10,9... | collective-permute-start | bytes 602120 | tf_op jit(solution)/shard_map/ppermute | solution.py:535
  31.1 7.7 %collective-permute-start.13 = (f32[8,8,128]{2,1,0:T(8,128)S(1)}, f32[8,8,128]{2,1,0:T(8,128)S(1)}, u32[]{:S(2)}, u32[]{:S(2)}) collective-permute-start(f32[8,8,128]{2,1,0:T(8,128)S(1)} %get-tuple-element.128), channel_id=1, source_target_pairs={{0,2},{1,3},{2,0},{3,1},{4,6},{5,7},{6,4},{7,5},{8,10},{9,11},{10,... | collective-permute-start | bytes 98312 | tf_op jit(solution)/shard_map/ppermute | solution.py:535
  32.5 10.7 %collective-permute-start.18 = (f32[33,8,128]{2,1,0:T(8,128)S(1)}, f32[33,8,128]{2,1,0:T(8,128)S(1)}, u32[]{:S(2)}, u32[]{:S(2)}) collective-permute-start(f32[33,8,128]{2,1,0:T(8,128)S(1)} %get-tuple-element.136), channel_id=1, source_target_pairs={{0,1},{1,2},{2,3},{3,0},{4,5},{5,6},{6,7},{7,4},{8,9},{9,10},{10,1... | collective-permute-start | bytes 405512 | tf_op jit(solution)/shard_map/ppermute | solution.py:535
  38.8 4.4 %collective-permute-start.19 = (f32[33,8,128]{2,1,0:T(8,128)S(1)}, f32[33,8,128]{2,1,0:T(8,128)S(1)}, u32[]{:S(2)}, u32[]{:S(2)}) collective-permute-start(f32[33,8,128]{2,1,0:T(8,128)S(1)} %get-tuple-element.137), channel_id=1, source_target_pairs={{0,3},{1,0},{2,1},{3,2},{4,7},{5,4},{6,5},{7,6},{8,11},{9,8},{10,9... | collective-permute-start | bytes 405512 | tf_op jit(solution)/shard_map/ppermute | solution.py:535
  43.4 6.3 %collective-permute-start.26 = (f32[8,8,128]{2,1,0:T(8,128)S(1)}, f32[8,8,128]{2,1,0:T(8,128)S(1)}, u32[]{:S(2)}, u32[]{:S(2)}) collective-permute-start(f32[8,8,128]{2,1,0:T(8,128)S(1)} %get-tuple-element.145), channel_id=1, source_target_pairs={{0,20},{4,24},{8,28},{12,0},{16,4},{20,8},{24,12},{28,16},{1,21},{... | collective-permute-start | bytes 98312 | tf_op jit(solution)/shard_map/ppermute | solution.py:535
  44.9 12.0 %collective-permute-start.23 = (f32[24,8,128]{2,1,0:T(8,128)S(1)}, f32[24,8,128]{2,1,0:T(8,128)S(1)}, u32[]{:S(2)}, u32[]{:S(2)}) collective-permute-start(f32[24,8,128]{2,1,0:T(8,128)S(1)} %get-tuple-element.143), channel_id=1, source_target_pairs={{0,4},{4,0},{8,12},{12,8},{16,20},{20,16},{24,28},{28,24},{1,5},{5... | collective-permute-start | bytes 294920 | tf_op jit(solution)/shard_map/ppermute | solution.py:539
  47.7 12.0 %collective-permute-start.21 = (f32[24,8,128]{2,1,0:T(8,128)S(1)}, f32[24,8,128]{2,1,0:T(8,128)S(1)}, u32[]{:S(2)}, u32[]{:S(2)}) collective-permute-start(f32[24,8,128]{2,1,0:T(8,128)S(1)} %get-tuple-element.140), channel_id=1, source_target_pairs={{0,4},{4,0},{8,12},{12,8},{16,20},{20,16},{24,28},{28,24},{1,5},{5... | collective-permute-start | bytes 294920 | tf_op jit(solution)/shard_map/ppermute | solution.py:539
  47.7 14.1 %collective-permute-start.16 = (f32[32,8,128]{2,1,0:T(8,128)S(1)}, f32[32,8,128]{2,1,0:T(8,128)S(1)}, u32[]{:S(2)}, u32[]{:S(2)}) collective-permute-start(f32[32,8,128]{2,1,0:T(8,128)S(1)} %get-tuple-element.133), channel_id=1, source_target_pairs={{0,4},{4,0},{8,12},{12,8},{16,20},{20,16},{24,28},{28,24},{1,5},{5... | collective-permute-start | bytes 393224 | tf_op jit(solution)/shard_map/ppermute | solution.py:539
  49.7 6.2 %collective-permute-start.25 = (f32[16,8,128]{2,1,0:T(8,128)S(1)}, f32[16,8,128]{2,1,0:T(8,128)S(1)}, u32[]{:S(2)}, u32[]{:S(2)}) collective-permute-start(f32[16,8,128]{2,1,0:T(8,128)S(1)} %get-tuple-element.144), channel_id=1, source_target_pairs={{0,12},{4,16},{8,20},{12,24},{16,28},{20,0},{24,4},{28,8},{1,13},{... | collective-permute-start | bytes 196616 | tf_op jit(solution)/shard_map/ppermute | solution.py:535
  50.0 9.8 %collective-permute-start.22 = (f32[24,8,128]{2,1,0:T(8,128)S(1)}, f32[24,8,128]{2,1,0:T(8,128)S(1)}, u32[]{:S(2)}, u32[]{:S(2)}) collective-permute-start(f32[24,8,128]{2,1,0:T(8,128)S(1)} %get-tuple-element.141), channel_id=1, source_target_pairs={{0,24},{4,12},{8,0},{12,20},{16,8},{20,28},{24,16},{28,4},{1,25},{... | collective-permute-start | bytes 294920 | tf_op jit(solution)/shard_map/ppermute | solution.py:544
  55.9 26.1 %collective-permute-start.5 = (f32[72,8,128]{2,1,0:T(8,128)S(1)}, f32[72,8,128]{2,1,0:T(8,128)S(1)}, u32[]{:S(2)}, u32[]{:S(2)}) collective-permute-start(f32[72,8,128]{2,1,0:T(8,128)S(1)} %get-tuple-element.110), channel_id=1, source_target_pairs={{0,4},{4,0},{8,12},{12,8},{16,20},{20,16},{24,28},{28,24},{1,5},{5... | collective-permute-start | bytes 884744 | tf_op jit(solution)/shard_map/ppermute | solution.py:539
  56.8 25.2 %collective-permute-start.6 = (f32[72,8,128]{2,1,0:T(8,128)S(1)}, f32[72,8,128]{2,1,0:T(8,128)S(1)}, u32[]{:S(2)}, u32[]{:S(2)}) collective-permute-start(f32[72,8,128]{2,1,0:T(8,128)S(1)} %get-tuple-element.111), channel_id=1, source_target_pairs={{0,24},{4,12},{8,0},{12,20},{16,8},{20,28},{24,16},{28,4},{1,25},{... | collective-permute-start | bytes 884744 | tf_op jit(solution)/shard_map/ppermute | solution.py:544
  59.7 22.3 %collective-permute-start.8 = (f32[72,8,128]{2,1,0:T(8,128)S(1)}, f32[72,8,128]{2,1,0:T(8,128)S(1)}, u32[]{:S(2)}, u32[]{:S(2)}) collective-permute-start(f32[72,8,128]{2,1,0:T(8,128)S(1)} %shard_map.91), channel_id=1, source_target_pairs={{0,8},{4,28},{8,16},{12,4},{16,24},{20,12},{24,0},{28,20},{1,9},{5... | collective-permute-start | bytes 884744 | tf_op jit(solution)/shard_map/ppermute | solution.py:544
  59.7 6.0 %collective-permute-start.14 = (f32[32,8,128]{2,1,0:T(8,128)S(1)}, f32[32,8,128]{2,1,0:T(8,128)S(1)}, u32[]{:S(2)}, u32[]{:S(2)}) collective-permute-start(f32[32,8,128]{2,1,0:T(8,128)S(1)} %get-tuple-element.130), channel_id=1, source_target_pairs={{0,4},{4,0},{8,12},{12,8},{16,20},{20,16},{24,28},{28,24},{1,5},{5... | collective-permute-start | bytes 393224 | tf_op jit(solution)/shard_map/ppermute | solution.py:539
  61.8 13.3 %collective-permute-start.15 = (f32[32,8,128]{2,1,0:T(8,128)S(1)}, f32[32,8,128]{2,1,0:T(8,128)S(1)}, u32[]{:S(2)}, u32[]{:S(2)}) collective-permute-start(f32[32,8,128]{2,1,0:T(8,128)S(1)} %get-tuple-element.131), channel_id=1, source_target_pairs={{0,24},{4,12},{8,0},{12,20},{16,8},{20,28},{24,16},{28,4},{1,25},{... | collective-permute-start | bytes 393224 | tf_op jit(solution)/shard_map/ppermute | solution.py:544
  65.8 16.3 %collective-permute-start.17 = (f32[32,8,128]{2,1,0:T(8,128)S(1)}, f32[32,8,128]{2,1,0:T(8,128)S(1)}, u32[]{:S(2)}, u32[]{:S(2)}) collective-permute-start(f32[32,8,128]{2,1,0:T(8,128)S(1)} %shard_map.96), channel_id=1, source_target_pairs={{0,8},{4,28},{8,16},{12,4},{16,24},{20,12},{24,0},{28,20},{1,9},{5... | collective-permute-start | bytes 393224 | tf_op jit(solution)/shard_map/ppermute | solution.py:544
  75.1 6.9 %collective-permute-start.24 = (f32[24,8,128]{2,1,0:T(8,128)S(1)}, f32[24,8,128]{2,1,0:T(8,128)S(1)}, u32[]{:S(2)}, u32[]{:S(2)}) collective-permute-start(f32[24,8,128]{2,1,0:T(8,128)S(1)} %shard_map.98), channel_id=1, source_target_pairs={{0,8},{4,28},{8,16},{12,4},{16,24},{20,12},{24,0},{28,20},{1,9},{5... | collective-permute-start | bytes 294920 | tf_op jit(solution)/shard_map/ppermute | solution.py:544
  90.6 10.7 %collective-permute-start.29 = (f32[73,8,128]{2,1,0:T(8,128)S(1)}, f32[73,8,128]{2,1,0:T(8,128)S(1)}, u32[]{:S(2)}, u32[]{:S(2)}) collective-permute-start(f32[73,8,128]{2,1,0:T(8,128)S(1)} %get-tuple-element.150), channel_id=1, source_target_pairs={{0,1},{1,2},{2,3},{3,0},{4,5},{5,6},{6,7},{7,4},{8,9},{9,10},{10,1... | collective-permute-start | bytes 897032 | tf_op jit(solution)/shard_map/ppermute | solution.py:535
  91.9 9.4 %collective-permute-start.30 = (f32[73,8,128]{2,1,0:T(8,128)S(1)}, f32[73,8,128]{2,1,0:T(8,128)S(1)}, u32[]{:S(2)}, u32[]{:S(2)}) collective-permute-start(f32[73,8,128]{2,1,0:T(8,128)S(1)} %get-tuple-element.151), channel_id=1, source_target_pairs={{0,3},{1,0},{2,1},{3,2},{4,7},{5,4},{6,5},{7,6},{8,11},{9,8},{10,9... | collective-permute-start | bytes 897032 | tf_op jit(solution)/shard_map/ppermute | solution.py:535
  92.4 10.1 %collective-permute-start.36 = (f32[20,8,128]{2,1,0:T(8,128)S(1)}, f32[20,8,128]{2,1,0:T(8,128)S(1)}, u32[]{:S(2)}, u32[]{:S(2)}) collective-permute-start(f32[20,8,128]{2,1,0:T(8,128)S(1)} %get-tuple-element.158), channel_id=1, source_target_pairs={{0,4},{4,8},{8,12},{12,16},{16,20},{20,24},{24,28},{28,0},{1,5},{5... | collective-permute-start | bytes 245768 | tf_op jit(solution)/shard_map/ppermute | solution.py:535
  93.4 9.1 %collective-permute-start.37 = (f32[20,8,128]{2,1,0:T(8,128)S(1)}, f32[20,8,128]{2,1,0:T(8,128)S(1)}, u32[]{:S(2)}, u32[]{:S(2)}) collective-permute-start(f32[20,8,128]{2,1,0:T(8,128)S(1)} %get-tuple-element.159), channel_id=1, source_target_pairs={{0,28},{4,0},{8,4},{12,8},{16,12},{20,16},{24,20},{28,24},{1,29},{... | collective-permute-start | bytes 245768 | tf_op jit(solution)/shard_map/ppermute | solution.py:535
  101.8 25.1 %collective-permute-start.34 = (f32[72,8,128]{2,1,0:T(8,128)S(1)}, f32[72,8,128]{2,1,0:T(8,128)S(1)}, u32[]{:S(2)}, u32[]{:S(2)}) collective-permute-start(f32[72,8,128]{2,1,0:T(8,128)S(1)} %get-tuple-element.157), channel_id=1, source_target_pairs={{0,4},{4,0},{8,12},{12,8},{16,20},{20,16},{24,28},{28,24},{1,5},{5... | collective-permute-start | bytes 884744 | tf_op jit(solution)/shard_map/ppermute | solution.py:539
  105.0 9.5 %collective-permute-start.38 = (f32[49,8,128]{2,1,0:T(8,128)S(1)}, f32[49,8,128]{2,1,0:T(8,128)S(1)}, u32[]{:S(2)}, u32[]{:S(2)}) collective-permute-start(f32[49,8,128]{2,1,0:T(8,128)S(1)} %get-tuple-element.164), channel_id=1, source_target_pairs={{0,1},{1,2},{2,3},{3,0},{4,5},{5,6},{6,7},{7,4},{8,9},{9,10},{10,1... | collective-permute-start | bytes 602120 | tf_op jit(solution)/shard_map/ppermute | solution.py:535
  105.0 10.3 %collective-permute-start.39 = (f32[49,8,128]{2,1,0:T(8,128)S(1)}, f32[49,8,128]{2,1,0:T(8,128)S(1)}, u32[]{:S(2)}, u32[]{:S(2)}) collective-permute-start(f32[49,8,128]{2,1,0:T(8,128)S(1)} %get-tuple-element.165), channel_id=1, source_target_pairs={{0,3},{1,0},{2,1},{3,2},{4,7},{5,4},{6,5},{7,6},{8,11},{9,8},{10,9... | collective-permute-start | bytes 602120 | tf_op jit(solution)/shard_map/ppermute | solution.py:535
  106.8 7.7 %collective-permute-start.40 = (f32[8,8,128]{2,1,0:T(8,128)S(1)}, f32[8,8,128]{2,1,0:T(8,128)S(1)}, u32[]{:S(2)}, u32[]{:S(2)}) collective-permute-start(f32[8,8,128]{2,1,0:T(8,128)S(1)} %get-tuple-element.166), channel_id=1, source_target_pairs={{0,2},{1,3},{2,0},{3,1},{4,6},{5,7},{6,4},{7,5},{8,10},{9,11},{10,... | collective-permute-start | bytes 98312 | tf_op jit(solution)/shard_map/ppermute | solution.py:535
  107.9 10.9 %collective-permute-start.45 = (f32[33,8,128]{2,1,0:T(8,128)S(1)}, f32[33,8,128]{2,1,0:T(8,128)S(1)}, u32[]{:S(2)}, u32[]{:S(2)}) collective-permute-start(f32[33,8,128]{2,1,0:T(8,128)S(1)} %get-tuple-element.174), channel_id=1, source_target_pairs={{0,1},{1,2},{2,3},{3,0},{4,5},{5,6},{6,7},{7,4},{8,9},{9,10},{10,1... | collective-permute-start | bytes 405512 | tf_op jit(solution)/shard_map/ppermute | solution.py:535
  114.4 4.4 %collective-permute-start.46 = (f32[33,8,128]{2,1,0:T(8,128)S(1)}, f32[33,8,128]{2,1,0:T(8,128)S(1)}, u32[]{:S(2)}, u32[]{:S(2)}) collective-permute-start(f32[33,8,128]{2,1,0:T(8,128)S(1)} %get-tuple-element.175), channel_id=1, source_target_pairs={{0,3},{1,0},{2,1},{3,2},{4,7},{5,4},{6,5},{7,6},{8,11},{9,8},{10,9... | collective-permute-start | bytes 405512 | tf_op jit(solution)/shard_map/ppermute | solution.py:535
  119.1 7.8 %collective-permute-start.53 = (f32[8,8,128]{2,1,0:T(8,128)S(1)}, f32[8,8,128]{2,1,0:T(8,128)S(1)}, u32[]{:S(2)}, u32[]{:S(2)}) collective-permute-start(f32[8,8,128]{2,1,0:T(8,128)S(1)} %get-tuple-element.183), channel_id=1, source_target_pairs={{0,20},{4,24},{8,28},{12,0},{16,4},{20,8},{24,12},{28,16},{1,21},{... | collective-permute-start | bytes 98312 | tf_op jit(solution)/shard_map/ppermute | solution.py:535
  119.9 14.2 %collective-permute-start.50 = (f32[24,8,128]{2,1,0:T(8,128)S(1)}, f32[24,8,128]{2,1,0:T(8,128)S(1)}, u32[]{:S(2)}, u32[]{:S(2)}) collective-permute-start(f32[24,8,128]{2,1,0:T(8,128)S(1)} %get-tuple-element.181), channel_id=1, source_target_pairs={{0,4},{4,0},{8,12},{12,8},{16,20},{20,16},{24,28},{28,24},{1,5},{5... | collective-permute-start | bytes 294920 | tf_op jit(solution)/shard_map/ppermute | solution.py:539
  124.8 12.2 %collective-permute-start.48 = (f32[24,8,128]{2,1,0:T(8,128)S(1)}, f32[24,8,128]{2,1,0:T(8,128)S(1)}, u32[]{:S(2)}, u32[]{:S(2)}) collective-permute-start(f32[24,8,128]{2,1,0:T(8,128)S(1)} %get-tuple-element.178), channel_id=1, source_target_pairs={{0,4},{4,0},{8,12},{12,8},{16,20},{20,16},{24,28},{28,24},{1,5},{5... | collective-permute-start | bytes 294920 | tf_op jit(solution)/shard_map/ppermute | solution.py:539
  124.8 14.8 %collective-permute-start.43 = (f32[32,8,128]{2,1,0:T(8,128)S(1)}, f32[32,8,128]{2,1,0:T(8,128)S(1)}, u32[]{:S(2)}, u32[]{:S(2)}) collective-permute-start(f32[32,8,128]{2,1,0:T(8,128)S(1)} %get-tuple-element.171), channel_id=1, source_target_pairs={{0,4},{4,0},{8,12},{12,8},{16,20},{20,16},{24,28},{28,24},{1,5},{5... | collective-permute-start | bytes 393224 | tf_op jit(solution)/shard_map/ppermute | solution.py:539
  126.8 6.9 %collective-permute-start.52 = (f32[16,8,128]{2,1,0:T(8,128)S(1)}, f32[16,8,128]{2,1,0:T(8,128)S(1)}, u32[]{:S(2)}, u32[]{:S(2)}) collective-permute-start(f32[16,8,128]{2,1,0:T(8,128)S(1)} %get-tuple-element.182), channel_id=1, source_target_pairs={{0,12},{4,16},{8,20},{12,24},{16,28},{20,0},{24,4},{28,8},{1,13},{... | collective-permute-start | bytes 196616 | tf_op jit(solution)/shard_map/ppermute | solution.py:535
  126.9 10.1 %collective-permute-start.49 = (f32[24,8,128]{2,1,0:T(8,128)S(1)}, f32[24,8,128]{2,1,0:T(8,128)S(1)}, u32[]{:S(2)}, u32[]{:S(2)}) collective-permute-start(f32[24,8,128]{2,1,0:T(8,128)S(1)} %get-tuple-element.179), channel_id=1, source_target_pairs={{0,24},{4,12},{8,0},{12,20},{16,8},{20,28},{24,16},{28,4},{1,25},{... | collective-permute-start | bytes 294920 | tf_op jit(solution)/shard_map/ppermute | solution.py:544
  133.7 26.8 %collective-permute-start.32 = (f32[72,8,128]{2,1,0:T(8,128)S(1)}, f32[72,8,128]{2,1,0:T(8,128)S(1)}, u32[]{:S(2)}, u32[]{:S(2)}) collective-permute-start(f32[72,8,128]{2,1,0:T(8,128)S(1)} %get-tuple-element.154), channel_id=1, source_target_pairs={{0,4},{4,0},{8,12},{12,8},{16,20},{20,16},{24,28},{28,24},{1,5},{5... | collective-permute-start | bytes 884744 | tf_op jit(solution)/shard_map/ppermute | solution.py:539
  134.1 26.5 %collective-permute-start.33 = (f32[72,8,128]{2,1,0:T(8,128)S(1)}, f32[72,8,128]{2,1,0:T(8,128)S(1)}, u32[]{:S(2)}, u32[]{:S(2)}) collective-permute-start(f32[72,8,128]{2,1,0:T(8,128)S(1)} %get-tuple-element.155), channel_id=1, source_target_pairs={{0,24},{4,12},{8,0},{12,20},{16,8},{20,28},{24,16},{28,4},{1,25},{... | collective-permute-start | bytes 884744 | tf_op jit(solution)/shard_map/ppermute | solution.py:544
  137.0 23.5 %collective-permute-start.35 = (f32[72,8,128]{2,1,0:T(8,128)S(1)}, f32[72,8,128]{2,1,0:T(8,128)S(1)}, u32[]{:S(2)}, u32[]{:S(2)}) collective-permute-start(f32[72,8,128]{2,1,0:T(8,128)S(1)} %shard_map.103), channel_id=1, source_target_pairs={{0,8},{4,28},{8,16},{12,4},{16,24},{20,12},{24,0},{28,20},{1,9},{5... | collective-permute-start | bytes 884744 | tf_op jit(solution)/shard_map/ppermute | solution.py:544
  137.0 8.0 %collective-permute-start.41 = (f32[32,8,128]{2,1,0:T(8,128)S(1)}, f32[32,8,128]{2,1,0:T(8,128)S(1)}, u32[]{:S(2)}, u32[]{:S(2)}) collective-permute-start(f32[32,8,128]{2,1,0:T(8,128)S(1)} %get-tuple-element.168), channel_id=1, source_target_pairs={{0,4},{4,0},{8,12},{12,8},{16,20},{20,16},{24,28},{28,24},{1,5},{5... | collective-permute-start | bytes 393224 | tf_op jit(solution)/shard_map/ppermute | solution.py:539
  139.6 14.5 %collective-permute-start.42 = (f32[32,8,128]{2,1,0:T(8,128)S(1)}, f32[32,8,128]{2,1,0:T(8,128)S(1)}, u32[]{:S(2)}, u32[]{:S(2)}) collective-permute-start(f32[32,8,128]{2,1,0:T(8,128)S(1)} %get-tuple-element.169), channel_id=1, source_target_pairs={{0,24},{4,12},{8,0},{12,20},{16,8},{20,28},{24,16},{28,4},{1,25},{... | collective-permute-start | bytes 393224 | tf_op jit(solution)/shard_map/ppermute | solution.py:544
  145.0 15.6 %collective-permute-start.44 = (f32[32,8,128]{2,1,0:T(8,128)S(1)}, f32[32,8,128]{2,1,0:T(8,128)S(1)}, u32[]{:S(2)}, u32[]{:S(2)}) collective-permute-start(f32[32,8,128]{2,1,0:T(8,128)S(1)} %shard_map.107), channel_id=1, source_target_pairs={{0,8},{4,28},{8,16},{12,4},{16,24},{20,12},{24,0},{28,20},{1,9},{5... | collective-permute-start | bytes 393224 | tf_op jit(solution)/shard_map/ppermute | solution.py:544
  154.1 6.4 %collective-permute-start.51 = (f32[24,8,128]{2,1,0:T(8,128)S(1)}, f32[24,8,128]{2,1,0:T(8,128)S(1)}, u32[]{:S(2)}, u32[]{:S(2)}) collective-permute-start(f32[24,8,128]{2,1,0:T(8,128)S(1)} %shard_map.109), channel_id=1, source_target_pairs={{0,8},{4,28},{8,16},{12,4},{16,24},{20,12},{24,0},{28,20},{1,9},{5... | collective-permute-start | bytes 294920 | tf_op jit(solution)/shard_map/ppermute | solution.py:544
  (6 other events, 24.3 us)
